TPU v7x, 32 devices: a whole 2x2x4 slice. The times are simulated.
32 devices in a mesh: node: 8 (over z, y), rep: 4 (over x, core).
Axes of the slice: x: 2, y: 2, z: 4, core: 2. Of those that a mesh axis runs over, the one named last changes fastest.
Arguments:
- coords: float32 [3, 4096], P(None, 'node'), may hold values from 0 to 2, as said below
- omega: bfloat16 [4096, 512], P('node', 'rep'), may hold values from -6 to 6
- skeleton: int32 [8, 256], P('node', 'rep'), may hold values from 0 to 4095, as said below
Outputs:
- row_sample: bfloat16 [4096, 512], P('node', 'rep')
- col_sample: float32 [4096, 512], P('node', 'rep')
Inputs may be any that keep to these rules, and one draw needn't show every extreme that they name: `skeleton`: each node's list holds distinct indices, none inside its own points, at most 73 inside the points of any one other node; in every draw one node's points hold exactly 73 indices of every other node's list. `coords`: the first coordinate of point p lies between 2 (p // 512) / 8 and 2 (p // 512 + 1) / 8; the other two lie in [0, 1].
All inputs are finite; a program needn't handle non-finite values.
Results may differ from a plain program's by a relative error of at most 0.0049.
Values may be sent and summed in bfloat16 or wider, within the bound.
No kernel may reach another device: no remote copies, remote signals or barrier semaphores. Data moves between devices by JAX's collectives and lax.ppermute only.
A program may use at most 128 MiB of HBM per device.

v0:
```python
import jax
import jax.numpy as jnp
from jax import lax
from jax.sharding import PartitionSpec as P

kernel_scale = 0.0078125
softening = 0.02


def passed_along(block, axis, distance):
    devices = range(lax.axis_size(axis))
    route = [(i - distance, i) for i in devices if i - distance in devices]
    return lax.ppermute(block, axis, route)


def kernel_tile(first_points, target_points):
    squared = (first_points[0][:, None] - target_points[0][None, :]) ** 2
    squared = squared + (first_points[1][:, None] - target_points[1][None, :]) ** 2
    squared = squared + (first_points[2][:, None] - target_points[2][None, :]) ** 2
    return (kernel_scale * lax.rsqrt(squared + softening * softening)).astype(jnp.bfloat16)


def on_device(coords, omega, skeleton):
    node_count = lax.axis_size("node")
    leaf_size = coords.shape[1]
    samp_dev = omega.shape[1]
    listed = lax.all_gather(skeleton, "rep", axis=1, tiled=True)[0]
    rank_size = listed.shape[0]
    capacity = max(8, 2 * rank_size // (node_count - 1))
    owners_of = listed // leaf_size
    local_index = listed % leaf_size
    owner_hits = (owners_of[:, None] == jnp.arange(node_count, dtype=jnp.int32)[None, :]).astype(
        jnp.int32
    )
    slot_rank = jnp.sum((jnp.cumsum(owner_hits, axis=0) - owner_hits) * owner_hits, axis=1)
    flat_slot = owners_of * capacity + slot_rank
    request = (
        jnp.zeros((node_count * capacity,), jnp.int32)
        .at[flat_slot]
        .set(local_index)
        .reshape(node_count, capacity)
    )
    lower_side = (
        passed_along(coords, "node", 1),
        passed_along(omega.astype(jnp.float32), "node", 1).astype(omega.dtype),
    )
    upper_side = (
        passed_along(coords, "node", -1),
        passed_along(omega.astype(jnp.float32), "node", -1).astype(omega.dtype),
    )
    wide_points = jnp.concatenate([lower_side[0], coords, upper_side[0]], axis=1)
    wide_rows = jnp.concatenate([lower_side[1], omega, upper_side[1]], axis=0)
    row_total = jnp.dot(
        kernel_tile(coords, wide_points), wide_rows, preferred_element_type=jnp.float32
    )
    asked_rows = lax.all_to_all(request, "node", split_axis=0, concat_axis=0, tiled=True)
    asked_points = jnp.transpose(coords[:, asked_rows], (1, 0, 2))
    asked_samples = omega[asked_rows]
    got_points, got_samples = (
        lax.all_to_all(asked_points, "node", split_axis=0, concat_axis=0, tiled=True),
        lax.all_to_all(
            asked_samples.astype(jnp.float32), "node", split_axis=0, concat_axis=0, tiled=True
        ).astype(asked_samples.dtype),
    )
    skel_points = jnp.transpose(got_points[owners_of, :, slot_rank])
    skel_tile = kernel_tile(coords, skel_points)
    row_total = row_total + jnp.dot(
        skel_tile, got_samples[owners_of, slot_rank], preferred_element_type=jnp.float32
    )
    transposed = lax.dot_general(
        skel_tile, omega, (((0,), (0,)), ((), ())), preferred_element_type=jnp.float32
    )
    outgoing = (
        jnp.zeros((node_count * capacity, samp_dev), jnp.float32).at[flat_slot].set(transposed)
    )
    incoming = lax.all_to_all(
        outgoing.reshape(node_count, capacity, samp_dev),
        "node",
        split_axis=0,
        concat_axis=0,
        tiled=True,
    )
    col_total = (
        jnp.zeros((leaf_size, samp_dev), jnp.float32)
        .at[asked_rows.reshape(-1)]
        .add(incoming.reshape(-1, samp_dev))
    )
    return (row_total.astype(jnp.bfloat16), col_total)


def solution(mesh):
    in_specs = (P(None, "node"), P("node", "rep"), P("node", "rep"))
    out_specs = (P("node", "rep"), P("node", "rep"))
    return jax.shard_map(
        on_device, mesh=mesh, in_specs=in_specs, out_specs=out_specs, check_vma=False
    )
```

profile of v0, /device:TPU:0, one launch (start us, length us, event | category | flops | bytes accessed | tf_op | source)
XLA Modules:
  0.0 83.8 jit_solution(1466101528876228582)
XLA Ops:
  0.6 5.0 %collective-permute-start = (f32[3,512]{1,0:T(4,128)}, f32[3,512]{1,0:T(4,128)S(1)}, u32[]{:S(2)}, u32[]{:S(2)}) collective-permute-start(f32[3,512]{1,0:T(4,128)} %param.3), channel_id=1, source_target_pairs={{0,4},{4,8},{8,12},{12,16},{16,20},{20,24},{24,28},{1,5},{5,9},{9,... | collective-permute-start | bytes 18440 | tf_op jit(solution)/shard_map/ppermute | solution.py:13
  5.7 1.3 %collective-permute-start.1 = (f32[3,512]{1,0:T(4,128)}, f32[3,512]{1,0:T(4,128)S(1)}, u32[]{:S(2)}, u32[]{:S(2)}) collective-permute-start(f32[3,512]{1,0:T(4,128)} %param.3), channel_id=1, source_target_pairs={{4,0},{8,4},{12,8},{16,12},{20,16},{24,20},{28,24},{5,1},{9,5},{13... | collective-permute-start | bytes 18440 | tf_op jit(solution)/shard_map/ppermute | solution.py:13
  7.0 1.3 %collective-permute-start.3 = (bf16[512,128]{1,0:T(8,128)(2,1)}, bf16[512,128]{1,0:T(8,128)(2,1)S(1)}, u32[]{:S(2)}, u32[]{:S(2)}) collective-permute-start(bf16[512,128]{1,0:T(8,128)(2,1)} %param.4), channel_id=1, source_target_pairs={{4,0},{8,4},{12,8},{16,12},{20,16},{24,20},{28,24},{5,1},{9,5},{13... | collective-permute-start | bytes 393224 | tf_op jit(solution)/shard_map/ppermute | solution.py:13
  8.3 5.2 %collective-permute-start.2 = (bf16[512,128]{1,0:T(8,128)(2,1)}, bf16[512,128]{1,0:T(8,128)(2,1)S(1)}, u32[]{:S(2)}, u32[]{:S(2)}) collective-permute-start(bf16[512,128]{1,0:T(8,128)(2,1)} %param.4), channel_id=1, source_target_pairs={{0,4},{4,8},{8,12},{12,16},{16,20},{20,24},{24,28},{1,5},{5,9},{9,... | collective-permute-start | bytes 393224 | tf_op jit(solution)/shard_map/ppermute | solution.py:13
  13.5 1.2 %dynamic-slice = u32[1]{0:T(128)} dynamic-slice(u32[32]{0:T(128)} %constant.82, u32[]{:T(128)S(6)} %add.135), dynamic_slice_sizes={1} | dynamic-slice | bytes 12
  15.4 0.8 bitcast_dynamic-update-slice_fusion
  16.1 4.9 %all-reduce = s32[256]{0:T(256)S(1)} all-reduce(s32[256]{0:T(256)S(1)} %bitcast_dynamic-update-slice_fusion), channel_id=1, replica_groups=mesh['node'=8,'rep'=4] {'rep'}, use_global_device_ids=true, to_apply=%add | all-reduce | flops 256 | bytes 2048 | tf_op jit(solution)/shard_map/squeeze | solution.py:27
  21.1 0.6 reduce-window.6
  21.7 0.2 slice_reduce_fusion.3
  21.9 0.1 fusion.15
  22.1 1.4 %scatter_custom_fusion = s32[584]{0:T(1024)S(1)} fusion(s32[256]{0:T(256)S(1)} %bitcast.52, s32[256]{0:T(256)S(1)} %get-tuple-element.13, s32[]{:T(128)} %constant.26.clone.1), kind=kCustom, calls=%fused_computation.51 | custom fusion | bytes 2340 | tf_op jit(solution)/shard_map/scatter | solution.py:40
  23.5 0.7 all_to_all.17
  24.1 6.3 %all-to-all-start = ((s32[8,1,73]{2,1,0:T(1,128)}), s32[8,1,73]{2,1,0:T(1,128)S(1)}, u32[]{:S(2)}, u32[]{:S(2)}) async-start(s32[8,1,73]{2,1,0:T(1,128)} %all_to_all.17), calls=%async_computation | async-start | bytes 8192 | tf_op jit(solution)/shard_map/all_to_all | solution.py:56
  30.4 0.8 fusion.32
  31.2 0.8 copy.12
  32.1 4.8 %all-to-all-done = s32[8,1,73]{2,1,0:T(1,128)S(1)} async-done(((s32[8,1,73]{2,1,0:T(1,128)}), s32[8,1,73]{2,1,0:T(1,128)S(1)}, u32[]{:S(2)}, u32[]{:S(2)}) %all-to-all-start) | async-done | bytes 2368 | tf_op jit(solution)/shard_map/all_to_all | solution.py:56
  36.8 0.1 reshape.236
  36.9 0.5 broadcast.315
  37.4 0.7 reduce.19
  38.1 0.1 reshape.231
  38.2 1.9 %gather_fusion.2 = bf16[584,128]{1,0:T(8,128)(2,1)S(1)} fusion(bf16[512,128]{1,0:T(8,128)(2,1)S(1)} %copy-done, s32[1024]{0:T(1024)S(1)} %pad_clamp_fusion), kind=kCustom, calls=%fused_computation.2 | custom fusion | bytes 301344 | tf_op jit(solution)/shard_map/gather | solution.py:58
  40.2 0.7 reshape.288
  40.9 1.6 %gather_fusion = f32[584,3]{1,0:T(8,128)S(1)} fusion(f32[3,512]{0,1:T(8,128)S(1)} %copy.12, s32[1024]{0:T(1024)S(1)} %pad_clamp_fusion), kind=kCustom, calls=%fused_computation | custom fusion | bytes 16352 | tf_op jit(solution)/shard_map/gather | solution.py:57
  42.5 0.1 copy.13
  42.7 0.1 reshape.239
  42.8 0.7 reshape.320
  43.5 3.3 %all-to-all-start.1 = ((f32[8,1,219]{2,1,0:T(1,128)}), f32[8,1,219]{2,1,0:T(1,128)S(1)}, u32[]{:S(2)}, u32[]{:S(2)}) async-start(f32[8,1,219]{2,1,0:T(1,128)} %reshape.320), calls=%async_computation.1 | async-start | bytes 16384 | tf_op jit(solution)/shard_map/all_to_all | solution.py:60
  46.8 0.0 collective-permute-done
  46.9 0.1 slice_reduce_fusion.6
  46.9 6.3 %all-to-all-done.1 = f32[8,1,219]{2,1,0:T(1,128)S(1)} async-done(((f32[8,1,219]{2,1,0:T(1,128)}), f32[8,1,219]{2,1,0:T(1,128)S(1)}, u32[]{:S(2)}, u32[]{:S(2)}) %all-to-all-start.1) | async-done | bytes 7040 | tf_op jit(solution)/shard_map/all_to_all | solution.py:60
  53.3 3.4 %all-to-all-start.2 = ((bf16[8,73,128]{2,1,0:T(8,128)(2,1)}), bf16[8,73,128]{2,1,0:T(8,128)(2,1)S(1)}, u32[]{:S(2)}, u32[]{:S(2)}) async-start(bf16[8,73,128]{2,1,0:T(8,128)(2,1)} %reshape.288), calls=%async_computation.2 | async-start | bytes 327680 | tf_op jit(solution)/shard_map/all_to_all | solution.py:61
  56.7 0.5 broadcast.317
  57.2 0.7 reduce.20
  57.8 0.1 reshape.321
  57.9 0.2 copy.15
  58.1 1.4 %gather_fusion.1 = f32[256,3]{1,0:T(8,128)S(1)} fusion(f32[8,3,73]{1,0,2:T(8,128)S(1)} %copy.15, s32[256]{0:T(256)S(1)} %bitcast.35), kind=kCustom, calls=%fused_computation.1 | custom fusion | bytes 8192 | tf_op jit(solution)/shard_map/gather | solution.py:65
  59.5 0.3 slice_reduce_fusion.2
  59.8 0.5 fusion.8
  60.3 1.2 %scatter_custom_fusion.1 = f32[584,128]{1,0:T(8,128)S(1)} fusion(s32[256]{0:T(256)S(1)} %bitcast.53, f32[256,128]{1,0:T(8,128)S(1)} %fusion.8, f32[]{:T(128)} %constant.52.clone.1), kind=kCustom, calls=%fused_computation.20 | custom fusion | bytes 299012 | tf_op jit(solution)/shard_map/scatter | solution.py:74
  61.5 0.7 reshape.232
  62.2 1.9 %all-to-all-done.2 = bf16[8,73,128]{2,1,0:T(8,128)(2,1)S(1)} async-done(((bf16[8,73,128]{2,1,0:T(8,128)(2,1)}), bf16[8,73,128]{2,1,0:T(8,128)(2,1)S(1)}, u32[]{:S(2)}, u32[]{:S(2)}) %all-to-all-start.2) | async-done | bytes 149536 | tf_op jit(solution)/shard_map/all_to_all | solution.py:61
  64.2 4.0 %all-to-all-start.3 = ((f32[8,73,128]{2,1,0:T(8,128)}), f32[8,73,128]{2,1,0:T(8,128)S(1)}, u32[]{:S(2)}, u32[]{:S(2)}) async-start(f32[8,73,128]{2,1,0:T(8,128)} %reshape.232), calls=%async_computation.3 | async-start | bytes 655360 | tf_op jit(solution)/shard_map/all_to_all | solution.py:76
  68.2 1.5 %gather_fusion.3 = bf16[256,128]{1,0:T(8,128)(2,1)S(1)} fusion(bf16[8,73,128]{2,0,1:T(8,128)(2,1)S(1)} %copy.18, s32[256]{0:T(256)S(1)} %bitcast.36), kind=kCustom, calls=%fused_computation.3 | custom fusion | bytes 133120 | tf_op jit(solution)/shard_map/gather | solution.py:68
  69.7 0.4 fusion.9
  70.1 0.0 collective-permute-done.3
  70.2 2.1 %fusion.2 = bf16[512,128]{1,0:T(8,128)(2,1)} fusion(f32[512,128]{1,0:T(8,128)S(1)} %fusion.9, f32[1536]{0:T(1024)S(1)} %get-tuple-element.6, f32[512]{0:T(512)S(1)} %bitcast.51, f32[1536]{0:T(1024)S(1)} %get-tuple-element.7, f32[512]{0:T(512)S(1)} %bitcast.48, f32[1536]{0:T(1024)S(1)} %get-tuple-element.5, f32[512]{0:T(512)S(1)} %bitcast.45, ...), kind=kOutput, calls=%fused_computation.10 | convolution fusion | flops 211288064 | bytes 811008 | tf_op jit(solution)/shard_map/dot_general | solution.py:53
  72.2 4.6 %all-to-all-done.3 = f32[8,73,128]{2,1,0:T(8,128)S(1)} async-done(((f32[8,73,128]{2,1,0:T(8,128)}), f32[8,73,128]{2,1,0:T(8,128)S(1)}, u32[]{:S(2)}, u32[]{:S(2)}) %all-to-all-start.3) | async-done | bytes 299040 | tf_op jit(solution)/shard_map/all_to_all | solution.py:76
  76.9 6.9 %scatter_custom_fusion.2 = f32[512,128]{1,0:T(8,128)} fusion(s32[584]{0:T(1024)S(1)} %fusion.17, f32[584,128]{1,0:T(8,128)S(1)} %reshape.282, f32[]{:T(128)} %constant.52.clone.1), kind=kCustom, calls=%fused_computation.25 | custom fusion | flops 74752 | bytes 262148 | tf_op jit(solution)/shard_map/scatter-add | solution.py:86
  (23 shorter events, 0.2 us)
Async XLA Ops:
  0.6 37.6 %copy-start = (bf16[512,128]{1,0:T(8,128)(2,1)S(1)}, bf16[512,128]{1,0:T(8,128)(2,1)}, u32[]{:S(2)}) copy-start(bf16[512,128]{1,0:T(8,128)(2,1)} %param.4) | copy-start | bytes 393220
  0.6 46.2 %collective-permute-start = (f32[3,512]{1,0:T(4,128)}, f32[3,512]{1,0:T(4,128)S(1)}, u32[]{:S(2)}, u32[]{:S(2)}) collective-permute-start(f32[3,512]{1,0:T(4,128)} %param.3), channel_id=1, source_target_pairs={{0,4},{4,8},{8,12},{12,16},{16,20},{20,24},{24,28},{1,5},{5,9},{9,... | collective-permute-start | bytes 18440 | tf_op jit(solution)/shard_map/ppermute | solution.py:13
  5.7 41.2 %collective-permute-start.1 = (f32[3,512]{1,0:T(4,128)}, f32[3,512]{1,0:T(4,128)S(1)}, u32[]{:S(2)}, u32[]{:S(2)}) collective-permute-start(f32[3,512]{1,0:T(4,128)} %param.3), channel_id=1, source_target_pairs={{4,0},{8,4},{12,8},{16,12},{20,16},{24,20},{28,24},{5,1},{9,5},{13... | collective-permute-start | bytes 18440 | tf_op jit(solution)/shard_map/ppermute | solution.py:13
  7.0 63.2 %collective-permute-start.3 = (bf16[512,128]{1,0:T(8,128)(2,1)}, bf16[512,128]{1,0:T(8,128)(2,1)S(1)}, u32[]{:S(2)}, u32[]{:S(2)}) collective-permute-start(bf16[512,128]{1,0:T(8,128)(2,1)} %param.4), channel_id=1, source_target_pairs={{4,0},{8,4},{12,8},{16,12},{20,16},{24,20},{28,24},{5,1},{9,5},{13... | collective-permute-start | bytes 393224 | tf_op jit(solution)/shard_map/ppermute | solution.py:13
  8.3 61.9 %collective-permute-start.2 = (bf16[512,128]{1,0:T(8,128)(2,1)}, bf16[512,128]{1,0:T(8,128)(2,1)S(1)}, u32[]{:S(2)}, u32[]{:S(2)}) collective-permute-start(bf16[512,128]{1,0:T(8,128)(2,1)} %param.4), channel_id=1, source_target_pairs={{0,4},{4,8},{8,12},{12,16},{16,20},{20,24},{24,28},{1,5},{5,9},{9,... | collective-permute-start | bytes 393224 | tf_op jit(solution)/shard_map/ppermute | solution.py:13
  24.1 12.7 %all-to-all-start = ((s32[8,1,73]{2,1,0:T(1,128)}), s32[8,1,73]{2,1,0:T(1,128)S(1)}, u32[]{:S(2)}, u32[]{:S(2)}) async-start(s32[8,1,73]{2,1,0:T(1,128)} %all_to_all.17), calls=%async_computation | async-start | bytes 8192 | tf_op jit(solution)/shard_map/all_to_all | solution.py:56
  40.9 5.9 %copy-start.1 = (f32[3,512]{1,0:T(4,128)S(1)}, f32[3,512]{1,0:T(4,128)}, u32[]{:S(2)}) copy-start(f32[3,512]{1,0:T(4,128)} %param.3) | copy-start | bytes 18436
  43.5 9.8 %all-to-all-start.1 = ((f32[8,1,219]{2,1,0:T(1,128)}), f32[8,1,219]{2,1,0:T(1,128)S(1)}, u32[]{:S(2)}, u32[]{:S(2)}) async-start(f32[8,1,219]{2,1,0:T(1,128)} %reshape.320), calls=%async_computation.1 | async-start | bytes 16384 | tf_op jit(solution)/shard_map/all_to_all | solution.py:60
  53.3 10.9 %all-to-all-start.2 = ((bf16[8,73,128]{2,1,0:T(8,128)(2,1)}), bf16[8,73,128]{2,1,0:T(8,128)(2,1)S(1)}, u32[]{:S(2)}, u32[]{:S(2)}) async-start(bf16[8,73,128]{2,1,0:T(8,128)(2,1)} %reshape.288), calls=%async_computation.2 | async-start | bytes 327680 | tf_op jit(solution)/shard_map/all_to_all | solution.py:61
  64.2 12.7 %all-to-all-start.3 = ((f32[8,73,128]{2,1,0:T(8,128)}), f32[8,73,128]{2,1,0:T(8,128)S(1)}, u32[]{:S(2)}, u32[]{:S(2)}) async-start(f32[8,73,128]{2,1,0:T(8,128)} %reshape.232), calls=%async_computation.3 | async-start | bytes 655360 | tf_op jit(solution)/shard_map/all_to_all | solution.py:76
where the time goes:
time: 84.5 us; the launch traced here: 83.8 us
  starting transfers between devices  29.8 us (35%)
  local copies, waits for them, and re-layouts  17.9 us (21%)
  waiting for transfers between devices  17.6 us (21%)
  other arithmetic  9.02 us (11%)
  blocking collectives  4.9 us (6%)
  matrix products  2.95 us (3%)
  between operations  1.56 us (2%)
    ppermute x4, starting transfers between devices, passed_along(): return lax.ppermute(block, axis, route)  12.8 us
    scatter-add x1, other arithmetic, on_device(): col_total = jnp.zeros((leaf_size, samp_dev), jnp.float32).at[asked_rows.r...  6.9 us
    all_to_all x1, waiting for transfers between devices, on_device(): lax.all_to_all(asked_points, 'node', split_axis=0, concat_axis=0, tiled=T...  6.33 us
    all_to_all x1, starting transfers between devices, on_device(): lax.all_to_all(request, 'node', split_axis=0, concat_axis=0, tiled=True)  6.28 us
    squeeze x1, blocking collectives, on_device(): listed = lax.all_gather(skeleton, 'rep', axis=1, tiled=True)[0]  4.9 us
    all_to_all x1, waiting for transfers between devices, on_device(): lax.all_to_all(request, 'node', split_axis=0, concat_axis=0, tiled=True)  4.76 us
    all_to_all x1, waiting for transfers between devices, on_device(): lax.all_to_all(outgoing.reshape(node_count, capacity, samp_dev), 'node',...  4.62 us
    all_to_all x1, starting transfers between devices, on_device(): lax.all_to_all(outgoing.reshape(node_count, capacity, samp_dev), 'node',...  4.02 us
  transfers between devices with their start and end apart: 8, of which 4 were waited for; matrix products, arithmetic and copies ran while one was open for 27% of the time, Pallas kernels for 0%

commit v1 on v0

v1 whole, which is shorter than its diff:
```python
import functools

import jax
import jax.numpy as jnp
from jax import lax
from jax.experimental import pallas as pl
from jax.experimental.pallas import tpu as pltpu
from jax.sharding import PartitionSpec as P

kernel_scale = 0.0078125
softening = 0.02
stretch = 1.0 / kernel_scale
soft_term = softening * softening
TERMS = 3
LANES = 128

VMEM = pl.BlockSpec(memory_space=pltpu.VMEM)
ROOM = pltpu.CompilerParams(vmem_limit_bytes=12 * 1024 * 1024)


def place_of(node, n):
    return jnp.where(node % 2 == 0, node // 2, n - 1 - node // 2)


def node_at(place, n):
    place = lax.rem(place + n, n)
    return jnp.where(place < (n + 1) // 2, 2 * place, 2 * (n - 1 - place) + 1)


def around(distance, n):
    return node_at(place_of(lax.axis_index("node"), n) + distance, n)


def coord_rows(leaf):
    rows = 3 * TERMS * (leaf // LANES)
    return -(-rows // 16) * 16


def prep_kernel(coords_ref, omega_ref, msg_ref, wide_ref):
    leaf = coords_ref.shape[1]
    chunks = leaf // LANES
    msg_ref[0:leaf, :] = omega_ref[...]
    scaled = coords_ref[...] * stretch
    rows = []
    for c in range(3):
        rest = scaled[c : c + 1, :]
        for _ in range(TERMS):
            term = rest.astype(jnp.bfloat16).astype(jnp.float32)
            rest = rest - term
            rows += [term[:, k * LANES : (k + 1) * LANES] for k in range(chunks)]
    pad = coord_rows(leaf) - len(rows)
    rows.append(jnp.zeros((pad, LANES), jnp.float32))
    msg_ref[leaf:, :] = jnp.concatenate(rows, axis=0).astype(jnp.bfloat16)
    eight = jnp.concatenate([scaled, jnp.zeros((5, leaf), jnp.float32)], axis=0)
    columns = eight.T
    for c in range(3):
        wide_ref[c] = jnp.broadcast_to(columns[:, c : c + 1], (leaf, LANES))


def prep(coords, omega):
    leaf = coords.shape[1]
    return pl.pallas_call(
        prep_kernel,
        out_shape=(
            jax.ShapeDtypeStruct((leaf + coord_rows(leaf), LANES), jnp.bfloat16),
            jax.ShapeDtypeStruct((3, leaf, LANES), jnp.float32),
        ),
        in_specs=[VMEM, VMEM],
        out_specs=(VMEM, VMEM),
        compiler_params=ROOM,
        name="prep",
    )(coords, omega)


def block_entries(wide_ref, msg_ref, tile_ref):
    leaf = wide_ref.shape[1]
    chunks = leaf // LANES
    tail = msg_ref[leaf:, :].astype(jnp.float32)
    for k in range(chunks):
        target = []
        for c in range(3):
            row = [tail[(c * TERMS + t) * chunks + k : (c * TERMS + t) * chunks + k + 1, :] for t in range(TERMS)]
            target.append((row[0] + row[1]) + row[2])
        step = 64
        for p in range(0, leaf, step):
            squared = (wide_ref[0, p : p + step, :] - target[0]) ** 2
            squared = squared + (wide_ref[1, p : p + step, :] - target[1]) ** 2
            squared = squared + (wide_ref[2, p : p + step, :] - target[2]) ** 2
            entry = lax.rsqrt(squared + soft_term * stretch * stretch)
            tile_ref[p : p + step, k * LANES : (k + 1) * LANES] = entry.astype(jnp.bfloat16)


def count_wide(lists_ref, first, rows, start, leaf):
    points = lax.broadcasted_iota(jnp.int32, (leaf, LANES), 0) + start
    total = jnp.zeros((leaf, LANES), jnp.float32)
    hits = [
        (points == lists_ref[pl.ds(first + r, 1), :]).astype(jnp.float32).astype(jnp.bfloat16)
        for r in range(rows)
    ]
    ones = jnp.ones((LANES, LANES), jnp.bfloat16)
    for hit in hits:
        total = total + jnp.dot(hit, ones, preferred_element_type=jnp.float32)
    return total


def own_kernel(wide_ref, msg_ref, row_ref, tile_ref):
    leaf = wide_ref.shape[1]
    block_entries(wide_ref, msg_ref, tile_ref)
    row_ref[...] = jnp.dot(tile_ref[...], msg_ref[0:leaf, :], preferred_element_type=jnp.float32)


def own_block(wide, msg):
    leaf = wide.shape[1]
    return pl.pallas_call(
        own_kernel,
        out_shape=jax.ShapeDtypeStruct((leaf, LANES), jnp.float32),
        in_specs=[VMEM, VMEM],
        out_specs=VMEM,
        scratch_shapes=[pltpu.VMEM((leaf, leaf), jnp.bfloat16)],
        compiler_params=ROOM,
        name="own_block",
    )(wide, msg)


def step_kernel(n, away, list_rows, wide_ref, mine_ref, row_in_ref, *refs):
    count = len(away)
    blocks, outs = refs[:count], refs[count : 2 * count]
    row_ref, tile_ref = refs[2 * count], refs[2 * count + 1]
    leaf = wide_ref.shape[1]
    me = lax.axis_index("node")
    total = row_in_ref[...]
    for b in range(count):
        block_entries(wide_ref, blocks[b], tile_ref)
        node = around(away[b], n)
        near = jnp.where(jnp.abs(node - me) <= 1, 1.0, 0.0)
        samples = blocks[b][0:leaf, :]
        weight = count_wide(mine_ref, 0, list_rows, node * leaf, leaf) + near
        weighted = (weight * samples.astype(jnp.float32)).astype(jnp.bfloat16)
        both = jnp.dot(
            tile_ref[...], jnp.concatenate([samples, weighted], axis=1), preferred_element_type=jnp.float32
        )
        outs[b][...] = both[:, :LANES]
        total = total + both[:, LANES:]
    row_ref[...] = total


def step_blocks(n, away, wide, mine, row, blocks):
    leaf = wide.shape[1]
    count = len(blocks)
    part = jax.ShapeDtypeStruct((leaf, LANES), jnp.float32)
    outs = pl.pallas_call(
        functools.partial(step_kernel, n, away, mine.shape[0]),
        out_shape=[part] * (count + 1),
        in_specs=[VMEM] * (3 + count),
        out_specs=[VMEM] * (count + 1),
        scratch_shapes=[pltpu.VMEM((leaf, leaf), jnp.bfloat16)],
        compiler_params=ROOM,
        name="step_blocks",
    )(wide, mine, row, *blocks)
    return outs[:count], outs[count]


def last_kernel(n, away, list_rows, lists_ref, row_in_ref, *refs):
    count = len(away)
    parts, row_ref, col_ref = refs[:count], refs[count], refs[count + 1]
    leaf = row_in_ref.shape[0]
    me = lax.axis_index("node")
    row_ref[...] = row_in_ref[...].astype(row_ref.dtype)
    total = jnp.zeros_like(row_in_ref)
    for b in range(count):
        slot = around(away[b], n) ^ me
        mask = count_wide(lists_ref, slot * list_rows, list_rows, me * leaf, leaf)
        total = total + mask * parts[b][...]
    col_ref[...] = total


def finish(n, away, lists, list_rows, row, parts):
    leaf = row.shape[0]
    return pl.pallas_call(
        functools.partial(last_kernel, n, away, list_rows),
        out_shape=(
            jax.ShapeDtypeStruct((leaf, LANES), jnp.bfloat16),
            jax.ShapeDtypeStruct((leaf, LANES), jnp.float32),
        ),
        in_specs=[VMEM] * (2 + len(parts)),
        out_specs=(VMEM, VMEM),
        compiler_params=ROOM,
        name="finish",
    )(lists, row, *parts)


def swap(block, axis, bit):
    return lax.ppermute(block, axis, [(i, i ^ bit) for i in range(lax.axis_size(axis))])


def on_device(coords, omega, skeleton):
    n = lax.axis_size("node")
    reps = lax.axis_size("rep")
    cycle = list(range(0, n, 2)) + list(range(n - 1 - n % 2, 0, -2))
    hops = [(cycle[k], cycle[(k + 1) % n]) for k in range(n)]
    back = [(b, a) for a, b in hops]

    msg, wide = prep(coords, omega)
    ahead, behind = [msg], [msg]
    for s in range(1, n // 2 + 1):
        ahead.append(lax.ppermute(ahead[-1], "node", hops))
        if s < n - s:
            behind.append(lax.ppermute(behind[-1], "node", back))

    mine = skeleton
    bit = 1
    while bit < reps:
        mine = jnp.concatenate([mine, swap(mine, "rep", bit)], axis=1 if mine.shape[1] < LANES else 0)
        bit *= 2
    list_rows = mine.shape[0]
    lists = mine
    bit = 1
    while bit < n:
        lists = jnp.concatenate([lists, swap(lists, "node", bit)], axis=0)
        bit *= 2

    row = own_block(wide, msg)
    parts, away = [], []
    for s in range(1, n // 2 + 1):
        blocks, at = [ahead[s]], [-s]
        if s < n - s:
            blocks.append(behind[s])
            at.append(s)
        outs, row = step_blocks(n, at, wide, mine, row, blocks)
        parts += outs
        away += at
    return finish(n, away, lists, list_rows, row, parts)


def solution(mesh):
    in_specs = (P(None, "node"), P("node", "rep"), P("node", "rep"))
    out_specs = (P("node", "rep"), P("node", "rep"))
    return jax.shard_map(on_device, mesh=mesh, in_specs=in_specs, out_specs=out_specs, check_vma=False)
```

time: 84.5 us -> 38.5 us (0.46)
  local copies, waits for them, and re-layouts: 17.9 us -> 1.62 us
  starting transfers between devices: 29.8 us -> 14.9 us
  other arithmetic: 9.02 us -> 0.3 us
  Pallas kernels: 0 us -> 7.3 us
  blocking collectives: 4.9 us -> 0 us
  waiting for transfers between devices: 17.6 us -> 13.4 us
  matrix products: 2.95 us -> 0 us
  between operations: 1.56 us -> 0.71 us
    all_to_all x4 -> x0, waiting for transfers between devices: 17.6 us -> none  [the longest x1 6.33 us: on_device(): lax.all_to_all(asked_points, 'node', split_axis=0, concat_axis=0, tiled=T...]
    all_to_all x4 -> x0, starting transfers between devices: 17 us -> none  [the longest x1 6.28 us: on_device(): lax.all_to_all(request, 'node', split_axis=0, concat_axis=0, tiled=True)]
    ppermute x4 -> x12, waiting for transfers between devices: 0.01 us -> 13.4 us  [the longest x4 6.71 us: on_device(): ahead.append(lax.ppermute(ahead[-1], 'node', hops))]
    pallas_call x0 -> x7, Pallas kernels: none -> 7.3 us  [the longest x4 4.87 us: step_blocks(): pl.pallas_call(functools.partial(step_kernel, n, away, mine.shape[0]), ou...]
    scatter-add x1 -> x0, other arithmetic: 6.9 us -> none  [on_device(): col_total = jnp.zeros((leaf_size, samp_dev), jnp.float32).at[asked_rows.r...]
    gather x6 -> x0, local copies, waits for them, and re-layouts: 6.69 us -> none  [the longest x1 1.95 us: on_device(): asked_samples = omega[asked_rows]]
    squeeze x1 -> x0, blocking collectives: 4.9 us -> none  [on_device(): listed = lax.all_gather(skeleton, 'rep', axis=1, tiled=True)[0]]
    dot_general x3 -> x0, matrix products: 2.95 us -> none  [the longest x1 2.06 us: on_device(): jnp.dot(kernel_tile(coords, wide_points), wide_rows, preferred_element_ty...]
  transfers between devices with their start and end apart: 8 -> 12, of which waited for: 4 -> 6; matrix products, arithmetic and copies ran while one was open for 27% -> 1% of each run, Pallas kernels for 0% -> 12%
where the time goes in v1:
time: 38.5 us; the launch traced here: 38.3 us
  starting transfers between devices  14.9 us (39%)
  waiting for transfers between devices  13.4 us (35%)
  Pallas kernels  7.3 us (19%)
  local copies, waits for them, and re-layouts  1.62 us (4%)
  between operations  0.71 us (2%)
    ppermute x4, starting transfers between devices, on_device(): ahead.append(lax.ppermute(ahead[-1], 'node', hops))  6.93 us
    ppermute x4, waiting for transfers between devices, on_device(): ahead.append(lax.ppermute(ahead[-1], 'node', hops))  6.71 us
    ppermute x5, waiting for transfers between devices, swap(): lax.ppermute(block, axis, [(i, i ^ bit) for i in range(lax.axis_size(axis...  6.7 us
    ppermute x5, starting transfers between devices, swap(): lax.ppermute(block, axis, [(i, i ^ bit) for i in range(lax.axis_size(axis...  5.89 us
    pallas_call x4, Pallas kernels, step_blocks(): pl.pallas_call(functools.partial(step_kernel, n, away, mine.shape[0]), ou...  4.87 us
    ppermute x3, starting transfers between devices, on_device(): behind.append(lax.ppermute(behind[-1], 'node', back))  2.09 us
    unnamed x6, local copies, waits for them, and re-layouts  1.6 us
    pallas_call x1, Pallas kernels, finish(): pl.pallas_call(functools.partial(last_kernel, n, away, list_rows), out_sh...  1.37 us
  transfers between devices with their start and end apart: 12, of which 6 were waited for; matrix products, arithmetic and copies ran while one was open for 1% of the time, Pallas kernels for 12%

profile of v1, /device:TPU:0, one launch (start us, length us, event | category | flops | bytes accessed | tf_op | source)
XLA Modules:
  0.0 38.3 jit_solution(13773133842681198011)
XLA Ops:
  0.6 0.0 copy-start
  0.6 0.9 %copy-done = bf16[512,128]{1,0:T(8,128)(2,1)S(1)} copy-done((bf16[512,128]{1,0:T(8,128)(2,1)S(1)}, bf16[512,128]{1,0:T(8,128)(2,1)}, u32[]{:S(2)}) %copy-start) | copy-done | bytes 131096
  1.5 0.0 copy-start.1
  1.5 0.7 %copy-done.1 = f32[3,512]{1,0:T(4,128)S(1)} copy-done((f32[3,512]{1,0:T(4,128)S(1)}, f32[3,512]{1,0:T(4,128)}, u32[]{:S(2)}) %copy-start.1) | copy-done | bytes 6168
  2.2 0.5 %prep.1 = (bf16[560,128]{1,0:T(8,128)(2,1)S(1)}, f32[3,512,128]{2,1,0:T(8,128)S(1)}) custom-call(f32[3,512]{1,0:T(4,128)S(1)} %copy-done.1, bf16[512,128]{1,0:T(8,128)(2,1)S(1)} %copy-done), custom_call_target="tpu_custom_call" | custom-call | tf_op jit(solution)/shard_map/prep/pallas_call | solution.py:62
  2.7 0.0 copy-start.2
  2.7 3.1 %collective-permute-start.5 = (bf16[560,128]{1,0:T(8,128)(2,1)S(1)}, bf16[560,128]{1,0:T(8,128)(2,1)S(1)}, u32[]{:S(2)}, u32[]{:S(2)}) collective-permute-start(bf16[560,128]{1,0:T(8,128)(2,1)S(1)} %get-tuple-element.16.msg_ref), channel_id=1, source_target_pairs={{0,8},{8,16},{16,24},{24,28},{28,20},{20,12},{12,4},{4,0},{1,9},{9... | collective-permute-start | bytes 430088 | tf_op jit(solution)/shard_map/ppermute | solution.py:206
  5.8 0.0 collective-permute-start.6
  5.8 3.7 %collective-permute-done.5.refs_0_ = bf16[560,128]{1,0:T(8,128)(2,1)S(1)} collective-permute-done((bf16[560,128]{1,0:T(8,128)(2,1)S(1)}, bf16[560,128]{1,0:T(8,128)(2,1)S(1)}, u32[]{:S(2)}, u32[]{:S(2)}) %collective-permute-start.5) | collective-permute-done | bytes 143392 | tf_op jit(solution)/shard_map/ppermute | solution.py:206
  9.5 1.8 %collective-permute-start.7 = (bf16[560,128]{1,0:T(8,128)(2,1)S(1)}, bf16[560,128]{1,0:T(8,128)(2,1)S(1)}, u32[]{:S(2)}, u32[]{:S(2)}) collective-permute-start(bf16[560,128]{1,0:T(8,128)(2,1)S(1)} %collective-permute-done.5.refs_0_), channel_id=1, source_target_pairs={{0,8},{8,16},{16,24},{24,28},{28,20},{20,12},{12,4},{4,0},{1,9},{9... | collective-permute-start | bytes 430088 | tf_op jit(solution)/shard_map/ppermute | solution.py:206
  11.3 0.0 copy-done.2
  11.3 0.0 collective-permute-start
  11.3 0.0 collective-permute-done.6.refs_1_
  11.3 0.3 collective-permute-start.8
  11.6 3.0 %collective-permute-done.7.refs_0_ = bf16[560,128]{1,0:T(8,128)(2,1)S(1)} collective-permute-done((bf16[560,128]{1,0:T(8,128)(2,1)S(1)}, bf16[560,128]{1,0:T(8,128)(2,1)S(1)}, u32[]{:S(2)}, u32[]{:S(2)}) %collective-permute-start.7) | collective-permute-done | bytes 143392 | tf_op jit(solution)/shard_map/ppermute | solution.py:206
  14.6 1.8 %collective-permute-start.9 = (bf16[560,128]{1,0:T(8,128)(2,1)S(1)}, bf16[560,128]{1,0:T(8,128)(2,1)S(1)}, u32[]{:S(2)}, u32[]{:S(2)}) collective-permute-start(bf16[560,128]{1,0:T(8,128)(2,1)S(1)} %collective-permute-done.7.refs_0_), channel_id=1, source_target_pairs={{0,8},{8,16},{16,24},{24,28},{28,20},{20,12},{12,4},{4,0},{1,9},{9... | collective-permute-start | bytes 430088 | tf_op jit(solution)/shard_map/ppermute | solution.py:206
  16.4 0.0 collective-permute-done
  16.4 0.1 pad_add_fusion.3
  16.5 1.5 %collective-permute-start.1 = (s32[1,128]{1,0:T(1,128)S(1)}, s32[1,128]{1,0:T(1,128)S(1)}, u32[]{:S(2)}, u32[]{:S(2)}) collective-permute-start(s32[1,128]{1,0:T(1,128)S(1)} %pad_add_fusion.3), channel_id=1, source_target_pairs={{0,2},{1,3},{2,0},{3,1},{4,6},{5,7},{6,4},{7,5},{8,10},{9,11},{10,... | collective-permute-start | bytes 1544 | tf_op jit(solution)/shard_map/ppermute | solution.py:193
  18.0 2.1 %collective-permute-done.1 = s32[1,128]{1,0:T(1,128)S(1)} collective-permute-done((s32[1,128]{1,0:T(1,128)S(1)}, s32[1,128]{1,0:T(1,128)S(1)}, u32[]{:S(2)}, u32[]{:S(2)}) %collective-permute-start.1) | collective-permute-done | bytes 544 | tf_op jit(solution)/shard_map/ppermute | solution.py:193
  20.1 0.1 pad_add_fusion.2.mine_ref
  20.1 0.2 collective-permute-start.2
  20.4 0.0 collective-permute-done.8.refs_1_
  20.4 1.8 %collective-permute-start.10 = (bf16[560,128]{1,0:T(8,128)(2,1)S(1)}, bf16[560,128]{1,0:T(8,128)(2,1)S(1)}, u32[]{:S(2)}, u32[]{:S(2)}) collective-permute-start(bf16[560,128]{1,0:T(8,128)(2,1)S(1)} %collective-permute-done.8.refs_1_), channel_id=1, source_target_pairs={{8,0},{16,8},{24,16},{28,24},{20,28},{12,20},{4,12},{0,4},{9,1},{1... | collective-permute-start | bytes 430088 | tf_op jit(solution)/shard_map/ppermute | solution.py:208
  22.2 0.0 collective-permute-done.9.refs_0_
  22.2 0.2 collective-permute-start.11
  22.4 1.3 %collective-permute-done.2 = s32[2,128]{1,0:T(2,128)S(1)} collective-permute-done((s32[2,128]{1,0:T(2,128)S(1)}, s32[2,128]{1,0:T(2,128)S(1)}, u32[]{:S(2)}, u32[]{:S(2)}) %collective-permute-start.2) | collective-permute-done | bytes 1056 | tf_op jit(solution)/shard_map/ppermute | solution.py:193
  23.7 0.1 pad_add_fusion.1
  23.8 1.6 %collective-permute-start.3 = (s32[4,128]{1,0:T(4,128)S(1)}, s32[4,128]{1,0:T(4,128)S(1)}, u32[]{:S(2)}, u32[]{:S(2)}) collective-permute-start(s32[4,128]{1,0:T(4,128)S(1)} %pad_add_fusion.1), channel_id=1, source_target_pairs={{0,8},{4,12},{8,0},{12,4},{16,24},{20,28},{24,16},{28,20},{1,9},{5... | collective-permute-start | bytes 6152 | tf_op jit(solution)/shard_map/ppermute | solution.py:193
  25.4 2.0 %collective-permute-done.3 = s32[4,128]{1,0:T(4,128)S(1)} collective-permute-done((s32[4,128]{1,0:T(4,128)S(1)}, s32[4,128]{1,0:T(4,128)S(1)}, u32[]{:S(2)}, u32[]{:S(2)}) %collective-permute-start.3) | collective-permute-done | bytes 2080 | tf_op jit(solution)/shard_map/ppermute | solution.py:193
  27.4 0.1 pad_add_fusion
  27.4 2.6 %collective-permute-start.4 = (s32[8,128]{1,0:T(8,128)S(1)}, s32[8,128]{1,0:T(8,128)S(1)}, u32[]{:S(2)}, u32[]{:S(2)}) collective-permute-start(s32[8,128]{1,0:T(8,128)S(1)} %pad_add_fusion), channel_id=1, source_target_pairs={{0,16},{4,20},{8,24},{12,28},{16,0},{20,4},{24,8},{28,12},{1,17},{... | collective-permute-start | bytes 12296 | tf_op jit(solution)/shard_map/ppermute | solution.py:193
  30.0 0.6 %own_block.1.row_in_ref = f32[512,128]{1,0:T(8,128)S(1)} custom-call(f32[3,512,128]{2,1,0:T(8,128)S(1)} %get-tuple-element.15.wide_ref, bf16[560,128]{1,0:T(8,128)(2,1)S(1)} %get-tuple-element.16.msg_ref), custom_call_target="tpu_custom_call" | custom-call | tf_op jit(solution)/shard_map/own_block/pallas_call | solution.py:114
  30.7 1.3 %collective-permute-done.4 = s32[8,128]{1,0:T(8,128)S(1)} collective-permute-done((s32[8,128]{1,0:T(8,128)S(1)}, s32[8,128]{1,0:T(8,128)S(1)}, u32[]{:S(2)}, u32[]{:S(2)}) %collective-permute-start.4) | collective-permute-done | bytes 4128 | tf_op jit(solution)/shard_map/ppermute | solution.py:193
  32.0 1.4 %step_blocks.4 = (f32[512,128]{1,0:T(8,128)S(1)}, f32[512,128]{1,0:T(8,128)S(1)}, f32[512,128]{1,0:T(8,128)S(1)}) custom-call(f32[3,512,128]{2,1,0:T(8,128)S(1)} %get-tuple-element.15.wide_ref, s32[2,128]{1,0:T(2,128)S(1)} %pad_add_fusion.2.mine_ref, f32[512,128]{1,0:T(8,128)S(1)} %own_block.1.row_in_ref, ...), custom_call_target="tpu_custom_call" | custom-call | tf_op jit(solution)/shard_map/step_blocks/pallas_call | solution.py:151
  33.3 1.4 %step_blocks.5 = (f32[512,128]{1,0:T(8,128)S(1)}, f32[512,128]{1,0:T(8,128)S(1)}, f32[512,128]{1,0:T(8,128)S(1)}) custom-call(f32[3,512,128]{2,1,0:T(8,128)S(1)} %get-tuple-element.15.wide_ref, s32[2,128]{1,0:T(2,128)S(1)} %pad_add_fusion.2.mine_ref, f32[512,128]{1,0:T(8,128)S(1)} %get-tuple-element.17.row_in_ref, ...), custom_call_target="tpu_custom_call" | custom-call | tf_op jit(solution)/shard_map/step_blocks/pallas_call | solution.py:151
  34.7 0.0 collective-permute-done.10.refs_1_
  34.7 1.4 %step_blocks.6 = (f32[512,128]{1,0:T(8,128)S(1)}, f32[512,128]{1,0:T(8,128)S(1)}, f32[512,128]{1,0:T(8,128)S(1)}) custom-call(f32[3,512,128]{2,1,0:T(8,128)S(1)} %get-tuple-element.15.wide_ref, s32[2,128]{1,0:T(2,128)S(1)} %pad_add_fusion.2.mine_ref, f32[512,128]{1,0:T(8,128)S(1)} %get-tuple-element.18.row_in_ref, ...), custom_call_target="tpu_custom_call" | custom-call | tf_op jit(solution)/shard_map/step_blocks/pallas_call | solution.py:151
  36.1 0.0 collective-permute-done.11.refs_0_
  36.1 0.8 %step_blocks.7 = (f32[512,128]{1,0:T(8,128)S(1)}, f32[512,128]{1,0:T(8,128)S(1)}) custom-call(f32[3,512,128]{2,1,0:T(8,128)S(1)} %get-tuple-element.15.wide_ref, s32[2,128]{1,0:T(2,128)S(1)} %pad_add_fusion.2.mine_ref, f32[512,128]{1,0:T(8,128)S(1)} %get-tuple-element.19.row_in_ref, bf16[560,128]{1,0:T(8,128)(2,1)S(1)} %collective-permute-done.11.refs_0_), custom_call_target="tpu_custom_call" | custom-call | tf_op jit(solution)/shard_map/step_blocks/pallas_call | solution.py:151
  36.9 1.4 %finish.1 = (bf16[512,128]{1,0:T(8,128)(2,1)}, f32[512,128]{1,0:T(8,128)}) custom-call(s32[16,128]{1,0:T(8,128)S(1)} %concatenate.22.lists_ref, f32[512,128]{1,0:T(8,128)S(1)} %get-tuple-element.20.row_in_ref, f32[512,128]{1,0:T(8,128)S(1)} %get-tuple-element.21.refs_0_, f32[512,128]{1,0:T(8,128)S(1)} %get-tuple-element.22.refs_1_, ...), custom_call_target="tpu_custom_call" | custom-call | tf_op jit(solution)/shard_map/finish/pallas_call | solution.py:179
  (1 shorter events, 0.0 us)
Async XLA Ops:
  0.6 0.9 %copy-start = (bf16[512,128]{1,0:T(8,128)(2,1)S(1)}, bf16[512,128]{1,0:T(8,128)(2,1)}, u32[]{:S(2)}) copy-start(bf16[512,128]{1,0:T(8,128)(2,1)} %omega_ref.1) | copy-start | bytes 393220
  1.5 0.7 %copy-start.1 = (f32[3,512]{1,0:T(4,128)S(1)}, f32[3,512]{1,0:T(4,128)}, u32[]{:S(2)}) copy-start(f32[3,512]{1,0:T(4,128)} %coords_ref.1) | copy-start | bytes 18436
  2.7 8.6 %copy-start.2 = (s32[1,64]{1,0:T(1,128)S(1)}, s32[1,64]{1,0:T(1,128)}, u32[]{:S(2)}) copy-start(s32[1,64]{1,0:T(1,128)} %param.5) | copy-start | bytes 772
  2.7 6.8 %collective-permute-start.5 = (bf16[560,128]{1,0:T(8,128)(2,1)S(1)}, bf16[560,128]{1,0:T(8,128)(2,1)S(1)}, u32[]{:S(2)}, u32[]{:S(2)}) collective-permute-start(bf16[560,128]{1,0:T(8,128)(2,1)S(1)} %get-tuple-element.16.msg_ref), channel_id=1, source_target_pairs={{0,8},{8,16},{16,24},{24,28},{28,20},{20,12},{12,4},{4,0},{1,9},{9... | collective-permute-start | bytes 430088 | tf_op jit(solution)/shard_map/ppermute | solution.py:206
  5.8 5.5 %collective-permute-start.6 = (bf16[560,128]{1,0:T(8,128)(2,1)S(1)}, bf16[560,128]{1,0:T(8,128)(2,1)S(1)}, u32[]{:S(2)}, u32[]{:S(2)}) collective-permute-start(bf16[560,128]{1,0:T(8,128)(2,1)S(1)} %get-tuple-element.16.msg_ref), channel_id=1, source_target_pairs={{8,0},{16,8},{24,16},{28,24},{20,28},{12,20},{4,12},{0,4},{9,1},{1... | collective-permute-start | bytes 430088 | tf_op jit(solution)/shard_map/ppermute | solution.py:208
  9.5 5.1 %collective-permute-start.7 = (bf16[560,128]{1,0:T(8,128)(2,1)S(1)}, bf16[560,128]{1,0:T(8,128)(2,1)S(1)}, u32[]{:S(2)}, u32[]{:S(2)}) collective-permute-start(bf16[560,128]{1,0:T(8,128)(2,1)S(1)} %collective-permute-done.5.refs_0_), channel_id=1, source_target_pairs={{0,8},{8,16},{16,24},{24,28},{28,20},{20,12},{12,4},{4,0},{1,9},{9... | collective-permute-start | bytes 430088 | tf_op jit(solution)/shard_map/ppermute | solution.py:206
  11.3 5.1 %collective-permute-start = (s32[1,64]{1,0:T(1,128)S(1)}, s32[1,64]{1,0:T(1,128)S(1)}, u32[]{:S(2)}, u32[]{:S(2)}) collective-permute-start(s32[1,64]{1,0:T(1,128)S(1)} %copy-done.2), channel_id=1, source_target_pairs={{0,1},{1,0},{2,3},{3,2},{4,5},{5,4},{6,7},{7,6},{8,9},{9,8},{10,11... | collective-permute-start | bytes 776 | tf_op jit(solution)/shard_map/ppermute | solution.py:193
  11.3 9.0 %collective-permute-start.8 = (bf16[560,128]{1,0:T(8,128)(2,1)S(1)}, bf16[560,128]{1,0:T(8,128)(2,1)S(1)}, u32[]{:S(2)}, u32[]{:S(2)}) collective-permute-start(bf16[560,128]{1,0:T(8,128)(2,1)S(1)} %collective-permute-done.6.refs_1_), channel_id=1, source_target_pairs={{8,0},{16,8},{24,16},{28,24},{20,28},{12,20},{4,12},{0,4},{9,1},{1... | collective-permute-start | bytes 430088 | tf_op jit(solution)/shard_map/ppermute | solution.py:208
  14.6 7.6 %collective-permute-start.9 = (bf16[560,128]{1,0:T(8,128)(2,1)S(1)}, bf16[560,128]{1,0:T(8,128)(2,1)S(1)}, u32[]{:S(2)}, u32[]{:S(2)}) collective-permute-start(bf16[560,128]{1,0:T(8,128)(2,1)S(1)} %collective-permute-done.7.refs_0_), channel_id=1, source_target_pairs={{0,8},{8,16},{16,24},{24,28},{28,20},{20,12},{12,4},{4,0},{1,9},{9... | collective-permute-start | bytes 430088 | tf_op jit(solution)/shard_map/ppermute | solution.py:206
  16.5 3.6 %collective-permute-start.1 = (s32[1,128]{1,0:T(1,128)S(1)}, s32[1,128]{1,0:T(1,128)S(1)}, u32[]{:S(2)}, u32[]{:S(2)}) collective-permute-start(s32[1,128]{1,0:T(1,128)S(1)} %pad_add_fusion.3), channel_id=1, source_target_pairs={{0,2},{1,3},{2,0},{3,1},{4,6},{5,7},{6,4},{7,5},{8,10},{9,11},{10,... | collective-permute-start | bytes 1544 | tf_op jit(solution)/shard_map/ppermute | solution.py:193
  20.1 3.6 %collective-permute-start.2 = (s32[2,128]{1,0:T(2,128)S(1)}, s32[2,128]{1,0:T(2,128)S(1)}, u32[]{:S(2)}, u32[]{:S(2)}) collective-permute-start(s32[2,128]{1,0:T(2,128)S(1)} %pad_add_fusion.2.mine_ref), channel_id=1, source_target_pairs={{0,4},{4,0},{8,12},{12,8},{16,20},{20,16},{24,28},{28,24},{1,5},{5... | collective-permute-start | bytes 3080 | tf_op jit(solution)/shard_map/ppermute | solution.py:193
  20.4 14.3 %collective-permute-start.10 = (bf16[560,128]{1,0:T(8,128)(2,1)S(1)}, bf16[560,128]{1,0:T(8,128)(2,1)S(1)}, u32[]{:S(2)}, u32[]{:S(2)}) collective-permute-start(bf16[560,128]{1,0:T(8,128)(2,1)S(1)} %collective-permute-done.8.refs_1_), channel_id=1, source_target_pairs={{8,0},{16,8},{24,16},{28,24},{20,28},{12,20},{4,12},{0,4},{9,1},{1... | collective-permute-start | bytes 430088 | tf_op jit(solution)/shard_map/ppermute | solution.py:208
  22.2 13.9 %collective-permute-start.11 = (bf16[560,128]{1,0:T(8,128)(2,1)S(1)}, bf16[560,128]{1,0:T(8,128)(2,1)S(1)}, u32[]{:S(2)}, u32[]{:S(2)}) collective-permute-start(bf16[560,128]{1,0:T(8,128)(2,1)S(1)} %collective-permute-done.9.refs_0_), channel_id=1, source_target_pairs={{0,8},{8,16},{16,24},{24,28},{28,20},{20,12},{12,4},{4,0},{1,9},{9... | collective-permute-start | bytes 430088 | tf_op jit(solution)/shard_map/ppermute | solution.py:206
  23.8 3.6 %collective-permute-start.3 = (s32[4,128]{1,0:T(4,128)S(1)}, s32[4,128]{1,0:T(4,128)S(1)}, u32[]{:S(2)}, u32[]{:S(2)}) collective-permute-start(s32[4,128]{1,0:T(4,128)S(1)} %pad_add_fusion.1), channel_id=1, source_target_pairs={{0,8},{4,12},{8,0},{12,4},{16,24},{20,28},{24,16},{28,20},{1,9},{5... | collective-permute-start | bytes 6152 | tf_op jit(solution)/shard_map/ppermute | solution.py:193
  27.4 4.5 %collective-permute-start.4 = (s32[8,128]{1,0:T(8,128)S(1)}, s32[8,128]{1,0:T(8,128)S(1)}, u32[]{:S(2)}, u32[]{:S(2)}) collective-permute-start(s32[8,128]{1,0:T(8,128)S(1)} %pad_add_fusion), channel_id=1, source_target_pairs={{0,16},{4,20},{8,24},{12,28},{16,0},{20,4},{24,8},{28,12},{1,17},{... | collective-permute-start | bytes 12296 | tf_op jit(solution)/shard_map/ppermute | solution.py:193

commit v2 on v0

v2 whole, which is shorter than its diff:
```python
import functools

import jax
import jax.numpy as jnp
from jax import lax
from jax.experimental import pallas as pl
from jax.experimental.pallas import tpu as pltpu
from jax.sharding import PartitionSpec as P


kernel_scale = 0.0078125
softening = 0.02
stretch = 1.0 / kernel_scale
soft_term = softening * softening * stretch * stretch
TERMS = 3
LANES = 128
BASE = 256
QUAD = (1, 2, 3)

VMEM = pl.BlockSpec(memory_space=pltpu.VMEM)
ROOM = pltpu.CompilerParams(vmem_limit_bytes=16 * 1024 * 1024)


def tail_rows(leaf, list_rows):
    rows = 3 * TERMS * (leaf // LANES)
    return -(-rows // 16) * 16 + -(-2 * list_rows // 16) * 16


def list_start(size, list_rows):
    return size - -(-2 * list_rows // 16) * 16


def prep_kernel(coords_ref, omega_ref, piece_ref, msg_ref, wide_ref, own_ref, points, sems):
    leaf = points.shape[1]
    chunks = leaf // LANES
    fetch = pltpu.make_async_copy(coords_ref, points, sems.at[0])
    block = pltpu.make_async_copy(omega_ref, msg_ref.at[pl.ds(0, leaf)], sems.at[1])
    piece = pltpu.make_async_copy(piece_ref, own_ref, sems.at[2])
    fetch.start()
    block.start()
    piece.start()
    fetch.wait()
    scaled = points[...] * stretch
    rows = []
    for c in range(3):
        rest = scaled[c : c + 1, :]
        for _ in range(TERMS):
            term = rest.astype(jnp.bfloat16).astype(jnp.float32)
            rest = rest - term
            rows += [term[:, k * LANES : (k + 1) * LANES] for k in range(chunks)]
    spare = msg_ref.shape[0] - leaf - len(rows)
    rows.append(jnp.zeros((spare, LANES), jnp.float32))
    msg_ref[leaf:, :] = jnp.concatenate(rows, axis=0).astype(jnp.bfloat16)
    columns = jnp.concatenate([scaled, jnp.zeros((5, leaf), jnp.float32)], axis=0).T
    for c in range(3):
        wide_ref[c] = jnp.broadcast_to(columns[:, c : c + 1], (leaf, LANES))
    block.wait()
    piece.wait()


def prep(list_rows, coords, omega, piece):
    leaf = coords.shape[1]
    return pl.pallas_call(
        prep_kernel,
        out_shape=(
            jax.ShapeDtypeStruct((leaf + tail_rows(leaf, list_rows), LANES), jnp.bfloat16),
            jax.ShapeDtypeStruct((3, leaf, LANES), jnp.float32),
            jax.ShapeDtypeStruct(piece.shape, piece.dtype),
        ),
        in_specs=[pl.BlockSpec(memory_space=pltpu.HBM)] * 3,
        out_specs=(VMEM,) * 3,
        scratch_shapes=[pltpu.VMEM(coords.shape, jnp.float32), pltpu.SemaphoreType.DMA((3,))],
        cost_estimate=pl.CostEstimate(flops=1000000, bytes_accessed=0, transcendentals=0),
        compiler_params=ROOM,
        name="prep",
    )(coords, omega, piece)


def attach_kernel(list_rows, msg_in_ref, *refs):
    pieces, msg_ref, tail_ref = refs[:-2], refs[-2], refs[-1]
    size, rows_all = tail_ref.shape[0], msg_ref.shape[0]
    first = list_start(rows_all, list_rows)
    listed = jnp.concatenate([piece[...] for piece in pieces], axis=1)
    rows = []
    for digit in (listed // BASE, listed % BASE):
        digit = digit.astype(jnp.float32)
        rows += [digit[:, r * LANES : (r + 1) * LANES] for r in range(list_rows)]
    rows.append(jnp.zeros((rows_all - first - len(rows), LANES), jnp.float32))
    rows = jnp.concatenate(rows, axis=0).astype(jnp.bfloat16)
    msg_ref[first:, :] = rows
    held = size - (rows_all - first)
    tail_ref[0:held, :] = msg_in_ref[rows_all - size : first, :]
    tail_ref[held:, :] = rows


def attach(list_rows, size, msg, pieces):
    return pl.pallas_call(
        functools.partial(attach_kernel, list_rows),
        out_shape=(
            jax.ShapeDtypeStruct(msg.shape, msg.dtype),
            jax.ShapeDtypeStruct((size, LANES), msg.dtype),
        ),
        in_specs=[VMEM] * (1 + len(pieces)),
        out_specs=(VMEM, VMEM),
        input_output_aliases={0: 0},
        compiler_params=ROOM,
        name="attach",
    )(msg, *pieces)


def pack_kernel(block_ref, tail_ref, msg_ref):
    leaf = block_ref.shape[0]
    msg_ref[0:leaf, :] = block_ref[...]
    msg_ref[leaf:, :] = tail_ref[...]


def pack(block, tail):
    return pl.pallas_call(
        pack_kernel,
        out_shape=jax.ShapeDtypeStruct((block.shape[0] + tail.shape[0], LANES), block.dtype),
        in_specs=[VMEM, VMEM],
        out_specs=VMEM,
        compiler_params=ROOM,
        name="pack",
    )(block, tail)


def block_entries(wide_ref, tail, tile_ref):
    leaf = wide_ref.shape[1]
    chunks = leaf // LANES
    step = 64
    for k in range(chunks):
        target = []
        for c in range(3):
            row = [(c * TERMS + t) * chunks + k for t in range(TERMS)]
            row = [tail[r : r + 1, :] for r in row]
            target.append((row[0] + row[1]) + row[2])
        for p in range(0, leaf, step):
            squared = (wide_ref[0, p : p + step, :] - target[0]) ** 2
            squared = squared + (wide_ref[1, p : p + step, :] - target[1]) ** 2
            squared = squared + (wide_ref[2, p : p + step, :] - target[2]) ** 2
            entry = lax.rsqrt(squared + soft_term)
            tile_ref[p : p + step, k * LANES : (k + 1) * LANES] = entry.astype(jnp.bfloat16)


def listed_in(tail, list_rows):
    first = list_start(tail.shape[0], list_rows)
    high = tail[first : first + list_rows, :]
    low = tail[first + list_rows : first + 2 * list_rows, :]
    return high * BASE + low


def count_wide(listed, node, leaf):
    points = lax.broadcasted_iota(jnp.int32, (leaf, LANES), 0) + node * leaf
    points = points.astype(jnp.float32)
    hits = jnp.zeros((leaf, LANES), jnp.float32)
    for r in range(listed.shape[0]):
        hits = hits + jnp.where(points == listed[r : r + 1, :], 1.0, 0.0)
    ones = jnp.ones((LANES, LANES), jnp.bfloat16)
    return jnp.dot(hits.astype(jnp.bfloat16), ones, preferred_element_type=jnp.float32)


def weight_wide(mine, node, me, leaf):
    near = jnp.where(jnp.abs(node - me) <= 1, 1.0, 0.0)
    return (count_wide(mine, node, leaf) + near).astype(jnp.bfloat16)


def both_products(tile, samples, weight):
    weighted = (weight.astype(jnp.float32) * samples.astype(jnp.float32)).astype(jnp.bfloat16)
    both = jnp.dot(tile, jnp.concatenate([samples, weighted], axis=1), preferred_element_type=jnp.float32)
    return both[:, :LANES], both[:, LANES:]


def blocks_kernel(list_rows, bits, started, wide_ref, tail_ref, *refs):
    msgs = refs[: len(bits)]
    row_ref, col_ref, tile_ref = refs[-3], refs[-2], refs[-1]
    leaf = wide_ref.shape[1]
    me = lax.axis_index("node")
    mine = listed_in(tail_ref[...].astype(jnp.float32), list_rows)
    if started:
        row_total, col_total = refs[len(bits)][...], refs[len(bits) + 1][...]
    else:
        row_total = jnp.zeros((leaf, LANES), jnp.float32)
        col_total = jnp.zeros((leaf, LANES), jnp.float32)
    for bit, msg in zip(bits, msgs):
        tail = msg[leaf:, :].astype(jnp.float32)
        block_entries(wide_ref, tail, tile_ref)
        weight = weight_wide(mine, me ^ bit, me, leaf)
        plain, taken = both_products(tile_ref[...], msg[0:leaf, :], weight)
        row_total = row_total + taken
        col_total = col_total + count_wide(listed_in(tail, list_rows), me, leaf) * plain
    row_ref[...] = row_total.astype(row_ref.dtype)
    col_ref[...] = col_total


def add_blocks(list_rows, bits, wide, tail, msgs, totals, row_type=jnp.float32):
    leaf = wide.shape[1]
    part = (leaf, LANES)
    return pl.pallas_call(
        functools.partial(blocks_kernel, list_rows, bits, bool(totals)),
        out_shape=(jax.ShapeDtypeStruct(part, row_type), jax.ShapeDtypeStruct(part, jnp.float32)),
        in_specs=[VMEM] * (2 + len(msgs) + len(totals)),
        out_specs=(VMEM, VMEM),
        scratch_shapes=[pltpu.VMEM((leaf, leaf), jnp.bfloat16)],
        compiler_params=ROOM,
        name="add_blocks",
    )(wide, tail, *msgs, *totals)


def swap(block, axis, bits):
    return lax.ppermute(block, axis, [(i, i ^ bits) for i in range(lax.axis_size(axis))])


def on_device(coords, omega, skeleton):
    nodes = lax.axis_size("node")
    reps = lax.axis_size("rep")
    leaf = coords.shape[1]
    list_rows = reps * skeleton.shape[1] // LANES
    size = tail_rows(leaf, list_rows)
    far_bits = [1 << k for k in range(2, nodes.bit_length() - 1)]

    across = [(0, omega)]
    for bit in reversed(far_bits):
        across += [(bits | bit, swap(block, "node", bit)) for bits, block in across]
    pieces = [swap(skeleton, "rep", bits) for bits in range(1, reps)]
    msg, wide, own_piece = prep(list_rows, coords, omega, skeleton)
    msg, tail = attach(list_rows, size, msg, [own_piece] + pieces)
    tails = [(0, tail)]
    for bit in reversed(far_bits):
        tails += [(bits | bit, swap(part, "node", bit)) for bits, part in tails]
    msgs = [swap(msg, "node", step) for step in QUAD]
    totals = add_blocks(list_rows, [0], wide, tail, [msg], ())
    totals = add_blocks(list_rows, QUAD, wide, tail, msgs, totals)
    for (bits, block), (_, part) in zip(across[1:], tails[1:]):
        msg = pack(block, part)
        msgs = [swap(msg, "node", step) for step in QUAD]
        totals = add_blocks(list_rows, [bits], wide, tail, [msg], totals)
        for step, msg in zip(QUAD, msgs):
            final = bits == across[-1][0] and step == QUAD[-1]
            totals = add_blocks(
                list_rows, [bits | step], wide, tail, [msg], totals, jnp.bfloat16 if final else jnp.float32
            )
    return totals


def solution(mesh):
    in_specs = (P(None, "node"), P("node", "rep"), P("node", "rep"))
    out_specs = (P("node", "rep"), P("node", "rep"))
    return jax.shard_map(on_device, mesh=mesh, in_specs=in_specs, out_specs=out_specs, check_vma=False)
```

time: 84.5 us -> 29.8 us (0.35)
  starting transfers between devices: 29.8 us -> 13.2 us
  local copies, waits for them, and re-layouts: 17.9 us -> 2.25 us
  waiting for transfers between devices: 17.6 us -> 5.9 us
  other arithmetic: 9.02 us -> 0 us
  Pallas kernels: 0 us -> 7.55 us
  blocking collectives: 4.9 us -> 0 us
  matrix products: 2.95 us -> 0 us
    all_to_all x4 -> x0, waiting for transfers between devices: 17.6 us -> none  [the longest x1 6.33 us: on_device(): lax.all_to_all(asked_points, 'node', split_axis=0, concat_axis=0, tiled=T...]
    all_to_all x4 -> x0, starting transfers between devices: 17 us -> none  [the longest x1 6.28 us: on_device(): lax.all_to_all(request, 'node', split_axis=0, concat_axis=0, tiled=True)]
    pallas_call x0 -> x9, Pallas kernels: none -> 7.55 us  [the longest x6 6.88 us: add_blocks(): pl.pallas_call(functools.partial(blocks_kernel, list_rows, bits, bool(tot...]
    scatter-add x1 -> x0, other arithmetic: 6.9 us -> none  [on_device(): col_total = jnp.zeros((leaf_size, samp_dev), jnp.float32).at[asked_rows.r...]
    gather x6 -> x0, local copies, waits for them, and re-layouts: 6.69 us -> none  [the longest x1 1.95 us: on_device(): asked_samples = omega[asked_rows]]
    ppermute x4 -> x11, waiting for transfers between devices: 0.01 us -> 5.9 us  [swap(): lax.ppermute(block, axis, [(i, i ^ bits) for i in range(lax.axis_size(axi...]
    squeeze x1 -> x0, blocking collectives: 4.9 us -> none  [on_device(): listed = lax.all_gather(skeleton, 'rep', axis=1, tiled=True)[0]]
    dot_general x3 -> x0, matrix products: 2.95 us -> none  [the longest x1 2.06 us: on_device(): jnp.dot(kernel_tile(coords, wide_points), wide_rows, preferred_element_ty...]
  transfers between devices with their start and end apart: 8 -> 11, of which waited for: 4 -> 2; matrix products, arithmetic and copies ran while one was open for 27% -> 0% of each run, Pallas kernels for 0% -> 20%
where the time goes in v2:
time: 29.8 us; the launch traced here: 29.6 us
  starting transfers between devices  13.2 us (44%)
  Pallas kernels  7.55 us (25%)
  waiting for transfers between devices  5.9 us (20%)
  local copies, waits for them, and re-layouts  2.25 us (8%)
  between operations  0.72 us (2%)
    ppermute x11, starting transfers between devices, swap(): lax.ppermute(block, axis, [(i, i ^ bits) for i in range(lax.axis_size(axi...  13.2 us
    pallas_call x6, Pallas kernels, add_blocks(): pl.pallas_call(functools.partial(blocks_kernel, list_rows, bits, bool(tot...  6.88 us
    ppermute x11, waiting for transfers between devices, swap(): lax.ppermute(block, axis, [(i, i ^ bits) for i in range(lax.axis_size(axi...  5.9 us
    unnamed x6, local copies, waits for them, and re-layouts  2.25 us
  transfers between devices with their start and end apart: 11, of which 2 were waited for; matrix products, arithmetic and copies ran while one was open for 0% of the time, Pallas kernels for 20%

profile of v2, /device:TPU:0, one launch (start us, length us, event | category | flops | bytes accessed | tf_op | source)
XLA Modules:
  0.0 29.6 jit_solution(15833826112213602455)
XLA Ops:
  0.6 0.6 %collective-permute-start = (s32[1,64]{1,0:T(1,128)}, s32[1,64]{1,0:T(1,128)S(1)}, u32[]{:S(2)}, u32[]{:S(2)}) collective-permute-start(s32[1,64]{1,0:T(1,128)} %piece_ref.1), channel_id=1, source_target_pairs={{0,1},{1,0},{2,3},{3,2},{4,5},{5,4},{6,7},{7,6},{8,9},{9,8},{10,11... | collective-permute-start | bytes 776 | tf_op jit(solution)/shard_map/ppermute | solution.py:211
  1.2 2.6 %collective-permute-start.1 = (s32[1,64]{1,0:T(1,128)}, s32[1,64]{1,0:T(1,128)S(1)}, u32[]{:S(2)}, u32[]{:S(2)}) collective-permute-start(s32[1,64]{1,0:T(1,128)} %piece_ref.1), channel_id=1, source_target_pairs={{0,2},{1,3},{2,0},{3,1},{4,6},{5,7},{6,4},{7,5},{8,10},{9,11},{10,... | collective-permute-start | bytes 776 | tf_op jit(solution)/shard_map/ppermute | solution.py:211
  3.7 0.0 collective-permute-start.2
  3.8 0.0 copy-start
  3.8 0.9 %copy-done = bf16[512,128]{1,0:T(8,128)(2,1)S(1)} copy-done((bf16[512,128]{1,0:T(8,128)(2,1)S(1)}, bf16[512,128]{1,0:T(8,128)(2,1)}, u32[]{:S(2)}) %copy-start) | copy-done | bytes 131096
  4.7 0.0 copy-start.1
  4.7 0.7 %copy-done.1 = f32[3,512]{1,0:T(4,128)S(1)} copy-done((f32[3,512]{1,0:T(4,128)S(1)}, f32[3,512]{1,0:T(4,128)}, u32[]{:S(2)}) %copy-start.1) | copy-done | bytes 6168
  5.4 0.0 copy-start.2
  5.4 0.7 %copy-done.2 = s32[1,64]{1,0:T(1,128)S(1)} copy-done((s32[1,64]{1,0:T(1,128)S(1)}, s32[1,64]{1,0:T(1,128)}, u32[]{:S(2)}) %copy-start.2) | copy-done | bytes 280
  6.0 0.6 %prep.1 = (bf16[576,128]{1,0:T(8,128)(2,1)S(1)}, f32[3,512,128]{2,1,0:T(8,128)S(1)}, s32[1,64]{1,0:T(1,128)S(1)}) custom-call(f32[3,512]{1,0:T(4,128)S(1)} %copy-done.1, bf16[512,128]{1,0:T(8,128)(2,1)S(1)} %copy-done, s32[1,64]{1,0:T(1,128)S(1)} %copy-done.2), custom_call_target="tpu_custom_call" | custom-call | flops 1000000 | tf_op jit(solution)/shard_map/prep/pallas_call | solution.py:63
  6.6 0.0 collective-permute-done.refs_1_
  6.6 0.0 collective-permute-done.1.refs_2_
  6.6 0.2 collective-permute-done.2.refs_3_
  6.9 0.1 attach.1
  7.0 2.6 %collective-permute-start.10 = (bf16[576,128]{1,0:T(8,128)(2,1)S(1)}, bf16[576,128]{1,0:T(8,128)(2,1)S(1)}, u32[]{:S(2)}, u32[]{:S(2)}) collective-permute-start(bf16[576,128]{1,0:T(8,128)(2,1)S(1)} %get-tuple-element.21.refs_0_), channel_id=1, source_target_pairs={{0,12},{4,8},{8,4},{12,0},{16,28},{20,24},{24,20},{28,16},{1,13},{... | collective-permute-start | bytes 442376 | tf_op jit(solution)/shard_map/ppermute | solution.py:211
  9.6 2.6 %collective-permute-start.3 = (bf16[512,128]{1,0:T(8,128)(2,1)S(1)}, bf16[512,128]{1,0:T(8,128)(2,1)S(1)}, u32[]{:S(2)}, u32[]{:S(2)}) collective-permute-start(bf16[512,128]{1,0:T(8,128)(2,1)S(1)} %copy-done), channel_id=1, source_target_pairs={{0,16},{4,20},{8,24},{12,28},{16,0},{20,4},{24,8},{28,12},{1,17},{... | collective-permute-start | bytes 393224 | tf_op jit(solution)/shard_map/ppermute | solution.py:211
  12.2 0.3 %collective-permute-start.4 = (bf16[64,128]{1,0:T(8,128)(2,1)S(1)}, bf16[64,128]{1,0:T(8,128)(2,1)S(1)}, u32[]{:S(2)}, u32[]{:S(2)}) collective-permute-start(bf16[64,128]{1,0:T(8,128)(2,1)S(1)} %get-tuple-element.20.tail_ref), channel_id=1, source_target_pairs={{0,16},{4,20},{8,24},{12,28},{16,0},{20,4},{24,8},{28,12},{1,17},{... | collective-permute-start | bytes 49160 | tf_op jit(solution)/shard_map/ppermute | solution.py:211
  12.5 0.5 %collective-permute-start.8 = (bf16[576,128]{1,0:T(8,128)(2,1)S(1)}, bf16[576,128]{1,0:T(8,128)(2,1)S(1)}, u32[]{:S(2)}, u32[]{:S(2)}) collective-permute-start(bf16[576,128]{1,0:T(8,128)(2,1)S(1)} %get-tuple-element.21.refs_0_), channel_id=1, source_target_pairs={{0,4},{4,0},{8,12},{12,8},{16,20},{20,16},{24,28},{28,24},{1,5},{5... | collective-permute-start | bytes 442376 | tf_op jit(solution)/shard_map/ppermute | solution.py:211
  13.0 0.4 %collective-permute-start.9 = (bf16[576,128]{1,0:T(8,128)(2,1)S(1)}, bf16[576,128]{1,0:T(8,128)(2,1)S(1)}, u32[]{:S(2)}, u32[]{:S(2)}) collective-permute-start(bf16[576,128]{1,0:T(8,128)(2,1)S(1)} %get-tuple-element.21.refs_0_), channel_id=1, source_target_pairs={{0,8},{4,12},{8,0},{12,4},{16,24},{20,28},{24,16},{28,20},{1,9},{5... | collective-permute-start | bytes 442376 | tf_op jit(solution)/shard_map/ppermute | solution.py:211
  13.4 5.6 %collective-permute-done.4.tail_ref = bf16[64,128]{1,0:T(8,128)(2,1)S(1)} collective-permute-done((bf16[64,128]{1,0:T(8,128)(2,1)S(1)}, bf16[64,128]{1,0:T(8,128)(2,1)S(1)}, u32[]{:S(2)}, u32[]{:S(2)}) %collective-permute-start.4) | collective-permute-done | bytes 16416 | tf_op jit(solution)/shard_map/ppermute | solution.py:211
  19.1 0.0 collective-permute-done.3.block_ref
  19.1 0.6 %collective-permute-start.7 = (bf16[576,128]{1,0:T(8,128)(2,1)S(1)}, bf16[576,128]{1,0:T(8,128)(2,1)S(1)}, u32[]{:S(2)}, u32[]{:S(2)}) collective-permute-start(bf16[576,128]{1,0:T(8,128)(2,1)S(1)} %pack.1.refs_0_), channel_id=1, source_target_pairs={{0,4},{4,0},{8,12},{12,8},{16,20},{20,16},{24,28},{28,24},{1,5},{5... | collective-permute-start | bytes 442376 | tf_op jit(solution)/shard_map/ppermute | solution.py:211
  19.7 1.4 %collective-permute-start.6 = (bf16[576,128]{1,0:T(8,128)(2,1)S(1)}, bf16[576,128]{1,0:T(8,128)(2,1)S(1)}, u32[]{:S(2)}, u32[]{:S(2)}) collective-permute-start(bf16[576,128]{1,0:T(8,128)(2,1)S(1)} %pack.1.refs_0_), channel_id=1, source_target_pairs={{0,8},{4,12},{8,0},{12,4},{16,24},{20,28},{24,16},{28,20},{1,9},{5... | collective-permute-start | bytes 442376 | tf_op jit(solution)/shard_map/ppermute | solution.py:211
  21.1 0.0 collective-permute-done.10.refs_2_
  21.1 1.5 %collective-permute-start.5 = (bf16[576,128]{1,0:T(8,128)(2,1)S(1)}, bf16[576,128]{1,0:T(8,128)(2,1)S(1)}, u32[]{:S(2)}, u32[]{:S(2)}) collective-permute-start(bf16[576,128]{1,0:T(8,128)(2,1)S(1)} %pack.1.refs_0_), channel_id=1, source_target_pairs={{0,12},{4,8},{8,4},{12,0},{16,28},{20,24},{24,20},{28,16},{1,13},{... | collective-permute-start | bytes 442376 | tf_op jit(solution)/shard_map/ppermute | solution.py:211
  22.7 0.8 %add_blocks.6 = (f32[512,128]{1,0:T(8,128)S(1)}, f32[512,128]{1,0:T(8,128)S(1)}) custom-call(f32[3,512,128]{2,1,0:T(8,128)S(1)} %get-tuple-element.17.wide_ref, bf16[64,128]{1,0:T(8,128)(2,1)S(1)} %get-tuple-element.20.tail_ref, bf16[576,128]{1,0:T(8,128)(2,1)S(1)} %get-tuple-element.21.refs_0_), custom_call_target="tpu_custom_call" | custom-call | tf_op jit(solution)/shard_map/add_blocks/pallas_call | solution.py:199
  23.4 0.0 collective-permute-done.8.refs_0_
  23.5 0.0 collective-permute-done.9.refs_1_
  23.5 2.1 %add_blocks.7 = (f32[512,128]{1,0:T(8,128)S(1)}, f32[512,128]{1,0:T(8,128)S(1)}) custom-call(f32[3,512,128]{2,1,0:T(8,128)S(1)} %get-tuple-element.17.wide_ref, bf16[64,128]{1,0:T(8,128)(2,1)S(1)} %get-tuple-element.20.tail_ref, bf16[576,128]{1,0:T(8,128)(2,1)S(1)} %collective-permute-done.8.refs_0_, bf16[576,128]{1,0:T(8,128)(2,1)S(1)} %collective-permute-done.9.refs_1_, ...), custom_call_target="tpu_custom_call" | custom-call | tf_op jit(solution)/shard_map/add_blocks/pallas_call | solution.py:199
  25.5 0.8 %add_blocks.8 = (f32[512,128]{1,0:T(8,128)S(1)}, f32[512,128]{1,0:T(8,128)S(1)}) custom-call(f32[3,512,128]{2,1,0:T(8,128)S(1)} %get-tuple-element.17.wide_ref, bf16[64,128]{1,0:T(8,128)(2,1)S(1)} %get-tuple-element.20.tail_ref, bf16[576,128]{1,0:T(8,128)(2,1)S(1)} %pack.1.refs_0_, f32[512,128]{1,0:T(8,128)S(1)} %get-tuple-element.24.refs_1_, ...), custom_call_target="tpu_custom_call" | custom-call | tf_op jit(solution)/shard_map/add_blocks/pallas_call | solution.py:199
  26.4 0.0 collective-permute-done.7.refs_0_
  26.4 0.8 %add_blocks.9 = (f32[512,128]{1,0:T(8,128)S(1)}, f32[512,128]{1,0:T(8,128)S(1)}) custom-call(f32[3,512,128]{2,1,0:T(8,128)S(1)} %get-tuple-element.17.wide_ref, bf16[64,128]{1,0:T(8,128)(2,1)S(1)} %get-tuple-element.20.tail_ref, bf16[576,128]{1,0:T(8,128)(2,1)S(1)} %collective-permute-done.7.refs_0_, f32[512,128]{1,0:T(8,128)S(1)} %get-tuple-element.26.refs_1_, ...), custom_call_target="tpu_custom_call" | custom-call | tf_op jit(solution)/shard_map/add_blocks/pallas_call | solution.py:199
  27.2 0.0 collective-permute-done.6.refs_0_
  27.2 0.8 %add_blocks.10 = (f32[512,128]{1,0:T(8,128)S(1)}, f32[512,128]{1,0:T(8,128)S(1)}) custom-call(f32[3,512,128]{2,1,0:T(8,128)S(1)} %get-tuple-element.17.wide_ref, bf16[64,128]{1,0:T(8,128)(2,1)S(1)} %get-tuple-element.20.tail_ref, bf16[576,128]{1,0:T(8,128)(2,1)S(1)} %collective-permute-done.6.refs_0_, f32[512,128]{1,0:T(8,128)S(1)} %get-tuple-element.28.refs_1_, ...), custom_call_target="tpu_custom_call" | custom-call | tf_op jit(solution)/shard_map/add_blocks/pallas_call | solution.py:199
  28.0 0.0 collective-permute-done.5.refs_0_
  28.0 1.6 %add_blocks.11 = (bf16[512,128]{1,0:T(8,128)(2,1)}, f32[512,128]{1,0:T(8,128)}) custom-call(f32[3,512,128]{2,1,0:T(8,128)S(1)} %get-tuple-element.17.wide_ref, bf16[64,128]{1,0:T(8,128)(2,1)S(1)} %get-tuple-element.20.tail_ref, bf16[576,128]{1,0:T(8,128)(2,1)S(1)} %collective-permute-done.5.refs_0_, f32[512,128]{1,0:T(8,128)S(1)} %get-tuple-element.30.refs_1_, ...), custom_call_target="tpu_custom_call" | custom-call | tf_op jit(solution)/shard_map/add_blocks/pallas_call | solution.py:199
  (1 shorter events, 0.0 us)
Async XLA Ops:
  0.6 6.0 %collective-permute-start = (s32[1,64]{1,0:T(1,128)}, s32[1,64]{1,0:T(1,128)S(1)}, u32[]{:S(2)}, u32[]{:S(2)}) collective-permute-start(s32[1,64]{1,0:T(1,128)} %piece_ref.1), channel_id=1, source_target_pairs={{0,1},{1,0},{2,3},{3,2},{4,5},{5,4},{6,7},{7,6},{8,9},{9,8},{10,11... | collective-permute-start | bytes 776 | tf_op jit(solution)/shard_map/ppermute | solution.py:211
  1.2 5.4 %collective-permute-start.1 = (s32[1,64]{1,0:T(1,128)}, s32[1,64]{1,0:T(1,128)S(1)}, u32[]{:S(2)}, u32[]{:S(2)}) collective-permute-start(s32[1,64]{1,0:T(1,128)} %piece_ref.1), channel_id=1, source_target_pairs={{0,2},{1,3},{2,0},{3,1},{4,6},{5,7},{6,4},{7,5},{8,10},{9,11},{10,... | collective-permute-start | bytes 776 | tf_op jit(solution)/shard_map/ppermute | solution.py:211
  3.7 3.1 %collective-permute-start.2 = (s32[1,64]{1,0:T(1,128)}, s32[1,64]{1,0:T(1,128)S(1)}, u32[]{:S(2)}, u32[]{:S(2)}) collective-permute-start(s32[1,64]{1,0:T(1,128)} %piece_ref.1), channel_id=1, source_target_pairs={{0,3},{1,2},{2,1},{3,0},{4,7},{5,6},{6,5},{7,4},{8,11},{9,10},{10,... | collective-permute-start | bytes 776 | tf_op jit(solution)/shard_map/ppermute | solution.py:211
  3.8 0.9 %copy-start = (bf16[512,128]{1,0:T(8,128)(2,1)S(1)}, bf16[512,128]{1,0:T(8,128)(2,1)}, u32[]{:S(2)}) copy-start(bf16[512,128]{1,0:T(8,128)(2,1)} %omega_ref.1) | copy-start | bytes 393220
  4.7 0.7 %copy-start.1 = (f32[3,512]{1,0:T(4,128)S(1)}, f32[3,512]{1,0:T(4,128)}, u32[]{:S(2)}) copy-start(f32[3,512]{1,0:T(4,128)} %coords_ref.1) | copy-start | bytes 18436
  5.4 0.7 %copy-start.2 = (s32[1,64]{1,0:T(1,128)S(1)}, s32[1,64]{1,0:T(1,128)}, u32[]{:S(2)}) copy-start(s32[1,64]{1,0:T(1,128)} %piece_ref.1) | copy-start | bytes 772
  7.0 14.2 %collective-permute-start.10 = (bf16[576,128]{1,0:T(8,128)(2,1)S(1)}, bf16[576,128]{1,0:T(8,128)(2,1)S(1)}, u32[]{:S(2)}, u32[]{:S(2)}) collective-permute-start(bf16[576,128]{1,0:T(8,128)(2,1)S(1)} %get-tuple-element.21.refs_0_), channel_id=1, source_target_pairs={{0,12},{4,8},{8,4},{12,0},{16,28},{20,24},{24,20},{28,16},{1,13},{... | collective-permute-start | bytes 442376 | tf_op jit(solution)/shard_map/ppermute | solution.py:211
  9.6 9.5 %collective-permute-start.3 = (bf16[512,128]{1,0:T(8,128)(2,1)S(1)}, bf16[512,128]{1,0:T(8,128)(2,1)S(1)}, u32[]{:S(2)}, u32[]{:S(2)}) collective-permute-start(bf16[512,128]{1,0:T(8,128)(2,1)S(1)} %copy-done), channel_id=1, source_target_pairs={{0,16},{4,20},{8,24},{12,28},{16,0},{20,4},{24,8},{28,12},{1,17},{... | collective-permute-start | bytes 393224 | tf_op jit(solution)/shard_map/ppermute | solution.py:211
  12.2 6.9 %collective-permute-start.4 = (bf16[64,128]{1,0:T(8,128)(2,1)S(1)}, bf16[64,128]{1,0:T(8,128)(2,1)S(1)}, u32[]{:S(2)}, u32[]{:S(2)}) collective-permute-start(bf16[64,128]{1,0:T(8,128)(2,1)S(1)} %get-tuple-element.20.tail_ref), channel_id=1, source_target_pairs={{0,16},{4,20},{8,24},{12,28},{16,0},{20,4},{24,8},{28,12},{1,17},{... | collective-permute-start | bytes 49160 | tf_op jit(solution)/shard_map/ppermute | solution.py:211
  12.5 10.9 %collective-permute-start.8 = (bf16[576,128]{1,0:T(8,128)(2,1)S(1)}, bf16[576,128]{1,0:T(8,128)(2,1)S(1)}, u32[]{:S(2)}, u32[]{:S(2)}) collective-permute-start(bf16[576,128]{1,0:T(8,128)(2,1)S(1)} %get-tuple-element.21.refs_0_), channel_id=1, source_target_pairs={{0,4},{4,0},{8,12},{12,8},{16,20},{20,16},{24,28},{28,24},{1,5},{5... | collective-permute-start | bytes 442376 | tf_op jit(solution)/shard_map/ppermute | solution.py:211
  13.0 10.4 %collective-permute-start.9 = (bf16[576,128]{1,0:T(8,128)(2,1)S(1)}, bf16[576,128]{1,0:T(8,128)(2,1)S(1)}, u32[]{:S(2)}, u32[]{:S(2)}) collective-permute-start(bf16[576,128]{1,0:T(8,128)(2,1)S(1)} %get-tuple-element.21.refs_0_), channel_id=1, source_target_pairs={{0,8},{4,12},{8,0},{12,4},{16,24},{20,28},{24,16},{28,20},{1,9},{5... | collective-permute-start | bytes 442376 | tf_op jit(solution)/shard_map/ppermute | solution.py:211
  19.1 7.2 %collective-permute-start.7 = (bf16[576,128]{1,0:T(8,128)(2,1)S(1)}, bf16[576,128]{1,0:T(8,128)(2,1)S(1)}, u32[]{:S(2)}, u32[]{:S(2)}) collective-permute-start(bf16[576,128]{1,0:T(8,128)(2,1)S(1)} %pack.1.refs_0_), channel_id=1, source_target_pairs={{0,4},{4,0},{8,12},{12,8},{16,20},{20,16},{24,28},{28,24},{1,5},{5... | collective-permute-start | bytes 442376 | tf_op jit(solution)/shard_map/ppermute | solution.py:211
  19.7 7.5 %collective-permute-start.6 = (bf16[576,128]{1,0:T(8,128)(2,1)S(1)}, bf16[576,128]{1,0:T(8,128)(2,1)S(1)}, u32[]{:S(2)}, u32[]{:S(2)}) collective-permute-start(bf16[576,128]{1,0:T(8,128)(2,1)S(1)} %pack.1.refs_0_), channel_id=1, source_target_pairs={{0,8},{4,12},{8,0},{12,4},{16,24},{20,28},{24,16},{28,20},{1,9},{5... | collective-permute-start | bytes 442376 | tf_op jit(solution)/shard_map/ppermute | solution.py:211
  21.1 6.9 %collective-permute-start.5 = (bf16[576,128]{1,0:T(8,128)(2,1)S(1)}, bf16[576,128]{1,0:T(8,128)(2,1)S(1)}, u32[]{:S(2)}, u32[]{:S(2)}) collective-permute-start(bf16[576,128]{1,0:T(8,128)(2,1)S(1)} %pack.1.refs_0_), channel_id=1, source_target_pairs={{0,12},{4,8},{8,4},{12,0},{16,28},{20,24},{24,20},{28,16},{1,13},{... | collective-permute-start | bytes 442376 | tf_op jit(solution)/shard_map/ppermute | solution.py:211

commit v3 on v2

--- a/solution.py
+++ b/solution.py
@@ -21,13 +21,12 @@
 ROOM = pltpu.CompilerParams(vmem_limit_bytes=16 * 1024 * 1024)
 
 
+def coord_rows(leaf):
+    return 3 * TERMS * (leaf // LANES)
+
+
 def tail_rows(leaf, list_rows):
-    rows = 3 * TERMS * (leaf // LANES)
-    return -(-rows // 16) * 16 + -(-2 * list_rows // 16) * 16
-
-
-def list_start(size, list_rows):
-    return size - -(-2 * list_rows // 16) * 16
+    return -(-(coord_rows(leaf) + 2 * list_rows) // 16) * 16
 
 
 def prep_kernel(coords_ref, omega_ref, piece_ref, msg_ref, wide_ref, own_ref, points, sems):
@@ -73,24 +72,23 @@
         cost_estimate=pl.CostEstimate(flops=1000000, bytes_accessed=0, transcendentals=0),
         compiler_params=ROOM,
         name="prep",
-    )(coords, omega, piece)
+    )(*[pltpu.with_memory_space_constraint(x, pltpu.HBM) for x in (coords, omega, piece)])
 
 
 def attach_kernel(list_rows, msg_in_ref, *refs):
     pieces, msg_ref, tail_ref = refs[:-2], refs[-2], refs[-1]
-    size, rows_all = tail_ref.shape[0], msg_ref.shape[0]
-    first = list_start(rows_all, list_rows)
+    leaf = msg_ref.shape[0] - tail_ref.shape[0]
+    first = coord_rows(leaf)
     listed = jnp.concatenate([piece[...] for piece in pieces], axis=1)
     rows = []
     for digit in (listed // BASE, listed % BASE):
         digit = digit.astype(jnp.float32)
         rows += [digit[:, r * LANES : (r + 1) * LANES] for r in range(list_rows)]
-    rows.append(jnp.zeros((rows_all - first - len(rows), LANES), jnp.float32))
-    rows = jnp.concatenate(rows, axis=0).astype(jnp.bfloat16)
-    msg_ref[first:, :] = rows
-    held = size - (rows_all - first)
-    tail_ref[0:held, :] = msg_in_ref[rows_all - size : first, :]
-    tail_ref[held:, :] = rows
+    tail = msg_in_ref[leaf:, :].astype(jnp.float32)
+    rows = [tail[:first, :]] + rows + [tail[first + 2 * list_rows :, :]]
+    tail = jnp.concatenate([part for part in rows if part.shape[0]], axis=0).astype(jnp.bfloat16)
+    msg_ref[leaf:, :] = tail
+    tail_ref[...] = tail
 
 
 def attach(list_rows, size, msg, pieces):
@@ -143,8 +141,8 @@
             tile_ref[p : p + step, k * LANES : (k + 1) * LANES] = entry.astype(jnp.bfloat16)
 
 
-def listed_in(tail, list_rows):
-    first = list_start(tail.shape[0], list_rows)
+def listed_in(tail, leaf, list_rows):
+    first = coord_rows(leaf)
     high = tail[first : first + list_rows, :]
     low = tail[first + list_rows : first + 2 * list_rows, :]
     return high * BASE + low
@@ -176,7 +174,7 @@
     row_ref, col_ref, tile_ref = refs[-3], refs[-2], refs[-1]
     leaf = wide_ref.shape[1]
     me = lax.axis_index("node")
-    mine = listed_in(tail_ref[...].astype(jnp.float32), list_rows)
+    mine = listed_in(tail_ref[...].astype(jnp.float32), leaf, list_rows)
     if started:
         row_total, col_total = refs[len(bits)][...], refs[len(bits) + 1][...]
     else:
@@ -188,7 +186,7 @@
         weight = weight_wide(mine, me ^ bit, me, leaf)
         plain, taken = both_products(tile_ref[...], msg[0:leaf, :], weight)
         row_total = row_total + taken
-        col_total = col_total + count_wide(listed_in(tail, list_rows), me, leaf) * plain
+        col_total = col_total + count_wide(listed_in(tail, leaf, list_rows), me, leaf) * plain
     row_ref[...] = row_total.astype(row_ref.dtype)
     col_ref[...] = col_total
 
@@ -222,24 +220,25 @@
     across = [(0, omega)]
     for bit in reversed(far_bits):
         across += [(bits | bit, swap(block, "node", bit)) for bits, block in across]
-    pieces = [swap(skeleton, "rep", bits) for bits in range(1, reps)]
+    pieces = [swap(skeleton, "rep", bits) for bits in reversed(range(1, reps))]
     msg, wide, own_piece = prep(list_rows, coords, omega, skeleton)
     msg, tail = attach(list_rows, size, msg, [own_piece] + pieces)
     tails = [(0, tail)]
     for bit in reversed(far_bits):
         tails += [(bits | bit, swap(part, "node", bit)) for bits, part in tails]
     msgs = [swap(msg, "node", step) for step in QUAD]
-    totals = add_blocks(list_rows, [0], wide, tail, [msg], ())
-    totals = add_blocks(list_rows, QUAD, wide, tail, msgs, totals)
+    arrived = [(step, msg) for step, msg in zip(QUAD, msgs)]
+    early = [(0, msg)]
+    late = []
     for (bits, block), (_, part) in zip(across[1:], tails[1:]):
         msg = pack(block, part)
-        msgs = [swap(msg, "node", step) for step in QUAD]
-        totals = add_blocks(list_rows, [bits], wide, tail, [msg], totals)
-        for step, msg in zip(QUAD, msgs):
-            final = bits == across[-1][0] and step == QUAD[-1]
-            totals = add_blocks(
-                list_rows, [bits | step], wide, tail, [msg], totals, jnp.bfloat16 if final else jnp.float32
-            )
+        late += [(bits | step, swap(msg, "node", step)) for step in QUAD]
+        early.append((bits, msg))
+    totals = ()
+    blocks = early + arrived[2:] + arrived[:2] + late
+    for place, (bits, msg) in enumerate(blocks):
+        row_type = jnp.float32 if place + 1 < len(blocks) else jnp.bfloat16
+        totals = add_blocks(list_rows, [bits], wide, tail, [msg], totals, row_type)
     return totals
 
 

time: 29.8 us -> 29.3 us (0.983)
  local copies, waits for them, and re-layouts: 2.25 us -> 0.01 us
  Pallas kernels: 7.55 us -> 8.58 us
  starting transfers between devices: 13.2 us -> 13.9 us
    unnamed x6 -> x2, local copies, waits for them, and re-layouts: 2.25 us -> 0.01 us
    ppermute x11, starting transfers between devices: 13.2 us -> 13.9 us  [swap(): lax.ppermute(block, axis, [(i, i ^ bits) for i in range(lax.axis_size(axi...]
    pallas_call x1, Pallas kernels: 0.57 us -> 1.12 us  [prep(): pl.pallas_call(prep_kernel, out_shape=(jax.ShapeDtypeStruct((leaf + tail_...]
    pallas_call x6 -> x8, Pallas kernels: 6.88 us -> 7.36 us  [add_blocks(): pl.pallas_call(functools.partial(blocks_kernel, list_rows, bits, bool(tot...]
  transfers between devices with their start and end apart: 11 -> 11, of which waited for: 2 -> 2; matrix products, arithmetic and copies ran while one was open for 0% -> 0% of each run, Pallas kernels for 20% -> 24%
where the time goes in v3:
time: 29.3 us; the launch traced here: 29.2 us
  starting transfers between devices  13.9 us (47%)
  Pallas kernels  8.58 us (29%)
  waiting for transfers between devices  6.01 us (21%)
  between operations  0.69 us (2%)
    ppermute x11, starting transfers between devices, swap(): lax.ppermute(block, axis, [(i, i ^ bits) for i in range(lax.axis_size(axi...  13.9 us
    pallas_call x8, Pallas kernels, add_blocks(): pl.pallas_call(functools.partial(blocks_kernel, list_rows, bits, bool(tot...  7.36 us
    ppermute x11, waiting for transfers between devices, swap(): lax.ppermute(block, axis, [(i, i ^ bits) for i in range(lax.axis_size(axi...  6.01 us
    pallas_call x1, Pallas kernels, prep(): pl.pallas_call(prep_kernel, out_shape=(jax.ShapeDtypeStruct((leaf + tail_...  1.12 us
  transfers between devices with their start and end apart: 11, of which 2 were waited for; matrix products, arithmetic and copies ran while one was open for 0% of the time, Pallas kernels for 24%

profile of v3, /device:TPU:0, one launch (start us, length us, event | category | flops | bytes accessed | tf_op | source)
XLA Modules:
  0.0 29.2 jit_solution(17677725536683705174)
XLA Ops:
  0.6 0.0 copy-start
  0.6 2.5 %collective-permute-start = (s32[1,64]{1,0:T(1,128)}, s32[1,64]{1,0:T(1,128)S(1)}, u32[]{:S(2)}, u32[]{:S(2)}) collective-permute-start(s32[1,64]{1,0:T(1,128)} %piece_ref.1), channel_id=1, source_target_pairs={{0,3},{1,2},{2,1},{3,0},{4,7},{5,6},{6,5},{7,4},{8,11},{9,10},{10,... | collective-permute-start | bytes 776 | tf_op jit(solution)/shard_map/ppermute | solution.py:209
  3.1 0.6 %collective-permute-start.1 = (s32[1,64]{1,0:T(1,128)}, s32[1,64]{1,0:T(1,128)S(1)}, u32[]{:S(2)}, u32[]{:S(2)}) collective-permute-start(s32[1,64]{1,0:T(1,128)} %piece_ref.1), channel_id=1, source_target_pairs={{0,2},{1,3},{2,0},{3,1},{4,6},{5,7},{6,4},{7,5},{8,10},{9,11},{10,... | collective-permute-start | bytes 776 | tf_op jit(solution)/shard_map/ppermute | solution.py:209
  3.8 0.0 collective-permute-start.2
  3.8 1.1 %prep.1 = (bf16[560,128]{1,0:T(8,128)(2,1)S(1)}, f32[3,512,128]{2,1,0:T(8,128)S(1)}, s32[1,64]{1,0:T(1,128)S(1)}) custom-call(f32[3,512]{1,0:T(4,128)} %coords_ref.1, bf16[512,128]{1,0:T(8,128)(2,1)} %omega_ref.1, s32[1,64]{1,0:T(1,128)} %piece_ref.1), custom_call_target="tpu_custom_call" | custom-call | flops 1000000 | tf_op jit(solution)/shard_map/prep/pallas_call | solution.py:62
  4.9 0.0 collective-permute-done.refs_1_
  4.9 1.9 %collective-permute-done.1.refs_2_ = s32[1,64]{1,0:T(1,128)S(1)} collective-permute-done((s32[1,64]{1,0:T(1,128)}, s32[1,64]{1,0:T(1,128)S(1)}, u32[]{:S(2)}, u32[]{:S(2)}) %collective-permute-start.1) | collective-permute-done | bytes 288 | tf_op jit(solution)/shard_map/ppermute | solution.py:209
  6.8 0.0 collective-permute-done.2.refs_3_
  6.8 0.1 attach.1
  6.9 2.6 %collective-permute-start.10 = (bf16[560,128]{1,0:T(8,128)(2,1)S(1)}, bf16[560,128]{1,0:T(8,128)(2,1)S(1)}, u32[]{:S(2)}, u32[]{:S(2)}) collective-permute-start(bf16[560,128]{1,0:T(8,128)(2,1)S(1)} %get-tuple-element.25.refs_0_), channel_id=1, source_target_pairs={{0,12},{4,8},{8,4},{12,0},{16,28},{20,24},{24,20},{28,16},{1,13},{... | collective-permute-start | bytes 430088 | tf_op jit(solution)/shard_map/ppermute | solution.py:209
  9.5 0.0 copy-done
  9.5 2.6 %collective-permute-start.3 = (bf16[512,128]{1,0:T(8,128)(2,1)S(1)}, bf16[512,128]{1,0:T(8,128)(2,1)S(1)}, u32[]{:S(2)}, u32[]{:S(2)}) collective-permute-start(bf16[512,128]{1,0:T(8,128)(2,1)S(1)} %copy-done), channel_id=1, source_target_pairs={{0,16},{4,20},{8,24},{12,28},{16,0},{20,4},{24,8},{28,12},{1,17},{... | collective-permute-start | bytes 393224 | tf_op jit(solution)/shard_map/ppermute | solution.py:209
  12.1 0.3 %collective-permute-start.4 = (bf16[48,128]{1,0:T(8,128)(2,1)S(1)}, bf16[48,128]{1,0:T(8,128)(2,1)S(1)}, u32[]{:S(2)}, u32[]{:S(2)}) collective-permute-start(bf16[48,128]{1,0:T(8,128)(2,1)S(1)} %get-tuple-element.24.tail_ref), channel_id=1, source_target_pairs={{0,16},{4,20},{8,24},{12,28},{16,0},{20,4},{24,8},{28,12},{1,17},{... | collective-permute-start | bytes 36872 | tf_op jit(solution)/shard_map/ppermute | solution.py:209
  12.4 0.5 %collective-permute-start.9 = (bf16[560,128]{1,0:T(8,128)(2,1)S(1)}, bf16[560,128]{1,0:T(8,128)(2,1)S(1)}, u32[]{:S(2)}, u32[]{:S(2)}) collective-permute-start(bf16[560,128]{1,0:T(8,128)(2,1)S(1)} %get-tuple-element.25.refs_0_), channel_id=1, source_target_pairs={{0,4},{4,0},{8,12},{12,8},{16,20},{20,16},{24,28},{28,24},{1,5},{5... | collective-permute-start | bytes 430088 | tf_op jit(solution)/shard_map/ppermute | solution.py:209
  12.9 0.4 %collective-permute-start.8 = (bf16[560,128]{1,0:T(8,128)(2,1)S(1)}, bf16[560,128]{1,0:T(8,128)(2,1)S(1)}, u32[]{:S(2)}, u32[]{:S(2)}) collective-permute-start(bf16[560,128]{1,0:T(8,128)(2,1)S(1)} %get-tuple-element.25.refs_0_), channel_id=1, source_target_pairs={{0,8},{4,12},{8,0},{12,4},{16,24},{20,28},{24,16},{28,20},{1,9},{5... | collective-permute-start | bytes 430088 | tf_op jit(solution)/shard_map/ppermute | solution.py:209
  13.4 4.1 %collective-permute-done.4.tail_ref = bf16[48,128]{1,0:T(8,128)(2,1)S(1)} collective-permute-done((bf16[48,128]{1,0:T(8,128)(2,1)S(1)}, bf16[48,128]{1,0:T(8,128)(2,1)S(1)}, u32[]{:S(2)}, u32[]{:S(2)}) %collective-permute-start.4) | collective-permute-done | bytes 12320 | tf_op jit(solution)/shard_map/ppermute | solution.py:209
  17.5 0.0 collective-permute-done.3.block_ref
  17.5 0.8 %collective-permute-start.7 = (bf16[560,128]{1,0:T(8,128)(2,1)S(1)}, bf16[560,128]{1,0:T(8,128)(2,1)S(1)}, u32[]{:S(2)}, u32[]{:S(2)}) collective-permute-start(bf16[560,128]{1,0:T(8,128)(2,1)S(1)} %pack.1.refs_0_), channel_id=1, source_target_pairs={{0,4},{4,0},{8,12},{12,8},{16,20},{20,16},{24,28},{28,24},{1,5},{5... | collective-permute-start | bytes 430088 | tf_op jit(solution)/shard_map/ppermute | solution.py:209
  18.3 2.3 %collective-permute-start.6 = (bf16[560,128]{1,0:T(8,128)(2,1)S(1)}, bf16[560,128]{1,0:T(8,128)(2,1)S(1)}, u32[]{:S(2)}, u32[]{:S(2)}) collective-permute-start(bf16[560,128]{1,0:T(8,128)(2,1)S(1)} %pack.1.refs_0_), channel_id=1, source_target_pairs={{0,8},{4,12},{8,0},{12,4},{16,24},{20,28},{24,16},{28,20},{1,9},{5... | collective-permute-start | bytes 430088 | tf_op jit(solution)/shard_map/ppermute | solution.py:209
  20.6 0.0 collective-permute-done.10.refs_0_
  20.6 1.2 %collective-permute-start.5 = (bf16[560,128]{1,0:T(8,128)(2,1)S(1)}, bf16[560,128]{1,0:T(8,128)(2,1)S(1)}, u32[]{:S(2)}, u32[]{:S(2)}) collective-permute-start(bf16[560,128]{1,0:T(8,128)(2,1)S(1)} %pack.1.refs_0_), channel_id=1, source_target_pairs={{0,12},{4,8},{8,4},{12,0},{16,28},{20,24},{24,20},{28,16},{1,13},{... | collective-permute-start | bytes 430088 | tf_op jit(solution)/shard_map/ppermute | solution.py:209
  21.8 0.8 %add_blocks.8 = (f32[512,128]{1,0:T(8,128)S(1)}, f32[512,128]{1,0:T(8,128)S(1)}) custom-call(f32[3,512,128]{2,1,0:T(8,128)S(1)} %get-tuple-element.21.wide_ref, bf16[48,128]{1,0:T(8,128)(2,1)S(1)} %get-tuple-element.24.tail_ref, bf16[560,128]{1,0:T(8,128)(2,1)S(1)} %get-tuple-element.25.refs_0_), custom_call_target="tpu_custom_call" | custom-call | tf_op jit(solution)/shard_map/add_blocks/pallas_call | solution.py:197
  22.6 0.8 %add_blocks.9 = (f32[512,128]{1,0:T(8,128)S(1)}, f32[512,128]{1,0:T(8,128)S(1)}) custom-call(f32[3,512,128]{2,1,0:T(8,128)S(1)} %get-tuple-element.21.wide_ref, bf16[48,128]{1,0:T(8,128)(2,1)S(1)} %get-tuple-element.24.tail_ref, bf16[560,128]{1,0:T(8,128)(2,1)S(1)} %pack.1.refs_0_, f32[512,128]{1,0:T(8,128)S(1)} %get-tuple-element.26.refs_1_, ...), custom_call_target="tpu_custom_call" | custom-call | tf_op jit(solution)/shard_map/add_blocks/pallas_call | solution.py:197
  23.4 0.8 %add_blocks.10 = (f32[512,128]{1,0:T(8,128)S(1)}, f32[512,128]{1,0:T(8,128)S(1)}) custom-call(f32[3,512,128]{2,1,0:T(8,128)S(1)} %get-tuple-element.21.wide_ref, bf16[48,128]{1,0:T(8,128)(2,1)S(1)} %get-tuple-element.24.tail_ref, bf16[560,128]{1,0:T(8,128)(2,1)S(1)} %collective-permute-done.10.refs_0_, f32[512,128]{1,0:T(8,128)S(1)} %get-tuple-element.28.refs_1_, ...), custom_call_target="tpu_custom_call" | custom-call | tf_op jit(solution)/shard_map/add_blocks/pallas_call | solution.py:197
  24.2 0.0 collective-permute-done.9.refs_0_
  24.2 0.8 %add_blocks.11 = (f32[512,128]{1,0:T(8,128)S(1)}, f32[512,128]{1,0:T(8,128)S(1)}) custom-call(f32[3,512,128]{2,1,0:T(8,128)S(1)} %get-tuple-element.21.wide_ref, bf16[48,128]{1,0:T(8,128)(2,1)S(1)} %get-tuple-element.24.tail_ref, bf16[560,128]{1,0:T(8,128)(2,1)S(1)} %collective-permute-done.9.refs_0_, f32[512,128]{1,0:T(8,128)S(1)} %get-tuple-element.30.refs_1_, ...), custom_call_target="tpu_custom_call" | custom-call | tf_op jit(solution)/shard_map/add_blocks/pallas_call | solution.py:197
  25.1 0.0 collective-permute-done.8.refs_0_
  25.1 0.8 %add_blocks.12 = (f32[512,128]{1,0:T(8,128)S(1)}, f32[512,128]{1,0:T(8,128)S(1)}) custom-call(f32[3,512,128]{2,1,0:T(8,128)S(1)} %get-tuple-element.21.wide_ref, bf16[48,128]{1,0:T(8,128)(2,1)S(1)} %get-tuple-element.24.tail_ref, bf16[560,128]{1,0:T(8,128)(2,1)S(1)} %collective-permute-done.8.refs_0_, f32[512,128]{1,0:T(8,128)S(1)} %get-tuple-element.32.refs_1_, ...), custom_call_target="tpu_custom_call" | custom-call | tf_op jit(solution)/shard_map/add_blocks/pallas_call | solution.py:197
  25.9 0.0 collective-permute-done.7.refs_0_
  25.9 0.8 %add_blocks.13 = (f32[512,128]{1,0:T(8,128)S(1)}, f32[512,128]{1,0:T(8,128)S(1)}) custom-call(f32[3,512,128]{2,1,0:T(8,128)S(1)} %get-tuple-element.21.wide_ref, bf16[48,128]{1,0:T(8,128)(2,1)S(1)} %get-tuple-element.24.tail_ref, bf16[560,128]{1,0:T(8,128)(2,1)S(1)} %collective-permute-done.7.refs_0_, f32[512,128]{1,0:T(8,128)S(1)} %get-tuple-element.34.refs_1_, ...), custom_call_target="tpu_custom_call" | custom-call | tf_op jit(solution)/shard_map/add_blocks/pallas_call | solution.py:197
  26.7 0.0 collective-permute-done.6.refs_0_
  26.7 0.8 %add_blocks.14 = (f32[512,128]{1,0:T(8,128)S(1)}, f32[512,128]{1,0:T(8,128)S(1)}) custom-call(f32[3,512,128]{2,1,0:T(8,128)S(1)} %get-tuple-element.21.wide_ref, bf16[48,128]{1,0:T(8,128)(2,1)S(1)} %get-tuple-element.24.tail_ref, bf16[560,128]{1,0:T(8,128)(2,1)S(1)} %collective-permute-done.6.refs_0_, f32[512,128]{1,0:T(8,128)S(1)} %get-tuple-element.36.refs_1_, ...), custom_call_target="tpu_custom_call" | custom-call | tf_op jit(solution)/shard_map/add_blocks/pallas_call | solution.py:197
  27.6 0.0 collective-permute-done.5.refs_0_
  27.6 1.6 %add_blocks.15 = (bf16[512,128]{1,0:T(8,128)(2,1)}, f32[512,128]{1,0:T(8,128)}) custom-call(f32[3,512,128]{2,1,0:T(8,128)S(1)} %get-tuple-element.21.wide_ref, bf16[48,128]{1,0:T(8,128)(2,1)S(1)} %get-tuple-element.24.tail_ref, bf16[560,128]{1,0:T(8,128)(2,1)S(1)} %collective-permute-done.5.refs_0_, f32[512,128]{1,0:T(8,128)S(1)} %get-tuple-element.38.refs_1_, ...), custom_call_target="tpu_custom_call" | custom-call | tf_op jit(solution)/shard_map/add_blocks/pallas_call | solution.py:197
  (1 shorter events, 0.0 us)
Async XLA Ops:
  0.6 8.9 %copy-start = (bf16[512,128]{1,0:T(8,128)(2,1)S(1)}, bf16[512,128]{1,0:T(8,128)(2,1)}, u32[]{:S(2)}) copy-start(bf16[512,128]{1,0:T(8,128)(2,1)} %omega_ref.1) | copy-start | bytes 393220
  0.6 4.3 %collective-permute-start = (s32[1,64]{1,0:T(1,128)}, s32[1,64]{1,0:T(1,128)S(1)}, u32[]{:S(2)}, u32[]{:S(2)}) collective-permute-start(s32[1,64]{1,0:T(1,128)} %piece_ref.1), channel_id=1, source_target_pairs={{0,3},{1,2},{2,1},{3,0},{4,7},{5,6},{6,5},{7,4},{8,11},{9,10},{10,... | collective-permute-start | bytes 776 | tf_op jit(solution)/shard_map/ppermute | solution.py:209
  3.1 3.7 %collective-permute-start.1 = (s32[1,64]{1,0:T(1,128)}, s32[1,64]{1,0:T(1,128)S(1)}, u32[]{:S(2)}, u32[]{:S(2)}) collective-permute-start(s32[1,64]{1,0:T(1,128)} %piece_ref.1), channel_id=1, source_target_pairs={{0,2},{1,3},{2,0},{3,1},{4,6},{5,7},{6,4},{7,5},{8,10},{9,11},{10,... | collective-permute-start | bytes 776 | tf_op jit(solution)/shard_map/ppermute | solution.py:209
  3.8 3.1 %collective-permute-start.2 = (s32[1,64]{1,0:T(1,128)}, s32[1,64]{1,0:T(1,128)S(1)}, u32[]{:S(2)}, u32[]{:S(2)}) collective-permute-start(s32[1,64]{1,0:T(1,128)} %piece_ref.1), channel_id=1, source_target_pairs={{0,1},{1,0},{2,3},{3,2},{4,5},{5,4},{6,7},{7,6},{8,9},{9,8},{10,11... | collective-permute-start | bytes 776 | tf_op jit(solution)/shard_map/ppermute | solution.py:209
  6.9 13.7 %collective-permute-start.10 = (bf16[560,128]{1,0:T(8,128)(2,1)S(1)}, bf16[560,128]{1,0:T(8,128)(2,1)S(1)}, u32[]{:S(2)}, u32[]{:S(2)}) collective-permute-start(bf16[560,128]{1,0:T(8,128)(2,1)S(1)} %get-tuple-element.25.refs_0_), channel_id=1, source_target_pairs={{0,12},{4,8},{8,4},{12,0},{16,28},{20,24},{24,20},{28,16},{1,13},{... | collective-permute-start | bytes 430088 | tf_op jit(solution)/shard_map/ppermute | solution.py:209
  9.5 8.0 %collective-permute-start.3 = (bf16[512,128]{1,0:T(8,128)(2,1)S(1)}, bf16[512,128]{1,0:T(8,128)(2,1)S(1)}, u32[]{:S(2)}, u32[]{:S(2)}) collective-permute-start(bf16[512,128]{1,0:T(8,128)(2,1)S(1)} %copy-done), channel_id=1, source_target_pairs={{0,16},{4,20},{8,24},{12,28},{16,0},{20,4},{24,8},{28,12},{1,17},{... | collective-permute-start | bytes 393224 | tf_op jit(solution)/shard_map/ppermute | solution.py:209
  12.1 5.4 %collective-permute-start.4 = (bf16[48,128]{1,0:T(8,128)(2,1)S(1)}, bf16[48,128]{1,0:T(8,128)(2,1)S(1)}, u32[]{:S(2)}, u32[]{:S(2)}) collective-permute-start(bf16[48,128]{1,0:T(8,128)(2,1)S(1)} %get-tuple-element.24.tail_ref), channel_id=1, source_target_pairs={{0,16},{4,20},{8,24},{12,28},{16,0},{20,4},{24,8},{28,12},{1,17},{... | collective-permute-start | bytes 36872 | tf_op jit(solution)/shard_map/ppermute | solution.py:209
  12.4 11.8 %collective-permute-start.9 = (bf16[560,128]{1,0:T(8,128)(2,1)S(1)}, bf16[560,128]{1,0:T(8,128)(2,1)S(1)}, u32[]{:S(2)}, u32[]{:S(2)}) collective-permute-start(bf16[560,128]{1,0:T(8,128)(2,1)S(1)} %get-tuple-element.25.refs_0_), channel_id=1, source_target_pairs={{0,4},{4,0},{8,12},{12,8},{16,20},{20,16},{24,28},{28,24},{1,5},{5... | collective-permute-start | bytes 430088 | tf_op jit(solution)/shard_map/ppermute | solution.py:209
  12.9 12.1 %collective-permute-start.8 = (bf16[560,128]{1,0:T(8,128)(2,1)S(1)}, bf16[560,128]{1,0:T(8,128)(2,1)S(1)}, u32[]{:S(2)}, u32[]{:S(2)}) collective-permute-start(bf16[560,128]{1,0:T(8,128)(2,1)S(1)} %get-tuple-element.25.refs_0_), channel_id=1, source_target_pairs={{0,8},{4,12},{8,0},{12,4},{16,24},{20,28},{24,16},{28,20},{1,9},{5... | collective-permute-start | bytes 430088 | tf_op jit(solution)/shard_map/ppermute | solution.py:209
  17.5 8.4 %collective-permute-start.7 = (bf16[560,128]{1,0:T(8,128)(2,1)S(1)}, bf16[560,128]{1,0:T(8,128)(2,1)S(1)}, u32[]{:S(2)}, u32[]{:S(2)}) collective-permute-start(bf16[560,128]{1,0:T(8,128)(2,1)S(1)} %pack.1.refs_0_), channel_id=1, source_target_pairs={{0,4},{4,0},{8,12},{12,8},{16,20},{20,16},{24,28},{28,24},{1,5},{5... | collective-permute-start | bytes 430088 | tf_op jit(solution)/shard_map/ppermute | solution.py:209
  18.3 8.5 %collective-permute-start.6 = (bf16[560,128]{1,0:T(8,128)(2,1)S(1)}, bf16[560,128]{1,0:T(8,128)(2,1)S(1)}, u32[]{:S(2)}, u32[]{:S(2)}) collective-permute-start(bf16[560,128]{1,0:T(8,128)(2,1)S(1)} %pack.1.refs_0_), channel_id=1, source_target_pairs={{0,8},{4,12},{8,0},{12,4},{16,24},{20,28},{24,16},{28,20},{1,9},{5... | collective-permute-start | bytes 430088 | tf_op jit(solution)/shard_map/ppermute | solution.py:209
  20.6 7.0 %collective-permute-start.5 = (bf16[560,128]{1,0:T(8,128)(2,1)S(1)}, bf16[560,128]{1,0:T(8,128)(2,1)S(1)}, u32[]{:S(2)}, u32[]{:S(2)}) collective-permute-start(bf16[560,128]{1,0:T(8,128)(2,1)S(1)} %pack.1.refs_0_), channel_id=1, source_target_pairs={{0,12},{4,8},{8,4},{12,0},{16,28},{20,24},{24,20},{28,16},{1,13},{... | collective-permute-start | bytes 430088 | tf_op jit(solution)/shard_map/ppermute | solution.py:209

commit v4 on v3

v4 whole, which is shorter than its diff:
```python
import functools

import jax
import jax.numpy as jnp
from jax import lax
from jax.experimental import pallas as pl
from jax.experimental.pallas import tpu as pltpu
from jax.sharding import PartitionSpec as P


kernel_scale = 0.0078125
softening = 0.02
stretch = 1.0 / kernel_scale
soft_term = softening * softening * stretch * stretch
TERMS = 3
LANES = 128
BASE = 256
QUAD = (1, 2, 3)

VMEM = pl.BlockSpec(memory_space=pltpu.VMEM)
ROOM = pltpu.CompilerParams(vmem_limit_bytes=16 * 1024 * 1024)


def term_rows(leaf):
    return -(-4 * (leaf // LANES) // 16) * 16


def spare_row(leaf, index):
    chunks = leaf // LANES
    return (index // chunks) * term_rows(leaf) + 4 * (index % chunks) + 3


def split(value):
    terms = []
    for _ in range(TERMS):
        term = value.astype(jnp.bfloat16).astype(jnp.float32)
        value = value - term
        terms.append(term)
    return terms


def row_kind(rows):
    return lax.broadcasted_iota(jnp.int32, (rows, LANES), 0) % 4


def centred(points, nodes, me):
    kind = row_kind(points.shape[0])
    first = (2 * me + 1).astype(jnp.float32) * (stretch / nodes)
    middle = jnp.where(kind == 0, first, 0.5 * stretch)
    return jnp.where(kind == 3, 0.0, points - middle)


def factors(points, left):
    spare = row_kind(points.shape[0]) == 3
    square = points * points
    norm = pltpu.roll(square, 1, 0) + pltpu.roll(square, 2, 0) + pltpu.roll(square, 3, 0)
    norm = jnp.where(spare, norm + soft_term if left else norm, 0.0)
    one = jnp.where(spare, 1.0, 0.0)
    high, middle, low = split(-2.0 * points if left else points)
    norms = split(norm)
    if left:
        groups = [high + norms[0], high + norms[1], middle + norms[2], middle + one, high + one, low + one, middle, low]
    else:
        groups = [high + one, middle + one, high + one, middle + norms[0], low + norms[1], high + norms[2], low, middle]
    return groups


def chunk_of(groups, k):
    return jnp.concatenate([group[4 * k : 4 * k + 4, :] for group in groups], axis=0)


def prep_kernel(nodes, coords_ref, omega_ref, piece_ref, msg_ref, left_ref, own_ref, points, sems):
    leaf = points.shape[1]
    chunks = leaf // LANES
    fetch = pltpu.make_async_copy(coords_ref, points, sems.at[0])
    block = pltpu.make_async_copy(omega_ref, msg_ref.at[pl.ds(0, leaf)], sems.at[1])
    piece = pltpu.make_async_copy(piece_ref, own_ref, sems.at[2])
    fetch.start()
    block.start()
    piece.start()
    fetch.wait()
    scaled = points[...] * stretch
    blank = jnp.zeros((1, LANES), jnp.float32)
    rows = []
    for k in range(chunks):
        rows += [scaled[c : c + 1, k * LANES : (k + 1) * LANES] for c in range(3)] + [blank]
    rows += [blank] * (term_rows(leaf) - len(rows))
    rows = jnp.concatenate(rows, axis=0)
    msg_ref[leaf:, :] = jnp.concatenate(split(rows), axis=0).astype(jnp.bfloat16)
    groups = factors(centred(rows, nodes, lax.axis_index("node")), True)
    for k in range(chunks):
        left_ref[k * LANES : (k + 1) * LANES, :] = chunk_of(groups, k).T.astype(jnp.bfloat16)
    block.wait()
    piece.wait()


def prep(coords, omega, piece):
    leaf = coords.shape[1]
    operands = [pltpu.with_memory_space_constraint(x, pltpu.HBM) for x in (coords, omega, piece)]
    return pl.pallas_call(
        functools.partial(prep_kernel, lax.axis_size("node")),
        out_shape=(
            jax.ShapeDtypeStruct((leaf + TERMS * term_rows(leaf), LANES), jnp.bfloat16),
            jax.ShapeDtypeStruct((leaf, 32), jnp.bfloat16),
            jax.ShapeDtypeStruct(piece.shape, piece.dtype),
        ),
        in_specs=[pl.BlockSpec(memory_space=pltpu.HBM)] * 3,
        out_specs=(VMEM,) * 3,
        scratch_shapes=[pltpu.VMEM(coords.shape, jnp.float32), pltpu.SemaphoreType.DMA((3,))],
        compiler_params=ROOM,
        name="prep",
    )(*operands)


def attach_kernel(list_rows, msg_in_ref, *refs):
    pieces, msg_ref, tail_ref = refs[:-2], refs[-2], refs[-1]
    leaf = msg_ref.shape[0] - tail_ref.shape[0]
    listed = jnp.concatenate([piece[...] for piece in pieces], axis=1)
    tail = msg_in_ref[leaf:, :].astype(jnp.float32)
    place = lax.broadcasted_iota(jnp.int32, tail.shape, 0)
    index = 0
    for digit in (listed // BASE, listed % BASE):
        digit = digit.astype(jnp.float32)
        for r in range(list_rows):
            tail = jnp.where(place == spare_row(leaf, index), digit[:, r * LANES : (r + 1) * LANES], tail)
            index += 1
    tail = tail.astype(jnp.bfloat16)
    msg_ref[leaf:, :] = tail
    tail_ref[...] = tail


def attach(list_rows, msg, pieces, leaf):
    return pl.pallas_call(
        functools.partial(attach_kernel, list_rows),
        out_shape=(
            jax.ShapeDtypeStruct(msg.shape, msg.dtype),
            jax.ShapeDtypeStruct((msg.shape[0] - leaf, LANES), msg.dtype),
        ),
        in_specs=[VMEM] * (1 + len(pieces)),
        out_specs=(VMEM, VMEM),
        input_output_aliases={0: 0},
        compiler_params=ROOM,
        name="attach",
    )(msg, *pieces)


def pack_kernel(block_ref, tail_ref, msg_ref):
    leaf = block_ref.shape[0]
    msg_ref[0:leaf, :] = block_ref[...]
    msg_ref[leaf:, :] = tail_ref[...]


def pack(block, tail):
    return pl.pallas_call(
        pack_kernel,
        out_shape=jax.ShapeDtypeStruct((block.shape[0] + tail.shape[0], LANES), block.dtype),
        in_specs=[VMEM, VMEM],
        out_specs=VMEM,
        compiler_params=ROOM,
        name="pack",
    )(block, tail)


def listed_in(tail, leaf, list_rows):
    digits = [tail[spare_row(leaf, r) : spare_row(leaf, r) + 1, :] for r in range(2 * list_rows)]
    return [digits[r] * BASE + digits[list_rows + r] for r in range(list_rows)]


def count_table(listed, first, rows):
    total = jnp.zeros((rows, LANES), jnp.float32)
    for index in listed:
        row = jnp.floor(index * (1.0 / LANES))
        column = index - row * LANES
        rows_hit = jnp.where(lax.broadcasted_iota(jnp.int32, (rows, LANES), 0).astype(jnp.float32) + first == row, 1.0, 0.0)
        lanes_hit = jnp.where(lax.broadcasted_iota(jnp.int32, (LANES, LANES), 0).astype(jnp.float32) == column, 1.0, 0.0)
        total = total + lax.dot_general(
            rows_hit.astype(jnp.bfloat16),
            lanes_hit.astype(jnp.bfloat16),
            (((1,), (1,)), ((), ())),
            preferred_element_type=jnp.float32,
        )
    return total


def widened(table):
    rows = table.shape[0]
    if rows % 8:
        table = jnp.concatenate([table, jnp.zeros((8 - rows % 8, LANES), jnp.float32)], axis=0)
    columns = table.T
    return jnp.concatenate([jnp.broadcast_to(columns[:, k : k + 1], (LANES, LANES)) for k in range(rows)], axis=0)


def block_kernel(nodes, list_rows, bits, started, left_ref, tail_ref, msg_ref, *refs):
    row_ref, col_ref, table_out_ref, right_ref, tile_ref = refs[-5:]
    leaf = left_ref.shape[0]
    chunks = leaf // LANES
    me = lax.axis_index("node")
    if started:
        row_in_ref, col_in_ref, table_ref = refs[:3]
    else:
        mine = listed_in(tail_ref[...].astype(jnp.float32), leaf, list_rows)
        table_out_ref[...] = count_table(mine, 0.0, table_out_ref.shape[0])
        table_ref = table_out_ref
    tail = msg_ref[leaf:, :].astype(jnp.float32)
    term = term_rows(leaf)
    points = (tail[0:term, :] + tail[term : 2 * term, :]) + tail[2 * term : 3 * term, :]
    groups = factors(centred(points, nodes, me), False)
    for k in range(chunks):
        right_ref[:, k * LANES : (k + 1) * LANES] = chunk_of(groups, k).astype(jnp.bfloat16)
    step = LANES
    for p in range(0, leaf, step):
        squared = jnp.dot(left_ref[p : p + step, :], right_ref[...], preferred_element_type=jnp.float32)
        tile_ref[p : p + step, :] = lax.rsqrt(squared).astype(jnp.bfloat16)
    node = me ^ bits
    near = jnp.where(jnp.abs(node - me) <= 1, 1.0, 0.0)
    samples = msg_ref[0:leaf, :]
    weight = widened(table_ref[pl.ds(node * chunks, chunks), :]) + near
    weighted = weight.astype(jnp.bfloat16) * samples
    first = (me * chunks).astype(jnp.float32)
    named = count_table(listed_in(tail, leaf, list_rows), first, -(-chunks // 8) * 8)
    mask = widened(named[0:chunks, :])
    both = jnp.dot(tile_ref[...], jnp.concatenate([samples, weighted], axis=1), preferred_element_type=jnp.float32)
    row, col = both[:, LANES:], mask * both[:, :LANES]
    if started:
        row, col = row_in_ref[...] + row, col_in_ref[...] + col
    row_ref[...] = row.astype(row_ref.dtype)
    col_ref[...] = col


def add_block(list_rows, bits, left, tail, msg, totals, row_type=jnp.float32):
    leaf = left.shape[0]
    nodes = lax.axis_size("node")
    part = (leaf, LANES)
    outs = [jax.ShapeDtypeStruct(part, row_type), jax.ShapeDtypeStruct(part, jnp.float32)]
    scratch = [pltpu.VMEM((32, leaf), jnp.bfloat16), pltpu.VMEM((leaf, leaf), jnp.bfloat16)]
    table_shape = (-(-nodes * (leaf // LANES) // 8) * 8, LANES)
    if totals:
        scratch = [pltpu.VMEM((8, LANES), jnp.float32)] + scratch
    else:
        outs.append(jax.ShapeDtypeStruct(table_shape, jnp.float32))
    result = pl.pallas_call(
        functools.partial(block_kernel, nodes, list_rows, bits, bool(totals)),
        out_shape=outs,
        in_specs=[VMEM] * (3 + len(totals)),
        out_specs=[VMEM] * len(outs),
        scratch_shapes=scratch,
        compiler_params=ROOM,
        name="add_block",
    )(left, tail, msg, *totals)
    return (result[0], result[1], totals[2] if totals else result[2])


def swap(block, axis, bits):
    return lax.ppermute(block, axis, [(i, i ^ bits) for i in range(lax.axis_size(axis))])


def on_device(coords, omega, skeleton):
    nodes = lax.axis_size("node")
    reps = lax.axis_size("rep")
    list_rows = reps * skeleton.shape[1] // LANES
    far_bits = [1 << k for k in range(2, nodes.bit_length() - 1)]

    across = [(0, omega)]
    for bit in reversed(far_bits):
        across += [(bits | bit, swap(block, "node", bit)) for bits, block in across]
    pieces = [swap(skeleton, "rep", bits) for bits in reversed(range(1, reps))]
    msg, left, own_piece = prep(coords, omega, skeleton)
    msg, tail = attach(list_rows, msg, [own_piece] + pieces, coords.shape[1])
    tails = [(0, tail)]
    for bit in reversed(far_bits):
        tails += [(bits | bit, swap(part, "node", bit)) for bits, part in tails]
    msgs = [swap(msg, "node", step) for step in QUAD]
    arrived = [(step, msg) for step, msg in zip(QUAD, msgs)]
    early = [(0, msg)]
    late = []
    for (bits, block), (_, part) in zip(across[1:], tails[1:]):
        msg = pack(block, part)
        late += [(bits | step, swap(msg, "node", step)) for step in QUAD]
        early.append((bits, msg))
    totals = ()
    blocks = early + arrived[2:] + arrived[:2] + late
    for place, (bits, msg) in enumerate(blocks):
        row_type = jnp.float32 if place + 1 < len(blocks) else jnp.bfloat16
        totals = add_block(list_rows, bits, left, tail, msg, totals, row_type)
    return totals[:2]


def solution(mesh):
    in_specs = (P(None, "node"), P("node", "rep"), P("node", "rep"))
    out_specs = (P("node", "rep"), P("node", "rep"))
    return jax.shard_map(on_device, mesh=mesh, in_specs=in_specs, out_specs=out_specs, check_vma=False)
```

time: 29.3 us -> 28.2 us (0.962)
  Pallas kernels: 8.58 us -> 7.29 us
    pallas_call x9, Pallas kernels: 8.48 us -> 7.2 us  [the longest x8 6.25 us: add_block(): pl.pallas_call(functools.partial(block_kernel, nodes, list_rows, bits, bo...]
  transfers between devices with their start and end apart: 11 -> 11, of which waited for: 2 -> 2; matrix products, arithmetic and copies ran while one was open for 0% -> 0% of each run, Pallas kernels for 24% -> 21%
where the time goes in v4:
time: 28.2 us; the launch traced here: 28.1 us
  starting transfers between devices  13.9 us (49%)
  Pallas kernels  7.29 us (26%)
  waiting for transfers between devices  6.18 us (22%)
  between operations  0.73 us (3%)
    ppermute x11, starting transfers between devices, swap(): lax.ppermute(block, axis, [(i, i ^ bits) for i in range(lax.axis_size(axi...  13.9 us
    pallas_call x8, Pallas kernels, add_block(): pl.pallas_call(functools.partial(block_kernel, nodes, list_rows, bits, bo...  6.25 us
    ppermute x11, waiting for transfers between devices, swap(): lax.ppermute(block, axis, [(i, i ^ bits) for i in range(lax.axis_size(axi...  6.18 us
    pallas_call x1, Pallas kernels, prep(): pl.pallas_call(functools.partial(prep_kernel, lax.axis_size('node')), out...  0.95 us
  transfers between devices with their start and end apart: 11, of which 2 were waited for; matrix products, arithmetic and copies ran while one was open for 0% of the time, Pallas kernels for 21%

profile of v4, /device:TPU:0, one launch (start us, length us, event | category | flops | bytes accessed | tf_op | source)
XLA Modules:
  0.0 28.1 jit_solution(13500080036419689888)
XLA Ops:
  0.6 0.0 copy-start
  0.6 2.5 %collective-permute-start = (s32[1,64]{1,0:T(1,128)}, s32[1,64]{1,0:T(1,128)S(1)}, u32[]{:S(2)}, u32[]{:S(2)}) collective-permute-start(s32[1,64]{1,0:T(1,128)} %piece_ref.1), channel_id=1, source_target_pairs={{0,3},{1,2},{2,1},{3,0},{4,7},{5,6},{6,5},{7,4},{8,11},{9,10},{10,... | collective-permute-start | bytes 776 | tf_op jit(solution)/shard_map/ppermute | solution.py:254
  3.1 0.6 %collective-permute-start.1 = (s32[1,64]{1,0:T(1,128)}, s32[1,64]{1,0:T(1,128)S(1)}, u32[]{:S(2)}, u32[]{:S(2)}) collective-permute-start(s32[1,64]{1,0:T(1,128)} %piece_ref.1), channel_id=1, source_target_pairs={{0,2},{1,3},{2,0},{3,1},{4,6},{5,7},{6,4},{7,5},{8,10},{9,11},{10,... | collective-permute-start | bytes 776 | tf_op jit(solution)/shard_map/ppermute | solution.py:254
  3.8 0.0 collective-permute-start.2
  3.8 0.9 %prep.1 = (bf16[560,128]{1,0:T(8,128)(2,1)S(1)}, bf16[512,32]{1,0:T(8,128)(2,1)S(1)}, s32[1,64]{1,0:T(1,128)S(1)}) custom-call(f32[3,512]{1,0:T(4,128)} %coords_ref.1, bf16[512,128]{1,0:T(8,128)(2,1)} %omega_ref.1, s32[1,64]{1,0:T(1,128)} %piece_ref.1), custom_call_target="tpu_custom_call" | custom-call | tf_op jit(solution)/shard_map/prep/pallas_call | solution.py:100
  4.7 0.0 collective-permute-done.refs_1_
  4.8 2.1 %collective-permute-done.1.refs_2_ = s32[1,64]{1,0:T(1,128)S(1)} collective-permute-done((s32[1,64]{1,0:T(1,128)}, s32[1,64]{1,0:T(1,128)S(1)}, u32[]{:S(2)}, u32[]{:S(2)}) %collective-permute-start.1) | collective-permute-done | bytes 288 | tf_op jit(solution)/shard_map/ppermute | solution.py:254
  6.8 0.0 collective-permute-done.2.refs_3_
  6.8 0.1 attach.1
  6.9 2.6 %collective-permute-start.10 = (bf16[560,128]{1,0:T(8,128)(2,1)S(1)}, bf16[560,128]{1,0:T(8,128)(2,1)S(1)}, u32[]{:S(2)}, u32[]{:S(2)}) collective-permute-start(bf16[560,128]{1,0:T(8,128)(2,1)S(1)} %get-tuple-element.26.msg_ref), channel_id=1, source_target_pairs={{0,12},{4,8},{8,4},{12,0},{16,28},{20,24},{24,20},{28,16},{1,13},{... | collective-permute-start | bytes 430088 | tf_op jit(solution)/shard_map/ppermute | solution.py:254
  9.5 0.0 copy-done
  9.5 2.6 %collective-permute-start.3 = (bf16[512,128]{1,0:T(8,128)(2,1)S(1)}, bf16[512,128]{1,0:T(8,128)(2,1)S(1)}, u32[]{:S(2)}, u32[]{:S(2)}) collective-permute-start(bf16[512,128]{1,0:T(8,128)(2,1)S(1)} %copy-done), channel_id=1, source_target_pairs={{0,16},{4,20},{8,24},{12,28},{16,0},{20,4},{24,8},{28,12},{1,17},{... | collective-permute-start | bytes 393224 | tf_op jit(solution)/shard_map/ppermute | solution.py:254
  12.1 0.3 %collective-permute-start.4 = (bf16[48,128]{1,0:T(8,128)(2,1)S(1)}, bf16[48,128]{1,0:T(8,128)(2,1)S(1)}, u32[]{:S(2)}, u32[]{:S(2)}) collective-permute-start(bf16[48,128]{1,0:T(8,128)(2,1)S(1)} %get-tuple-element.25.tail_ref), channel_id=1, source_target_pairs={{0,16},{4,20},{8,24},{12,28},{16,0},{20,4},{24,8},{28,12},{1,17},{... | collective-permute-start | bytes 36872 | tf_op jit(solution)/shard_map/ppermute | solution.py:254
  12.4 0.5 %collective-permute-start.9 = (bf16[560,128]{1,0:T(8,128)(2,1)S(1)}, bf16[560,128]{1,0:T(8,128)(2,1)S(1)}, u32[]{:S(2)}, u32[]{:S(2)}) collective-permute-start(bf16[560,128]{1,0:T(8,128)(2,1)S(1)} %get-tuple-element.26.msg_ref), channel_id=1, source_target_pairs={{0,4},{4,0},{8,12},{12,8},{16,20},{20,16},{24,28},{28,24},{1,5},{5... | collective-permute-start | bytes 430088 | tf_op jit(solution)/shard_map/ppermute | solution.py:254
  12.9 0.4 %collective-permute-start.8 = (bf16[560,128]{1,0:T(8,128)(2,1)S(1)}, bf16[560,128]{1,0:T(8,128)(2,1)S(1)}, u32[]{:S(2)}, u32[]{:S(2)}) collective-permute-start(bf16[560,128]{1,0:T(8,128)(2,1)S(1)} %get-tuple-element.26.msg_ref), channel_id=1, source_target_pairs={{0,8},{4,12},{8,0},{12,4},{16,24},{20,28},{24,16},{28,20},{1,9},{5... | collective-permute-start | bytes 430088 | tf_op jit(solution)/shard_map/ppermute | solution.py:254
  13.4 4.1 %collective-permute-done.4.tail_ref = bf16[48,128]{1,0:T(8,128)(2,1)S(1)} collective-permute-done((bf16[48,128]{1,0:T(8,128)(2,1)S(1)}, bf16[48,128]{1,0:T(8,128)(2,1)S(1)}, u32[]{:S(2)}, u32[]{:S(2)}) %collective-permute-start.4) | collective-permute-done | bytes 12320 | tf_op jit(solution)/shard_map/ppermute | solution.py:254
  17.5 0.0 collective-permute-done.3.block_ref
  17.5 0.8 %collective-permute-start.7 = (bf16[560,128]{1,0:T(8,128)(2,1)S(1)}, bf16[560,128]{1,0:T(8,128)(2,1)S(1)}, u32[]{:S(2)}, u32[]{:S(2)}) collective-permute-start(bf16[560,128]{1,0:T(8,128)(2,1)S(1)} %pack.1.msg_ref), channel_id=1, source_target_pairs={{0,4},{4,0},{8,12},{12,8},{16,20},{20,16},{24,28},{28,24},{1,5},{5... | collective-permute-start | bytes 430088 | tf_op jit(solution)/shard_map/ppermute | solution.py:254
  18.3 2.3 %collective-permute-start.6 = (bf16[560,128]{1,0:T(8,128)(2,1)S(1)}, bf16[560,128]{1,0:T(8,128)(2,1)S(1)}, u32[]{:S(2)}, u32[]{:S(2)}) collective-permute-start(bf16[560,128]{1,0:T(8,128)(2,1)S(1)} %pack.1.msg_ref), channel_id=1, source_target_pairs={{0,8},{4,12},{8,0},{12,4},{16,24},{20,28},{24,16},{28,20},{1,9},{5... | collective-permute-start | bytes 430088 | tf_op jit(solution)/shard_map/ppermute | solution.py:254
  20.6 0.0 collective-permute-done.10.msg_ref
  20.6 1.2 %collective-permute-start.5 = (bf16[560,128]{1,0:T(8,128)(2,1)S(1)}, bf16[560,128]{1,0:T(8,128)(2,1)S(1)}, u32[]{:S(2)}, u32[]{:S(2)}) collective-permute-start(bf16[560,128]{1,0:T(8,128)(2,1)S(1)} %pack.1.msg_ref), channel_id=1, source_target_pairs={{0,12},{4,8},{8,4},{12,0},{16,28},{20,24},{24,20},{28,16},{1,13},{... | collective-permute-start | bytes 430088 | tf_op jit(solution)/shard_map/ppermute | solution.py:254
  21.8 0.8 %add_block.8 = (f32[512,128]{1,0:T(8,128)S(1)}, f32[512,128]{1,0:T(8,128)S(1)}, f32[32,128]{1,0:T(8,128)S(1)}) custom-call(bf16[512,32]{1,0:T(8,128)(2,1)S(1)} %get-tuple-element.22.left_ref, bf16[48,128]{1,0:T(8,128)(2,1)S(1)} %get-tuple-element.25.tail_ref, bf16[560,128]{1,0:T(8,128)(2,1)S(1)} %get-tuple-element.26.msg_ref), custom_call_target="tpu_custom_call" | custom-call | tf_op jit(solution)/shard_map/add_block/pallas_call | solution.py:241
  22.6 0.7 %add_block.9 = (f32[512,128]{1,0:T(8,128)S(1)}, f32[512,128]{1,0:T(8,128)S(1)}) custom-call(bf16[512,32]{1,0:T(8,128)(2,1)S(1)} %get-tuple-element.22.left_ref, bf16[48,128]{1,0:T(8,128)(2,1)S(1)} %get-tuple-element.25.tail_ref, bf16[560,128]{1,0:T(8,128)(2,1)S(1)} %pack.1.msg_ref, f32[512,128]{1,0:T(8,128)S(1)} %get-tuple-element.27.refs_0_, ...), custom_call_target="tpu_custom_call" | custom-call | tf_op jit(solution)/shard_map/add_block/pallas_call | solution.py:241
  23.2 0.7 %add_block.10 = (f32[512,128]{1,0:T(8,128)S(1)}, f32[512,128]{1,0:T(8,128)S(1)}) custom-call(bf16[512,32]{1,0:T(8,128)(2,1)S(1)} %get-tuple-element.22.left_ref, bf16[48,128]{1,0:T(8,128)(2,1)S(1)} %get-tuple-element.25.tail_ref, bf16[560,128]{1,0:T(8,128)(2,1)S(1)} %collective-permute-done.10.msg_ref, f32[512,128]{1,0:T(8,128)S(1)} %get-tuple-element.30.refs_0_, ...), custom_call_target="tpu_custom_call" | custom-call | tf_op jit(solution)/shard_map/add_block/pallas_call | solution.py:241
  23.9 0.0 collective-permute-done.9.msg_ref
  23.9 0.7 %add_block.11 = (f32[512,128]{1,0:T(8,128)S(1)}, f32[512,128]{1,0:T(8,128)S(1)}) custom-call(bf16[512,32]{1,0:T(8,128)(2,1)S(1)} %get-tuple-element.22.left_ref, bf16[48,128]{1,0:T(8,128)(2,1)S(1)} %get-tuple-element.25.tail_ref, bf16[560,128]{1,0:T(8,128)(2,1)S(1)} %collective-permute-done.9.msg_ref, f32[512,128]{1,0:T(8,128)S(1)} %get-tuple-element.32.refs_0_, ...), custom_call_target="tpu_custom_call" | custom-call | tf_op jit(solution)/shard_map/add_block/pallas_call | solution.py:241
  24.6 0.0 collective-permute-done.8.msg_ref
  24.6 0.7 %add_block.12 = (f32[512,128]{1,0:T(8,128)S(1)}, f32[512,128]{1,0:T(8,128)S(1)}) custom-call(bf16[512,32]{1,0:T(8,128)(2,1)S(1)} %get-tuple-element.22.left_ref, bf16[48,128]{1,0:T(8,128)(2,1)S(1)} %get-tuple-element.25.tail_ref, bf16[560,128]{1,0:T(8,128)(2,1)S(1)} %collective-permute-done.8.msg_ref, f32[512,128]{1,0:T(8,128)S(1)} %get-tuple-element.34.refs_0_, ...), custom_call_target="tpu_custom_call" | custom-call | tf_op jit(solution)/shard_map/add_block/pallas_call | solution.py:241
  25.3 0.0 collective-permute-done.7.msg_ref
  25.3 0.7 %add_block.13 = (f32[512,128]{1,0:T(8,128)S(1)}, f32[512,128]{1,0:T(8,128)S(1)}) custom-call(bf16[512,32]{1,0:T(8,128)(2,1)S(1)} %get-tuple-element.22.left_ref, bf16[48,128]{1,0:T(8,128)(2,1)S(1)} %get-tuple-element.25.tail_ref, bf16[560,128]{1,0:T(8,128)(2,1)S(1)} %collective-permute-done.7.msg_ref, f32[512,128]{1,0:T(8,128)S(1)} %get-tuple-element.36.refs_0_, ...), custom_call_target="tpu_custom_call" | custom-call | tf_op jit(solution)/shard_map/add_block/pallas_call | solution.py:241
  26.0 0.0 collective-permute-done.6.msg_ref
  26.0 0.7 %add_block.14 = (f32[512,128]{1,0:T(8,128)S(1)}, f32[512,128]{1,0:T(8,128)S(1)}) custom-call(bf16[512,32]{1,0:T(8,128)(2,1)S(1)} %get-tuple-element.22.left_ref, bf16[48,128]{1,0:T(8,128)(2,1)S(1)} %get-tuple-element.25.tail_ref, bf16[560,128]{1,0:T(8,128)(2,1)S(1)} %collective-permute-done.6.msg_ref, f32[512,128]{1,0:T(8,128)S(1)} %get-tuple-element.38.refs_0_, ...), custom_call_target="tpu_custom_call" | custom-call | tf_op jit(solution)/shard_map/add_block/pallas_call | solution.py:241
  26.7 0.0 collective-permute-done.5.msg_ref
  26.7 1.4 %add_block.15 = (bf16[512,128]{1,0:T(8,128)(2,1)}, f32[512,128]{1,0:T(8,128)}) custom-call(bf16[512,32]{1,0:T(8,128)(2,1)S(1)} %get-tuple-element.22.left_ref, bf16[48,128]{1,0:T(8,128)(2,1)S(1)} %get-tuple-element.25.tail_ref, bf16[560,128]{1,0:T(8,128)(2,1)S(1)} %collective-permute-done.5.msg_ref, f32[512,128]{1,0:T(8,128)S(1)} %get-tuple-element.40.refs_0_, ...), custom_call_target="tpu_custom_call" | custom-call | tf_op jit(solution)/shard_map/add_block/pallas_call | solution.py:241
  (1 shorter events, 0.0 us)
Async XLA Ops:
  0.6 8.9 %copy-start = (bf16[512,128]{1,0:T(8,128)(2,1)S(1)}, bf16[512,128]{1,0:T(8,128)(2,1)}, u32[]{:S(2)}) copy-start(bf16[512,128]{1,0:T(8,128)(2,1)} %omega_ref.1) | copy-start | bytes 393220
  0.6 4.1 %collective-permute-start = (s32[1,64]{1,0:T(1,128)}, s32[1,64]{1,0:T(1,128)S(1)}, u32[]{:S(2)}, u32[]{:S(2)}) collective-permute-start(s32[1,64]{1,0:T(1,128)} %piece_ref.1), channel_id=1, source_target_pairs={{0,3},{1,2},{2,1},{3,0},{4,7},{5,6},{6,5},{7,4},{8,11},{9,10},{10,... | collective-permute-start | bytes 776 | tf_op jit(solution)/shard_map/ppermute | solution.py:254
  3.1 3.7 %collective-permute-start.1 = (s32[1,64]{1,0:T(1,128)}, s32[1,64]{1,0:T(1,128)S(1)}, u32[]{:S(2)}, u32[]{:S(2)}) collective-permute-start(s32[1,64]{1,0:T(1,128)} %piece_ref.1), channel_id=1, source_target_pairs={{0,2},{1,3},{2,0},{3,1},{4,6},{5,7},{6,4},{7,5},{8,10},{9,11},{10,... | collective-permute-start | bytes 776 | tf_op jit(solution)/shard_map/ppermute | solution.py:254
  3.8 3.1 %collective-permute-start.2 = (s32[1,64]{1,0:T(1,128)}, s32[1,64]{1,0:T(1,128)S(1)}, u32[]{:S(2)}, u32[]{:S(2)}) collective-permute-start(s32[1,64]{1,0:T(1,128)} %piece_ref.1), channel_id=1, source_target_pairs={{0,1},{1,0},{2,3},{3,2},{4,5},{5,4},{6,7},{7,6},{8,9},{9,8},{10,11... | collective-permute-start | bytes 776 | tf_op jit(solution)/shard_map/ppermute | solution.py:254
  6.9 13.7 %collective-permute-start.10 = (bf16[560,128]{1,0:T(8,128)(2,1)S(1)}, bf16[560,128]{1,0:T(8,128)(2,1)S(1)}, u32[]{:S(2)}, u32[]{:S(2)}) collective-permute-start(bf16[560,128]{1,0:T(8,128)(2,1)S(1)} %get-tuple-element.26.msg_ref), channel_id=1, source_target_pairs={{0,12},{4,8},{8,4},{12,0},{16,28},{20,24},{24,20},{28,16},{1,13},{... | collective-permute-start | bytes 430088 | tf_op jit(solution)/shard_map/ppermute | solution.py:254
  9.5 8.0 %collective-permute-start.3 = (bf16[512,128]{1,0:T(8,128)(2,1)S(1)}, bf16[512,128]{1,0:T(8,128)(2,1)S(1)}, u32[]{:S(2)}, u32[]{:S(2)}) collective-permute-start(bf16[512,128]{1,0:T(8,128)(2,1)S(1)} %copy-done), channel_id=1, source_target_pairs={{0,16},{4,20},{8,24},{12,28},{16,0},{20,4},{24,8},{28,12},{1,17},{... | collective-permute-start | bytes 393224 | tf_op jit(solution)/shard_map/ppermute | solution.py:254
  12.1 5.4 %collective-permute-start.4 = (bf16[48,128]{1,0:T(8,128)(2,1)S(1)}, bf16[48,128]{1,0:T(8,128)(2,1)S(1)}, u32[]{:S(2)}, u32[]{:S(2)}) collective-permute-start(bf16[48,128]{1,0:T(8,128)(2,1)S(1)} %get-tuple-element.25.tail_ref), channel_id=1, source_target_pairs={{0,16},{4,20},{8,24},{12,28},{16,0},{20,4},{24,8},{28,12},{1,17},{... | collective-permute-start | bytes 36872 | tf_op jit(solution)/shard_map/ppermute | solution.py:254
  12.4 11.5 %collective-permute-start.9 = (bf16[560,128]{1,0:T(8,128)(2,1)S(1)}, bf16[560,128]{1,0:T(8,128)(2,1)S(1)}, u32[]{:S(2)}, u32[]{:S(2)}) collective-permute-start(bf16[560,128]{1,0:T(8,128)(2,1)S(1)} %get-tuple-element.26.msg_ref), channel_id=1, source_target_pairs={{0,4},{4,0},{8,12},{12,8},{16,20},{20,16},{24,28},{28,24},{1,5},{5... | collective-permute-start | bytes 430088 | tf_op jit(solution)/shard_map/ppermute | solution.py:254
  12.9 11.7 %collective-permute-start.8 = (bf16[560,128]{1,0:T(8,128)(2,1)S(1)}, bf16[560,128]{1,0:T(8,128)(2,1)S(1)}, u32[]{:S(2)}, u32[]{:S(2)}) collective-permute-start(bf16[560,128]{1,0:T(8,128)(2,1)S(1)} %get-tuple-element.26.msg_ref), channel_id=1, source_target_pairs={{0,8},{4,12},{8,0},{12,4},{16,24},{20,28},{24,16},{28,20},{1,9},{5... | collective-permute-start | bytes 430088 | tf_op jit(solution)/shard_map/ppermute | solution.py:254
  17.5 7.8 %collective-permute-start.7 = (bf16[560,128]{1,0:T(8,128)(2,1)S(1)}, bf16[560,128]{1,0:T(8,128)(2,1)S(1)}, u32[]{:S(2)}, u32[]{:S(2)}) collective-permute-start(bf16[560,128]{1,0:T(8,128)(2,1)S(1)} %pack.1.msg_ref), channel_id=1, source_target_pairs={{0,4},{4,0},{8,12},{12,8},{16,20},{20,16},{24,28},{28,24},{1,5},{5... | collective-permute-start | bytes 430088 | tf_op jit(solution)/shard_map/ppermute | solution.py:254
  18.3 7.7 %collective-permute-start.6 = (bf16[560,128]{1,0:T(8,128)(2,1)S(1)}, bf16[560,128]{1,0:T(8,128)(2,1)S(1)}, u32[]{:S(2)}, u32[]{:S(2)}) collective-permute-start(bf16[560,128]{1,0:T(8,128)(2,1)S(1)} %pack.1.msg_ref), channel_id=1, source_target_pairs={{0,8},{4,12},{8,0},{12,4},{16,24},{20,28},{24,16},{28,20},{1,9},{5... | collective-permute-start | bytes 430088 | tf_op jit(solution)/shard_map/ppermute | solution.py:254
  20.6 6.1 %collective-permute-start.5 = (bf16[560,128]{1,0:T(8,128)(2,1)S(1)}, bf16[560,128]{1,0:T(8,128)(2,1)S(1)}, u32[]{:S(2)}, u32[]{:S(2)}) collective-permute-start(bf16[560,128]{1,0:T(8,128)(2,1)S(1)} %pack.1.msg_ref), channel_id=1, source_target_pairs={{0,12},{4,8},{8,4},{12,0},{16,28},{20,24},{24,20},{28,16},{1,13},{... | collective-permute-start | bytes 430088 | tf_op jit(solution)/shard_map/ppermute | solution.py:254

commit v5 on v4

--- a/solution.py
+++ b/solution.py
@@ -125,6 +125,7 @@
             tail = jnp.where(place == spare_row(leaf, index), digit[:, r * LANES : (r + 1) * LANES], tail)
             index += 1
     tail = tail.astype(jnp.bfloat16)
+    msg_ref[0:leaf, :] = msg_in_ref[0:leaf, :]
     msg_ref[leaf:, :] = tail
     tail_ref[...] = tail
 
@@ -138,31 +139,36 @@
         ),
         in_specs=[VMEM] * (1 + len(pieces)),
         out_specs=(VMEM, VMEM),
-        input_output_aliases={0: 0},
         compiler_params=ROOM,
         name="attach",
     )(msg, *pieces)
 
 
-def pack_kernel(block_ref, tail_ref, msg_ref):
+def pack_kernel(list_rows, block_ref, tail_ref, own_ref, msg_ref):
     leaf = block_ref.shape[0]
     msg_ref[0:leaf, :] = block_ref[...]
-    msg_ref[leaf:, :] = tail_ref[...]
-
-
-def pack(block, tail):
+    tail, own = tail_ref[...].astype(jnp.float32), own_ref[...].astype(jnp.float32)
+    place = lax.broadcasted_iota(jnp.int32, tail.shape, 0)
+    for r in range(2 * list_rows):
+        held = spare_row(leaf, r)
+        tail = jnp.where(place == spare_row(leaf, 2 * list_rows + r), own[held : held + 1, :], tail)
+    msg_ref[leaf:, :] = tail.astype(jnp.bfloat16)
+
+
+def pack(list_rows, block, tail, own):
     return pl.pallas_call(
-        pack_kernel,
+        functools.partial(pack_kernel, list_rows),
         out_shape=jax.ShapeDtypeStruct((block.shape[0] + tail.shape[0], LANES), block.dtype),
-        in_specs=[VMEM, VMEM],
+        in_specs=[VMEM] * 3,
         out_specs=VMEM,
         compiler_params=ROOM,
         name="pack",
-    )(block, tail)
-
-
-def listed_in(tail, leaf, list_rows):
-    digits = [tail[spare_row(leaf, r) : spare_row(leaf, r) + 1, :] for r in range(2 * list_rows)]
+    )(block, tail, own)
+
+
+def listed_in(tail, leaf, list_rows, slot=0):
+    places = [spare_row(leaf, 2 * list_rows * slot + r) for r in range(2 * list_rows)]
+    digits = [tail[place : place + 1, :] for place in places]
     return [digits[r] * BASE + digits[list_rows + r] for r in range(list_rows)]
 
 
@@ -190,64 +196,76 @@
     return jnp.concatenate([jnp.broadcast_to(columns[:, k : k + 1], (LANES, LANES)) for k in range(rows)], axis=0)
 
 
-def block_kernel(nodes, list_rows, bits, started, left_ref, tail_ref, msg_ref, *refs):
-    row_ref, col_ref, table_out_ref, right_ref, tile_ref = refs[-5:]
+def block_kernel(nodes, list_rows, bits, started, masked, waiting, *refs):
+    left_ref, tail_ref, msg_ref = refs[:3]
+    right_ref, tile_ref = refs[-2:]
     leaf = left_ref.shape[0]
     chunks = leaf // LANES
     me = lax.axis_index("node")
+    first = (me * chunks).astype(jnp.float32)
     if started:
-        row_in_ref, col_in_ref, table_ref = refs[:3]
+        row_in_ref, col_in_ref, table_ref = refs[3:6]
+        outs = refs[6 + waiting : -2]
     else:
+        outs = refs[3:-2]
         mine = listed_in(tail_ref[...].astype(jnp.float32), leaf, list_rows)
-        table_out_ref[...] = count_table(mine, 0.0, table_out_ref.shape[0])
-        table_ref = table_out_ref
+        table_ref = outs[2]
+        table_ref[...] = count_table(mine, 0.0, table_ref.shape[0])
     tail = msg_ref[leaf:, :].astype(jnp.float32)
     term = term_rows(leaf)
     points = (tail[0:term, :] + tail[term : 2 * term, :]) + tail[2 * term : 3 * term, :]
     groups = factors(centred(points, nodes, me), False)
     for k in range(chunks):
         right_ref[:, k * LANES : (k + 1) * LANES] = chunk_of(groups, k).astype(jnp.bfloat16)
-    step = LANES
-    for p in range(0, leaf, step):
-        squared = jnp.dot(left_ref[p : p + step, :], right_ref[...], preferred_element_type=jnp.float32)
-        tile_ref[p : p + step, :] = lax.rsqrt(squared).astype(jnp.bfloat16)
+    for p in range(0, leaf, LANES):
+        squared = jnp.dot(left_ref[p : p + LANES, :], right_ref[...], preferred_element_type=jnp.float32)
+        tile_ref[p : p + LANES, :] = lax.rsqrt(squared).astype(jnp.bfloat16)
     node = me ^ bits
     near = jnp.where(jnp.abs(node - me) <= 1, 1.0, 0.0)
     samples = msg_ref[0:leaf, :]
     weight = widened(table_ref[pl.ds(node * chunks, chunks), :]) + near
     weighted = weight.astype(jnp.bfloat16) * samples
-    first = (me * chunks).astype(jnp.float32)
-    named = count_table(listed_in(tail, leaf, list_rows), first, -(-chunks // 8) * 8)
-    mask = widened(named[0:chunks, :])
     both = jnp.dot(tile_ref[...], jnp.concatenate([samples, weighted], axis=1), preferred_element_type=jnp.float32)
-    row, col = both[:, LANES:], mask * both[:, :LANES]
+    row, col = both[:, LANES:], both[:, :LANES]
     if started:
-        row, col = row_in_ref[...] + row, col_in_ref[...] + col
-    row_ref[...] = row.astype(row_ref.dtype)
-    col_ref[...] = col
-
-
-def add_block(list_rows, bits, left, tail, msg, totals, row_type=jnp.float32):
+        row = row_in_ref[...] + row
+    outs[0][...] = row.astype(outs[0].dtype)
+    if not masked:
+        outs[1][...] = col
+        return
+    table_rows = -(-chunks // 8) * 8
+    named = count_table(listed_in(tail, leaf, list_rows), first, table_rows)
+    col = widened(named[0:chunks, :]) * col
+    if started:
+        col = col_in_ref[...] + col
+    if waiting:
+        named = count_table(listed_in(tail, leaf, list_rows, 1), first, table_rows)
+        col = col + widened(named[0:chunks, :]) * refs[6][...]
+    outs[1][...] = col
+
+
+def add_block(list_rows, bits, left, tail, msg, totals, masked=True, waiting=(), row_type=jnp.float32):
     leaf = left.shape[0]
     nodes = lax.axis_size("node")
     part = (leaf, LANES)
     outs = [jax.ShapeDtypeStruct(part, row_type), jax.ShapeDtypeStruct(part, jnp.float32)]
-    scratch = [pltpu.VMEM((32, leaf), jnp.bfloat16), pltpu.VMEM((leaf, leaf), jnp.bfloat16)]
-    table_shape = (-(-nodes * (leaf // LANES) // 8) * 8, LANES)
-    if totals:
-        scratch = [pltpu.VMEM((8, LANES), jnp.float32)] + scratch
-    else:
+    if not totals:
+        table_shape = (-(-nodes * (leaf // LANES) // 8) * 8, LANES)
         outs.append(jax.ShapeDtypeStruct(table_shape, jnp.float32))
     result = pl.pallas_call(
-        functools.partial(block_kernel, nodes, list_rows, bits, bool(totals)),
+        functools.partial(block_kernel, nodes, list_rows, bits, bool(totals), masked, len(waiting)),
         out_shape=outs,
-        in_specs=[VMEM] * (3 + len(totals)),
+        in_specs=[VMEM] * (3 + len(totals) + len(waiting)),
         out_specs=[VMEM] * len(outs),
-        scratch_shapes=scratch,
+        scratch_shapes=[pltpu.VMEM((32, leaf), jnp.bfloat16), pltpu.VMEM((leaf, leaf), jnp.bfloat16)],
         compiler_params=ROOM,
         name="add_block",
-    )(left, tail, msg, *totals)
-    return (result[0], result[1], totals[2] if totals else result[2])
+    )(left, tail, msg, *totals, *waiting)
+    if not totals:
+        return tuple(result), None
+    if not masked:
+        return (result[0], totals[1], totals[2]), result[1]
+    return (result[0], result[1], totals[2]), None
 
 
 def swap(block, axis, bits):
@@ -264,24 +282,33 @@
     for bit in reversed(far_bits):
         across += [(bits | bit, swap(block, "node", bit)) for bits, block in across]
     pieces = [swap(skeleton, "rep", bits) for bits in reversed(range(1, reps))]
-    msg, left, own_piece = prep(coords, omega, skeleton)
-    msg, tail = attach(list_rows, msg, [own_piece] + pieces, coords.shape[1])
+    plain, left, own_piece = prep(coords, omega, skeleton)
+    ahead = {step: swap(plain, "node", step) for step in (QUAD[0], QUAD[2])}
+    msg, tail = attach(list_rows, plain, [own_piece] + pieces, coords.shape[1])
     tails = [(0, tail)]
     for bit in reversed(far_bits):
         tails += [(bits | bit, swap(part, "node", bit)) for bits, part in tails]
-    msgs = [swap(msg, "node", step) for step in QUAD]
-    arrived = [(step, msg) for step, msg in zip(QUAD, msgs)]
-    early = [(0, msg)]
-    late = []
+    group = {step: swap(msg, "node", step) for step in QUAD[1:2]}
+    early, late = [], []
     for (bits, block), (_, part) in zip(across[1:], tails[1:]):
-        msg = pack(block, part)
-        late += [(bits | step, swap(msg, "node", step)) for step in QUAD]
-        early.append((bits, msg))
-    totals = ()
-    blocks = early + arrived[2:] + arrived[:2] + late
-    for place, (bits, msg) in enumerate(blocks):
-        row_type = jnp.float32 if place + 1 < len(blocks) else jnp.bfloat16
-        totals = add_block(list_rows, bits, left, tail, msg, totals, row_type)
+        packed = pack(list_rows, block, part, tail)
+        sent = {}
+        for step in (1, 3, 2):
+            sent[step] = swap(packed, "node", step)
+        late += [(bits, step, sent[step]) for step in (1, 3, 2)]
+        early.append((bits, packed, True))
+    early += [(step, block, True) for step, block in group.items()]
+    totals, waiting = (), {}
+    totals, _ = add_block(list_rows, 0, left, tail, msg, totals)
+    for step, block in ahead.items():
+        totals, left_over = add_block(list_rows, step, left, tail, block, totals, False)
+        waiting[step] = (left_over,)
+    for bits, block, masked in early:
+        totals, _ = add_block(list_rows, bits, left, tail, block, totals, masked)
+    for place, (bits, step, block) in enumerate(late):
+        row_type = jnp.float32 if place + 1 < len(late) else jnp.bfloat16
+        extra = waiting.pop(step, ())
+        totals, _ = add_block(list_rows, bits | step, left, tail, block, totals, True, extra, row_type)
     return totals[:2]
 
 

time: 28.2 us -> 28.7 us (1.018)
  Pallas kernels: 7.29 us -> 8.39 us
  waiting for transfers between devices: 6.18 us -> 5.67 us
    pallas_call x8, Pallas kernels: 6.25 us -> 7.29 us  [add_block(): pl.pallas_call(functools.partial(block_kernel, nodes, list_rows, bits, bo...]
    ppermute x11, waiting for transfers between devices: 6.18 us -> 5.67 us  [swap(): lax.ppermute(block, axis, [(i, i ^ bits) for i in range(lax.axis_size(axi...]
  transfers between devices with their start and end apart: 11 -> 11, of which waited for: 2 -> 5; matrix products, arithmetic and copies ran while one was open for 0% -> 0% of each run, Pallas kernels for 21% -> 21%
where the time goes in v5:
time: 28.7 us; the launch traced here: 28.5 us
  starting transfers between devices  13.7 us (48%)
  Pallas kernels  8.39 us (29%)
  waiting for transfers between devices  5.67 us (20%)
  between operations  0.72 us (3%)
    ppermute x11, starting transfers between devices, swap(): lax.ppermute(block, axis, [(i, i ^ bits) for i in range(lax.axis_size(axi...  13.7 us
    pallas_call x8, Pallas kernels, add_block(): pl.pallas_call(functools.partial(block_kernel, nodes, list_rows, bits, bo...  7.29 us
    ppermute x11, waiting for transfers between devices, swap(): lax.ppermute(block, axis, [(i, i ^ bits) for i in range(lax.axis_size(axi...  5.67 us
    pallas_call x1, Pallas kernels, prep(): pl.pallas_call(functools.partial(prep_kernel, lax.axis_size('node')), out...  1 us
  transfers between devices with their start and end apart: 11, of which 5 were waited for; matrix products, arithmetic and copies ran while one was open for 0% of the time, Pallas kernels for 21%

profile of v5, /device:TPU:0, one launch (start us, length us, event | category | flops | bytes accessed | tf_op | source)
XLA Modules:
  0.0 28.5 jit_solution(10437269710338663561)
XLA Ops:
  0.6 0.0 copy-start
  0.6 1.0 %prep.1 = (bf16[560,128]{1,0:T(8,128)(2,1)S(1)}, bf16[512,32]{1,0:T(8,128)(2,1)S(1)}, s32[1,64]{1,0:T(1,128)S(1)}) custom-call(f32[3,512]{1,0:T(4,128)} %coords_ref.1, bf16[512,128]{1,0:T(8,128)(2,1)} %omega_ref.1, s32[1,64]{1,0:T(1,128)} %piece_ref.1), custom_call_target="tpu_custom_call" | custom-call | tf_op jit(solution)/shard_map/prep/pallas_call | solution.py:100
  1.6 0.0 copy-start.1
  1.7 3.1 %collective-permute-start.10 = (bf16[560,128]{1,0:T(8,128)(2,1)S(1)}, bf16[560,128]{1,0:T(8,128)(2,1)S(1)}, u32[]{:S(2)}, u32[]{:S(2)}) collective-permute-start(bf16[560,128]{1,0:T(8,128)(2,1)S(1)} %get-tuple-element.23.msg_in_ref), channel_id=1, source_target_pairs={{0,4},{4,0},{8,12},{12,8},{16,20},{20,16},{24,28},{28,24},{1,5},{5... | collective-permute-start | bytes 430088 | tf_op jit(solution)/shard_map/ppermute | solution.py:272
  4.7 0.0 copy-done
  4.7 2.6 %collective-permute-start.3 = (bf16[512,128]{1,0:T(8,128)(2,1)S(1)}, bf16[512,128]{1,0:T(8,128)(2,1)S(1)}, u32[]{:S(2)}, u32[]{:S(2)}) collective-permute-start(bf16[512,128]{1,0:T(8,128)(2,1)S(1)} %copy-done), channel_id=1, source_target_pairs={{0,16},{4,20},{8,24},{12,28},{16,0},{20,4},{24,8},{28,12},{1,17},{... | collective-permute-start | bytes 393224 | tf_op jit(solution)/shard_map/ppermute | solution.py:272
  7.3 0.0 copy-done.1
  7.3 0.4 %collective-permute-start = (s32[1,64]{1,0:T(1,128)S(1)}, s32[1,64]{1,0:T(1,128)S(1)}, u32[]{:S(2)}, u32[]{:S(2)}) collective-permute-start(s32[1,64]{1,0:T(1,128)S(1)} %copy-done.1), channel_id=1, source_target_pairs={{0,3},{1,2},{2,1},{3,0},{4,7},{5,6},{6,5},{7,4},{8,11},{9,10},{10,... | collective-permute-start | bytes 776 | tf_op jit(solution)/shard_map/ppermute | solution.py:272
  7.7 1.1 %collective-permute-start.1 = (s32[1,64]{1,0:T(1,128)S(1)}, s32[1,64]{1,0:T(1,128)S(1)}, u32[]{:S(2)}, u32[]{:S(2)}) collective-permute-start(s32[1,64]{1,0:T(1,128)S(1)} %copy-done.1), channel_id=1, source_target_pairs={{0,2},{1,3},{2,0},{3,1},{4,6},{5,7},{6,4},{7,5},{8,10},{9,11},{10,... | collective-permute-start | bytes 776 | tf_op jit(solution)/shard_map/ppermute | solution.py:272
  8.8 0.4 %collective-permute-start.2 = (s32[1,64]{1,0:T(1,128)S(1)}, s32[1,64]{1,0:T(1,128)S(1)}, u32[]{:S(2)}, u32[]{:S(2)}) collective-permute-start(s32[1,64]{1,0:T(1,128)S(1)} %copy-done.1), channel_id=1, source_target_pairs={{0,1},{1,0},{2,3},{3,2},{4,5},{5,4},{6,7},{7,6},{8,9},{9,8},{10,11... | collective-permute-start | bytes 776 | tf_op jit(solution)/shard_map/ppermute | solution.py:272
  9.2 1.1 %collective-permute-done.refs_1_ = s32[1,64]{1,0:T(1,128)S(1)} collective-permute-done((s32[1,64]{1,0:T(1,128)S(1)}, s32[1,64]{1,0:T(1,128)S(1)}, u32[]{:S(2)}, u32[]{:S(2)}) %collective-permute-start) | collective-permute-done | bytes 288 | tf_op jit(solution)/shard_map/ppermute | solution.py:272
  10.3 0.9 %collective-permute-done.1.refs_2_ = s32[1,64]{1,0:T(1,128)S(1)} collective-permute-done((s32[1,64]{1,0:T(1,128)S(1)}, s32[1,64]{1,0:T(1,128)S(1)}, u32[]{:S(2)}, u32[]{:S(2)}) %collective-permute-start.1) | collective-permute-done | bytes 288 | tf_op jit(solution)/shard_map/ppermute | solution.py:272
  11.3 0.0 collective-permute-done.2.refs_3_
  11.3 0.1 attach.1
  11.3 0.4 %collective-permute-start.4 = (bf16[48,128]{1,0:T(8,128)(2,1)S(1)}, bf16[48,128]{1,0:T(8,128)(2,1)S(1)}, u32[]{:S(2)}, u32[]{:S(2)}) collective-permute-start(bf16[48,128]{1,0:T(8,128)(2,1)S(1)} %get-tuple-element.25.own_ref.refs_1_), channel_id=1, source_target_pairs={{0,16},{4,20},{8,24},{12,28},{16,0},{20,4},{24,8},{28,12},{1,17},{... | collective-permute-start | bytes 36872 | tf_op jit(solution)/shard_map/ppermute | solution.py:272
  11.8 1.8 %collective-permute-start.9 = (bf16[560,128]{1,0:T(8,128)(2,1)S(1)}, bf16[560,128]{1,0:T(8,128)(2,1)S(1)}, u32[]{:S(2)}, u32[]{:S(2)}) collective-permute-start(bf16[560,128]{1,0:T(8,128)(2,1)S(1)} %get-tuple-element.23.msg_in_ref), channel_id=1, source_target_pairs={{0,12},{4,8},{8,4},{12,0},{16,28},{20,24},{24,20},{28,16},{1,13},{... | collective-permute-start | bytes 430088 | tf_op jit(solution)/shard_map/ppermute | solution.py:272
  13.6 0.4 %collective-permute-start.8 = (bf16[560,128]{1,0:T(8,128)(2,1)S(1)}, bf16[560,128]{1,0:T(8,128)(2,1)S(1)}, u32[]{:S(2)}, u32[]{:S(2)}) collective-permute-start(bf16[560,128]{1,0:T(8,128)(2,1)S(1)} %get-tuple-element.26.refs_2_), channel_id=1, source_target_pairs={{0,8},{4,12},{8,0},{12,4},{16,24},{20,28},{24,16},{28,20},{1,9},{5... | collective-permute-start | bytes 430088 | tf_op jit(solution)/shard_map/ppermute | solution.py:272
  14.0 2.1 %collective-permute-done.4.tail_ref = bf16[48,128]{1,0:T(8,128)(2,1)S(1)} collective-permute-done((bf16[48,128]{1,0:T(8,128)(2,1)S(1)}, bf16[48,128]{1,0:T(8,128)(2,1)S(1)}, u32[]{:S(2)}, u32[]{:S(2)}) %collective-permute-start.4) | collective-permute-done | bytes 12320 | tf_op jit(solution)/shard_map/ppermute | solution.py:272
  16.1 0.0 collective-permute-done.3.block_ref
  16.1 0.6 %collective-permute-start.7 = (bf16[560,128]{1,0:T(8,128)(2,1)S(1)}, bf16[560,128]{1,0:T(8,128)(2,1)S(1)}, u32[]{:S(2)}, u32[]{:S(2)}) collective-permute-start(bf16[560,128]{1,0:T(8,128)(2,1)S(1)} %pack.1.refs_2_), channel_id=1, source_target_pairs={{0,4},{4,0},{8,12},{12,8},{16,20},{20,16},{24,28},{28,24},{1,5},{5... | collective-permute-start | bytes 430088 | tf_op jit(solution)/shard_map/ppermute | solution.py:272
  16.7 2.6 %collective-permute-start.6 = (bf16[560,128]{1,0:T(8,128)(2,1)S(1)}, bf16[560,128]{1,0:T(8,128)(2,1)S(1)}, u32[]{:S(2)}, u32[]{:S(2)}) collective-permute-start(bf16[560,128]{1,0:T(8,128)(2,1)S(1)} %pack.1.refs_2_), channel_id=1, source_target_pairs={{0,12},{4,8},{8,4},{12,0},{16,28},{20,24},{24,20},{28,16},{1,13},{... | collective-permute-start | bytes 430088 | tf_op jit(solution)/shard_map/ppermute | solution.py:272
  19.3 0.0 collective-permute-done.10.refs_2_
  19.3 0.4 %collective-permute-start.5 = (bf16[560,128]{1,0:T(8,128)(2,1)S(1)}, bf16[560,128]{1,0:T(8,128)(2,1)S(1)}, u32[]{:S(2)}, u32[]{:S(2)}) collective-permute-start(bf16[560,128]{1,0:T(8,128)(2,1)S(1)} %pack.1.refs_2_), channel_id=1, source_target_pairs={{0,8},{4,12},{8,0},{12,4},{16,24},{20,28},{24,16},{28,20},{1,9},{5... | collective-permute-start | bytes 430088 | tf_op jit(solution)/shard_map/ppermute | solution.py:272
  19.7 1.0 %add_block.8 = (f32[512,128]{1,0:T(8,128)S(1)}, f32[512,128]{1,0:T(8,128)S(1)}, f32[32,128]{1,0:T(8,128)S(1)}) custom-call(bf16[512,32]{1,0:T(8,128)(2,1)S(1)} %get-tuple-element.22.refs_0_, bf16[48,128]{1,0:T(8,128)(2,1)S(1)} %get-tuple-element.25.own_ref.refs_1_, bf16[560,128]{1,0:T(8,128)(2,1)S(1)} %get-tuple-element.26.refs_2_), custom_call_target="tpu_custom_call" | custom-call | tf_op jit(solution)/shard_map/add_block/pallas_call | solution.py:255
  20.7 0.6 %add_block.9 = (f32[512,128]{1,0:T(8,128)S(1)}, f32[512,128]{1,0:T(8,128)S(1)}) custom-call(bf16[512,32]{1,0:T(8,128)(2,1)S(1)} %get-tuple-element.22.refs_0_, bf16[48,128]{1,0:T(8,128)(2,1)S(1)} %get-tuple-element.25.own_ref.refs_1_, bf16[560,128]{1,0:T(8,128)(2,1)S(1)} %collective-permute-done.10.refs_2_, f32[512,128]{1,0:T(8,128)S(1)} %get-tuple-element.27.refs_3_, ...), custom_call_target="tpu_custom_call" | custom-call | tf_op jit(solution)/shard_map/add_block/pallas_call | solution.py:255
  21.3 0.0 collective-permute-done.9.refs_2_
  21.3 0.6 %add_block.10 = (f32[512,128]{1,0:T(8,128)S(1)}, f32[512,128]{1,0:T(8,128)S(1)}) custom-call(bf16[512,32]{1,0:T(8,128)(2,1)S(1)} %get-tuple-element.22.refs_0_, bf16[48,128]{1,0:T(8,128)(2,1)S(1)} %get-tuple-element.25.own_ref.refs_1_, bf16[560,128]{1,0:T(8,128)(2,1)S(1)} %collective-permute-done.9.refs_2_, f32[512,128]{1,0:T(8,128)S(1)} %get-tuple-element.30.refs_3_, ...), custom_call_target="tpu_custom_call" | custom-call | tf_op jit(solution)/shard_map/add_block/pallas_call | solution.py:255
  21.9 0.8 %add_block.11 = (f32[512,128]{1,0:T(8,128)S(1)}, f32[512,128]{1,0:T(8,128)S(1)}) custom-call(bf16[512,32]{1,0:T(8,128)(2,1)S(1)} %get-tuple-element.22.refs_0_, bf16[48,128]{1,0:T(8,128)(2,1)S(1)} %get-tuple-element.25.own_ref.refs_1_, bf16[560,128]{1,0:T(8,128)(2,1)S(1)} %pack.1.refs_2_, f32[512,128]{1,0:T(8,128)S(1)} %get-tuple-element.31.refs_3_, ...), custom_call_target="tpu_custom_call" | custom-call | tf_op jit(solution)/shard_map/add_block/pallas_call | solution.py:255
  22.7 0.0 collective-permute-done.8.refs_2_
  22.7 0.8 %add_block.12 = (f32[512,128]{1,0:T(8,128)S(1)}, f32[512,128]{1,0:T(8,128)S(1)}) custom-call(bf16[512,32]{1,0:T(8,128)(2,1)S(1)} %get-tuple-element.22.refs_0_, bf16[48,128]{1,0:T(8,128)(2,1)S(1)} %get-tuple-element.25.own_ref.refs_1_, bf16[560,128]{1,0:T(8,128)(2,1)S(1)} %collective-permute-done.8.refs_2_, f32[512,128]{1,0:T(8,128)S(1)} %get-tuple-element.32.refs_3_, ...), custom_call_target="tpu_custom_call" | custom-call | tf_op jit(solution)/shard_map/add_block/pallas_call | solution.py:255
  23.5 0.0 collective-permute-done.7.refs_2_
  23.5 1.0 %add_block.13 = (f32[512,128]{1,0:T(8,128)S(1)}, f32[512,128]{1,0:T(8,128)S(1)}) custom-call(bf16[512,32]{1,0:T(8,128)(2,1)S(1)} %get-tuple-element.22.refs_0_, bf16[48,128]{1,0:T(8,128)(2,1)S(1)} %get-tuple-element.25.own_ref.refs_1_, bf16[560,128]{1,0:T(8,128)(2,1)S(1)} %collective-permute-done.7.refs_2_, f32[512,128]{1,0:T(8,128)S(1)} %get-tuple-element.34.refs_3_, ...), custom_call_target="tpu_custom_call" | custom-call | tf_op jit(solution)/shard_map/add_block/pallas_call | solution.py:255
  24.5 0.9 %collective-permute-done.6.refs_2_ = bf16[560,128]{1,0:T(8,128)(2,1)S(1)} collective-permute-done((bf16[560,128]{1,0:T(8,128)(2,1)S(1)}, bf16[560,128]{1,0:T(8,128)(2,1)S(1)}, u32[]{:S(2)}, u32[]{:S(2)}) %collective-permute-start.6) | collective-permute-done | bytes 143392 | tf_op jit(solution)/shard_map/ppermute | solution.py:272
  25.4 1.0 %add_block.14 = (f32[512,128]{1,0:T(8,128)S(1)}, f32[512,128]{1,0:T(8,128)S(1)}) custom-call(bf16[512,32]{1,0:T(8,128)(2,1)S(1)} %get-tuple-element.22.refs_0_, bf16[48,128]{1,0:T(8,128)(2,1)S(1)} %get-tuple-element.25.own_ref.refs_1_, bf16[560,128]{1,0:T(8,128)(2,1)S(1)} %collective-permute-done.6.refs_2_, f32[512,128]{1,0:T(8,128)S(1)} %get-tuple-element.37.refs_3_, ...), custom_call_target="tpu_custom_call" | custom-call | tf_op jit(solution)/shard_map/add_block/pallas_call | solution.py:255
  26.4 0.6 %collective-permute-done.5.refs_2_ = bf16[560,128]{1,0:T(8,128)(2,1)S(1)} collective-permute-done((bf16[560,128]{1,0:T(8,128)(2,1)S(1)}, bf16[560,128]{1,0:T(8,128)(2,1)S(1)}, u32[]{:S(2)}, u32[]{:S(2)}) %collective-permute-start.5) | collective-permute-done | bytes 143392 | tf_op jit(solution)/shard_map/ppermute | solution.py:272
  27.0 1.5 %add_block.15 = (bf16[512,128]{1,0:T(8,128)(2,1)}, f32[512,128]{1,0:T(8,128)}) custom-call(bf16[512,32]{1,0:T(8,128)(2,1)S(1)} %get-tuple-element.22.refs_0_, bf16[48,128]{1,0:T(8,128)(2,1)S(1)} %get-tuple-element.25.own_ref.refs_1_, bf16[560,128]{1,0:T(8,128)(2,1)S(1)} %collective-permute-done.5.refs_2_, f32[512,128]{1,0:T(8,128)S(1)} %get-tuple-element.40.refs_3_, ...), custom_call_target="tpu_custom_call" | custom-call | tf_op jit(solution)/shard_map/add_block/pallas_call | solution.py:255
  (1 shorter events, 0.0 us)
Async XLA Ops:
  0.6 4.1 %copy-start = (bf16[512,128]{1,0:T(8,128)(2,1)S(1)}, bf16[512,128]{1,0:T(8,128)(2,1)}, u32[]{:S(2)}) copy-start(bf16[512,128]{1,0:T(8,128)(2,1)} %omega_ref.1) | copy-start | bytes 393220
  1.6 5.7 %copy-start.1 = (s32[1,64]{1,0:T(1,128)S(1)}, s32[1,64]{1,0:T(1,128)}, u32[]{:S(2)}) copy-start(s32[1,64]{1,0:T(1,128)} %piece_ref.1) | copy-start | bytes 772
  1.7 17.6 %collective-permute-start.10 = (bf16[560,128]{1,0:T(8,128)(2,1)S(1)}, bf16[560,128]{1,0:T(8,128)(2,1)S(1)}, u32[]{:S(2)}, u32[]{:S(2)}) collective-permute-start(bf16[560,128]{1,0:T(8,128)(2,1)S(1)} %get-tuple-element.23.msg_in_ref), channel_id=1, source_target_pairs={{0,4},{4,0},{8,12},{12,8},{16,20},{20,16},{24,28},{28,24},{1,5},{5... | collective-permute-start | bytes 430088 | tf_op jit(solution)/shard_map/ppermute | solution.py:272
  4.7 11.4 %collective-permute-start.3 = (bf16[512,128]{1,0:T(8,128)(2,1)S(1)}, bf16[512,128]{1,0:T(8,128)(2,1)S(1)}, u32[]{:S(2)}, u32[]{:S(2)}) collective-permute-start(bf16[512,128]{1,0:T(8,128)(2,1)S(1)} %copy-done), channel_id=1, source_target_pairs={{0,16},{4,20},{8,24},{12,28},{16,0},{20,4},{24,8},{28,12},{1,17},{... | collective-permute-start | bytes 393224 | tf_op jit(solution)/shard_map/ppermute | solution.py:272
  7.3 3.0 %collective-permute-start = (s32[1,64]{1,0:T(1,128)S(1)}, s32[1,64]{1,0:T(1,128)S(1)}, u32[]{:S(2)}, u32[]{:S(2)}) collective-permute-start(s32[1,64]{1,0:T(1,128)S(1)} %copy-done.1), channel_id=1, source_target_pairs={{0,3},{1,2},{2,1},{3,0},{4,7},{5,6},{6,5},{7,4},{8,11},{9,10},{10,... | collective-permute-start | bytes 776 | tf_op jit(solution)/shard_map/ppermute | solution.py:272
  7.7 3.6 %collective-permute-start.1 = (s32[1,64]{1,0:T(1,128)S(1)}, s32[1,64]{1,0:T(1,128)S(1)}, u32[]{:S(2)}, u32[]{:S(2)}) collective-permute-start(s32[1,64]{1,0:T(1,128)S(1)} %copy-done.1), channel_id=1, source_target_pairs={{0,2},{1,3},{2,0},{3,1},{4,6},{5,7},{6,4},{7,5},{8,10},{9,11},{10,... | collective-permute-start | bytes 776 | tf_op jit(solution)/shard_map/ppermute | solution.py:272
  8.8 2.4 %collective-permute-start.2 = (s32[1,64]{1,0:T(1,128)S(1)}, s32[1,64]{1,0:T(1,128)S(1)}, u32[]{:S(2)}, u32[]{:S(2)}) collective-permute-start(s32[1,64]{1,0:T(1,128)S(1)} %copy-done.1), channel_id=1, source_target_pairs={{0,1},{1,0},{2,3},{3,2},{4,5},{5,4},{6,7},{7,6},{8,9},{9,8},{10,11... | collective-permute-start | bytes 776 | tf_op jit(solution)/shard_map/ppermute | solution.py:272
  11.3 4.8 %collective-permute-start.4 = (bf16[48,128]{1,0:T(8,128)(2,1)S(1)}, bf16[48,128]{1,0:T(8,128)(2,1)S(1)}, u32[]{:S(2)}, u32[]{:S(2)}) collective-permute-start(bf16[48,128]{1,0:T(8,128)(2,1)S(1)} %get-tuple-element.25.own_ref.refs_1_), channel_id=1, source_target_pairs={{0,16},{4,20},{8,24},{12,28},{16,0},{20,4},{24,8},{28,12},{1,17},{... | collective-permute-start | bytes 36872 | tf_op jit(solution)/shard_map/ppermute | solution.py:272
  11.8 9.5 %collective-permute-start.9 = (bf16[560,128]{1,0:T(8,128)(2,1)S(1)}, bf16[560,128]{1,0:T(8,128)(2,1)S(1)}, u32[]{:S(2)}, u32[]{:S(2)}) collective-permute-start(bf16[560,128]{1,0:T(8,128)(2,1)S(1)} %get-tuple-element.23.msg_in_ref), channel_id=1, source_target_pairs={{0,12},{4,8},{8,4},{12,0},{16,28},{20,24},{24,20},{28,16},{1,13},{... | collective-permute-start | bytes 430088 | tf_op jit(solution)/shard_map/ppermute | solution.py:272
  13.6 9.2 %collective-permute-start.8 = (bf16[560,128]{1,0:T(8,128)(2,1)S(1)}, bf16[560,128]{1,0:T(8,128)(2,1)S(1)}, u32[]{:S(2)}, u32[]{:S(2)}) collective-permute-start(bf16[560,128]{1,0:T(8,128)(2,1)S(1)} %get-tuple-element.26.refs_2_), channel_id=1, source_target_pairs={{0,8},{4,12},{8,0},{12,4},{16,24},{20,28},{24,16},{28,20},{1,9},{5... | collective-permute-start | bytes 430088 | tf_op jit(solution)/shard_map/ppermute | solution.py:272
  16.1 7.4 %collective-permute-start.7 = (bf16[560,128]{1,0:T(8,128)(2,1)S(1)}, bf16[560,128]{1,0:T(8,128)(2,1)S(1)}, u32[]{:S(2)}, u32[]{:S(2)}) collective-permute-start(bf16[560,128]{1,0:T(8,128)(2,1)S(1)} %pack.1.refs_2_), channel_id=1, source_target_pairs={{0,4},{4,0},{8,12},{12,8},{16,20},{20,16},{24,28},{28,24},{1,5},{5... | collective-permute-start | bytes 430088 | tf_op jit(solution)/shard_map/ppermute | solution.py:272
  16.7 8.7 %collective-permute-start.6 = (bf16[560,128]{1,0:T(8,128)(2,1)S(1)}, bf16[560,128]{1,0:T(8,128)(2,1)S(1)}, u32[]{:S(2)}, u32[]{:S(2)}) collective-permute-start(bf16[560,128]{1,0:T(8,128)(2,1)S(1)} %pack.1.refs_2_), channel_id=1, source_target_pairs={{0,12},{4,8},{8,4},{12,0},{16,28},{20,24},{24,20},{28,16},{1,13},{... | collective-permute-start | bytes 430088 | tf_op jit(solution)/shard_map/ppermute | solution.py:272
  19.3 7.7 %collective-permute-start.5 = (bf16[560,128]{1,0:T(8,128)(2,1)S(1)}, bf16[560,128]{1,0:T(8,128)(2,1)S(1)}, u32[]{:S(2)}, u32[]{:S(2)}) collective-permute-start(bf16[560,128]{1,0:T(8,128)(2,1)S(1)} %pack.1.refs_2_), channel_id=1, source_target_pairs={{0,8},{4,12},{8,0},{12,4},{16,24},{20,28},{24,16},{28,20},{1,9},{5... | collective-permute-start | bytes 430088 | tf_op jit(solution)/shard_map/ppermute | solution.py:272

commit v6 on v5

--- a/solution.py
+++ b/solution.py
@@ -19,6 +19,7 @@
 
 VMEM = pl.BlockSpec(memory_space=pltpu.VMEM)
 ROOM = pltpu.CompilerParams(vmem_limit_bytes=16 * 1024 * 1024)
+FAST = pltpu.CompilerParams(vmem_limit_bytes=16 * 1024 * 1024)
 
 
 def term_rows(leaf):
@@ -217,9 +218,9 @@
     groups = factors(centred(points, nodes, me), False)
     for k in range(chunks):
         right_ref[:, k * LANES : (k + 1) * LANES] = chunk_of(groups, k).astype(jnp.bfloat16)
-    for p in range(0, leaf, LANES):
-        squared = jnp.dot(left_ref[p : p + LANES, :], right_ref[...], preferred_element_type=jnp.float32)
-        tile_ref[p : p + LANES, :] = lax.rsqrt(squared).astype(jnp.bfloat16)
+    for p in range(0, leaf, 2 * LANES):
+        squared = jnp.dot(left_ref[...], right_ref[:, p : p + 2 * LANES], preferred_element_type=jnp.float32)
+        tile_ref[:, p : p + 2 * LANES] = lax.rsqrt(squared).astype(jnp.bfloat16)
     node = me ^ bits
     near = jnp.where(jnp.abs(node - me) <= 1, 1.0, 0.0)
     samples = msg_ref[0:leaf, :]
@@ -258,7 +259,7 @@
         in_specs=[VMEM] * (3 + len(totals) + len(waiting)),
         out_specs=[VMEM] * len(outs),
         scratch_shapes=[pltpu.VMEM((32, leaf), jnp.bfloat16), pltpu.VMEM((leaf, leaf), jnp.bfloat16)],
-        compiler_params=ROOM,
+        compiler_params=FAST,
         name="add_block",
     )(left, tail, msg, *totals, *waiting)
     if not totals:

time: 28.7 us -> 28.7 us (level)
  transfers between devices with their start and end apart: 11 -> 11, of which waited for: 5 -> 5; matrix products, arithmetic and copies ran while one was open for 0% -> 0% of each run, Pallas kernels for 21% -> 20%
where the time goes in v6:
time: 28.7 us; the launch traced here: 28.5 us
  starting transfers between devices  13.7 us (48%)
  Pallas kernels  8.11 us (28%)
  waiting for transfers between devices  5.95 us (21%)
  between operations  0.72 us (3%)
    ppermute x11, starting transfers between devices, swap(): lax.ppermute(block, axis, [(i, i ^ bits) for i in range(lax.axis_size(axi...  13.7 us
    pallas_call x8, Pallas kernels, add_block(): pl.pallas_call(functools.partial(block_kernel, nodes, list_rows, bits, bo...  7.02 us
    ppermute x11, waiting for transfers between devices, swap(): lax.ppermute(block, axis, [(i, i ^ bits) for i in range(lax.axis_size(axi...  5.95 us
    pallas_call x1, Pallas kernels, prep(): pl.pallas_call(functools.partial(prep_kernel, lax.axis_size('node')), out...  1 us
  transfers between devices with their start and end apart: 11, of which 5 were waited for; matrix products, arithmetic and copies ran while one was open for 0% of the time, Pallas kernels for 20%

profile of v6, /device:TPU:0, one launch (start us, length us, event | category | flops | bytes accessed | tf_op | source)
XLA Modules:
  0.0 28.5 jit_solution(9700447227611151177)
XLA Ops:
  0.6 0.0 copy-start
  0.6 1.0 %prep.1 = (bf16[560,128]{1,0:T(8,128)(2,1)S(1)}, bf16[512,32]{1,0:T(8,128)(2,1)S(1)}, s32[1,64]{1,0:T(1,128)S(1)}) custom-call(f32[3,512]{1,0:T(4,128)} %coords_ref.1, bf16[512,128]{1,0:T(8,128)(2,1)} %omega_ref.1, s32[1,64]{1,0:T(1,128)} %piece_ref.1), custom_call_target="tpu_custom_call" | custom-call | tf_op jit(solution)/shard_map/prep/pallas_call | solution.py:101
  1.6 0.0 copy-start.1
  1.7 3.1 %collective-permute-start.10 = (bf16[560,128]{1,0:T(8,128)(2,1)S(1)}, bf16[560,128]{1,0:T(8,128)(2,1)S(1)}, u32[]{:S(2)}, u32[]{:S(2)}) collective-permute-start(bf16[560,128]{1,0:T(8,128)(2,1)S(1)} %get-tuple-element.23.msg_in_ref), channel_id=1, source_target_pairs={{0,4},{4,0},{8,12},{12,8},{16,20},{20,16},{24,28},{28,24},{1,5},{5... | collective-permute-start | bytes 430088 | tf_op jit(solution)/shard_map/ppermute | solution.py:273
  4.7 0.0 copy-done
  4.7 2.6 %collective-permute-start.3 = (bf16[512,128]{1,0:T(8,128)(2,1)S(1)}, bf16[512,128]{1,0:T(8,128)(2,1)S(1)}, u32[]{:S(2)}, u32[]{:S(2)}) collective-permute-start(bf16[512,128]{1,0:T(8,128)(2,1)S(1)} %copy-done), channel_id=1, source_target_pairs={{0,16},{4,20},{8,24},{12,28},{16,0},{20,4},{24,8},{28,12},{1,17},{... | collective-permute-start | bytes 393224 | tf_op jit(solution)/shard_map/ppermute | solution.py:273
  7.3 0.0 copy-done.1
  7.3 0.4 %collective-permute-start = (s32[1,64]{1,0:T(1,128)S(1)}, s32[1,64]{1,0:T(1,128)S(1)}, u32[]{:S(2)}, u32[]{:S(2)}) collective-permute-start(s32[1,64]{1,0:T(1,128)S(1)} %copy-done.1), channel_id=1, source_target_pairs={{0,3},{1,2},{2,1},{3,0},{4,7},{5,6},{6,5},{7,4},{8,11},{9,10},{10,... | collective-permute-start | bytes 776 | tf_op jit(solution)/shard_map/ppermute | solution.py:273
  7.7 1.1 %collective-permute-start.1 = (s32[1,64]{1,0:T(1,128)S(1)}, s32[1,64]{1,0:T(1,128)S(1)}, u32[]{:S(2)}, u32[]{:S(2)}) collective-permute-start(s32[1,64]{1,0:T(1,128)S(1)} %copy-done.1), channel_id=1, source_target_pairs={{0,2},{1,3},{2,0},{3,1},{4,6},{5,7},{6,4},{7,5},{8,10},{9,11},{10,... | collective-permute-start | bytes 776 | tf_op jit(solution)/shard_map/ppermute | solution.py:273
  8.8 0.4 %collective-permute-start.2 = (s32[1,64]{1,0:T(1,128)S(1)}, s32[1,64]{1,0:T(1,128)S(1)}, u32[]{:S(2)}, u32[]{:S(2)}) collective-permute-start(s32[1,64]{1,0:T(1,128)S(1)} %copy-done.1), channel_id=1, source_target_pairs={{0,1},{1,0},{2,3},{3,2},{4,5},{5,4},{6,7},{7,6},{8,9},{9,8},{10,11... | collective-permute-start | bytes 776 | tf_op jit(solution)/shard_map/ppermute | solution.py:273
  9.2 1.1 %collective-permute-done.refs_1_ = s32[1,64]{1,0:T(1,128)S(1)} collective-permute-done((s32[1,64]{1,0:T(1,128)S(1)}, s32[1,64]{1,0:T(1,128)S(1)}, u32[]{:S(2)}, u32[]{:S(2)}) %collective-permute-start) | collective-permute-done | bytes 288 | tf_op jit(solution)/shard_map/ppermute | solution.py:273
  10.3 0.9 %collective-permute-done.1.refs_2_ = s32[1,64]{1,0:T(1,128)S(1)} collective-permute-done((s32[1,64]{1,0:T(1,128)S(1)}, s32[1,64]{1,0:T(1,128)S(1)}, u32[]{:S(2)}, u32[]{:S(2)}) %collective-permute-start.1) | collective-permute-done | bytes 288 | tf_op jit(solution)/shard_map/ppermute | solution.py:273
  11.3 0.0 collective-permute-done.2.refs_3_
  11.3 0.1 attach.1
  11.3 0.4 %collective-permute-start.4 = (bf16[48,128]{1,0:T(8,128)(2,1)S(1)}, bf16[48,128]{1,0:T(8,128)(2,1)S(1)}, u32[]{:S(2)}, u32[]{:S(2)}) collective-permute-start(bf16[48,128]{1,0:T(8,128)(2,1)S(1)} %get-tuple-element.25.own_ref.refs_1_), channel_id=1, source_target_pairs={{0,16},{4,20},{8,24},{12,28},{16,0},{20,4},{24,8},{28,12},{1,17},{... | collective-permute-start | bytes 36872 | tf_op jit(solution)/shard_map/ppermute | solution.py:273
  11.8 1.8 %collective-permute-start.9 = (bf16[560,128]{1,0:T(8,128)(2,1)S(1)}, bf16[560,128]{1,0:T(8,128)(2,1)S(1)}, u32[]{:S(2)}, u32[]{:S(2)}) collective-permute-start(bf16[560,128]{1,0:T(8,128)(2,1)S(1)} %get-tuple-element.23.msg_in_ref), channel_id=1, source_target_pairs={{0,12},{4,8},{8,4},{12,0},{16,28},{20,24},{24,20},{28,16},{1,13},{... | collective-permute-start | bytes 430088 | tf_op jit(solution)/shard_map/ppermute | solution.py:273
  13.6 0.4 %collective-permute-start.8 = (bf16[560,128]{1,0:T(8,128)(2,1)S(1)}, bf16[560,128]{1,0:T(8,128)(2,1)S(1)}, u32[]{:S(2)}, u32[]{:S(2)}) collective-permute-start(bf16[560,128]{1,0:T(8,128)(2,1)S(1)} %get-tuple-element.26.refs_2_), channel_id=1, source_target_pairs={{0,8},{4,12},{8,0},{12,4},{16,24},{20,28},{24,16},{28,20},{1,9},{5... | collective-permute-start | bytes 430088 | tf_op jit(solution)/shard_map/ppermute | solution.py:273
  14.0 2.1 %collective-permute-done.4.tail_ref = bf16[48,128]{1,0:T(8,128)(2,1)S(1)} collective-permute-done((bf16[48,128]{1,0:T(8,128)(2,1)S(1)}, bf16[48,128]{1,0:T(8,128)(2,1)S(1)}, u32[]{:S(2)}, u32[]{:S(2)}) %collective-permute-start.4) | collective-permute-done | bytes 12320 | tf_op jit(solution)/shard_map/ppermute | solution.py:273
  16.1 0.0 collective-permute-done.3.block_ref
  16.1 0.6 %collective-permute-start.7 = (bf16[560,128]{1,0:T(8,128)(2,1)S(1)}, bf16[560,128]{1,0:T(8,128)(2,1)S(1)}, u32[]{:S(2)}, u32[]{:S(2)}) collective-permute-start(bf16[560,128]{1,0:T(8,128)(2,1)S(1)} %pack.1.refs_2_), channel_id=1, source_target_pairs={{0,4},{4,0},{8,12},{12,8},{16,20},{20,16},{24,28},{28,24},{1,5},{5... | collective-permute-start | bytes 430088 | tf_op jit(solution)/shard_map/ppermute | solution.py:273
  16.7 2.6 %collective-permute-start.6 = (bf16[560,128]{1,0:T(8,128)(2,1)S(1)}, bf16[560,128]{1,0:T(8,128)(2,1)S(1)}, u32[]{:S(2)}, u32[]{:S(2)}) collective-permute-start(bf16[560,128]{1,0:T(8,128)(2,1)S(1)} %pack.1.refs_2_), channel_id=1, source_target_pairs={{0,12},{4,8},{8,4},{12,0},{16,28},{20,24},{24,20},{28,16},{1,13},{... | collective-permute-start | bytes 430088 | tf_op jit(solution)/shard_map/ppermute | solution.py:273
  19.3 0.0 collective-permute-done.10.refs_2_
  19.3 0.4 %collective-permute-start.5 = (bf16[560,128]{1,0:T(8,128)(2,1)S(1)}, bf16[560,128]{1,0:T(8,128)(2,1)S(1)}, u32[]{:S(2)}, u32[]{:S(2)}) collective-permute-start(bf16[560,128]{1,0:T(8,128)(2,1)S(1)} %pack.1.refs_2_), channel_id=1, source_target_pairs={{0,8},{4,12},{8,0},{12,4},{16,24},{20,28},{24,16},{28,20},{1,9},{5... | collective-permute-start | bytes 430088 | tf_op jit(solution)/shard_map/ppermute | solution.py:273
  19.7 0.9 %add_block.8 = (f32[512,128]{1,0:T(8,128)S(1)}, f32[512,128]{1,0:T(8,128)S(1)}, f32[32,128]{1,0:T(8,128)S(1)}) custom-call(bf16[512,32]{1,0:T(8,128)(2,1)S(1)} %get-tuple-element.22.refs_0_, bf16[48,128]{1,0:T(8,128)(2,1)S(1)} %get-tuple-element.25.own_ref.refs_1_, bf16[560,128]{1,0:T(8,128)(2,1)S(1)} %get-tuple-element.26.refs_2_), custom_call_target="tpu_custom_call" | custom-call | tf_op jit(solution)/shard_map/add_block/pallas_call | solution.py:256
  20.6 0.6 %add_block.9 = (f32[512,128]{1,0:T(8,128)S(1)}, f32[512,128]{1,0:T(8,128)S(1)}) custom-call(bf16[512,32]{1,0:T(8,128)(2,1)S(1)} %get-tuple-element.22.refs_0_, bf16[48,128]{1,0:T(8,128)(2,1)S(1)} %get-tuple-element.25.own_ref.refs_1_, bf16[560,128]{1,0:T(8,128)(2,1)S(1)} %collective-permute-done.10.refs_2_, f32[512,128]{1,0:T(8,128)S(1)} %get-tuple-element.27.refs_3_, ...), custom_call_target="tpu_custom_call" | custom-call | tf_op jit(solution)/shard_map/add_block/pallas_call | solution.py:256
  21.2 0.0 collective-permute-done.9.refs_2_
  21.2 0.6 %add_block.10 = (f32[512,128]{1,0:T(8,128)S(1)}, f32[512,128]{1,0:T(8,128)S(1)}) custom-call(bf16[512,32]{1,0:T(8,128)(2,1)S(1)} %get-tuple-element.22.refs_0_, bf16[48,128]{1,0:T(8,128)(2,1)S(1)} %get-tuple-element.25.own_ref.refs_1_, bf16[560,128]{1,0:T(8,128)(2,1)S(1)} %collective-permute-done.9.refs_2_, f32[512,128]{1,0:T(8,128)S(1)} %get-tuple-element.30.refs_3_, ...), custom_call_target="tpu_custom_call" | custom-call | tf_op jit(solution)/shard_map/add_block/pallas_call | solution.py:256
  21.8 0.8 %add_block.11 = (f32[512,128]{1,0:T(8,128)S(1)}, f32[512,128]{1,0:T(8,128)S(1)}) custom-call(bf16[512,32]{1,0:T(8,128)(2,1)S(1)} %get-tuple-element.22.refs_0_, bf16[48,128]{1,0:T(8,128)(2,1)S(1)} %get-tuple-element.25.own_ref.refs_1_, bf16[560,128]{1,0:T(8,128)(2,1)S(1)} %pack.1.refs_2_, f32[512,128]{1,0:T(8,128)S(1)} %get-tuple-element.31.refs_3_, ...), custom_call_target="tpu_custom_call" | custom-call | tf_op jit(solution)/shard_map/add_block/pallas_call | solution.py:256
  22.6 0.0 collective-permute-done.8.refs_2_
  22.6 0.8 %add_block.12 = (f32[512,128]{1,0:T(8,128)S(1)}, f32[512,128]{1,0:T(8,128)S(1)}) custom-call(bf16[512,32]{1,0:T(8,128)(2,1)S(1)} %get-tuple-element.22.refs_0_, bf16[48,128]{1,0:T(8,128)(2,1)S(1)} %get-tuple-element.25.own_ref.refs_1_, bf16[560,128]{1,0:T(8,128)(2,1)S(1)} %collective-permute-done.8.refs_2_, f32[512,128]{1,0:T(8,128)S(1)} %get-tuple-element.32.refs_3_, ...), custom_call_target="tpu_custom_call" | custom-call | tf_op jit(solution)/shard_map/add_block/pallas_call | solution.py:256
  23.4 0.0 collective-permute-done.7.refs_2_
  23.4 0.9 %add_block.13 = (f32[512,128]{1,0:T(8,128)S(1)}, f32[512,128]{1,0:T(8,128)S(1)}) custom-call(bf16[512,32]{1,0:T(8,128)(2,1)S(1)} %get-tuple-element.22.refs_0_, bf16[48,128]{1,0:T(8,128)(2,1)S(1)} %get-tuple-element.25.own_ref.refs_1_, bf16[560,128]{1,0:T(8,128)(2,1)S(1)} %collective-permute-done.7.refs_2_, f32[512,128]{1,0:T(8,128)S(1)} %get-tuple-element.34.refs_3_, ...), custom_call_target="tpu_custom_call" | custom-call | tf_op jit(solution)/shard_map/add_block/pallas_call | solution.py:256
  24.3 1.1 %collective-permute-done.6.refs_2_ = bf16[560,128]{1,0:T(8,128)(2,1)S(1)} collective-permute-done((bf16[560,128]{1,0:T(8,128)(2,1)S(1)}, bf16[560,128]{1,0:T(8,128)(2,1)S(1)}, u32[]{:S(2)}, u32[]{:S(2)}) %collective-permute-start.6) | collective-permute-done | bytes 143392 | tf_op jit(solution)/shard_map/ppermute | solution.py:273
  25.4 0.9 %add_block.14 = (f32[512,128]{1,0:T(8,128)S(1)}, f32[512,128]{1,0:T(8,128)S(1)}) custom-call(bf16[512,32]{1,0:T(8,128)(2,1)S(1)} %get-tuple-element.22.refs_0_, bf16[48,128]{1,0:T(8,128)(2,1)S(1)} %get-tuple-element.25.own_ref.refs_1_, bf16[560,128]{1,0:T(8,128)(2,1)S(1)} %collective-permute-done.6.refs_2_, f32[512,128]{1,0:T(8,128)S(1)} %get-tuple-element.37.refs_3_, ...), custom_call_target="tpu_custom_call" | custom-call | tf_op jit(solution)/shard_map/add_block/pallas_call | solution.py:256
  26.3 0.7 %collective-permute-done.5.refs_2_ = bf16[560,128]{1,0:T(8,128)(2,1)S(1)} collective-permute-done((bf16[560,128]{1,0:T(8,128)(2,1)S(1)}, bf16[560,128]{1,0:T(8,128)(2,1)S(1)}, u32[]{:S(2)}, u32[]{:S(2)}) %collective-permute-start.5) | collective-permute-done | bytes 143392 | tf_op jit(solution)/shard_map/ppermute | solution.py:273
  27.0 1.5 %add_block.15 = (bf16[512,128]{1,0:T(8,128)(2,1)}, f32[512,128]{1,0:T(8,128)}) custom-call(bf16[512,32]{1,0:T(8,128)(2,1)S(1)} %get-tuple-element.22.refs_0_, bf16[48,128]{1,0:T(8,128)(2,1)S(1)} %get-tuple-element.25.own_ref.refs_1_, bf16[560,128]{1,0:T(8,128)(2,1)S(1)} %collective-permute-done.5.refs_2_, f32[512,128]{1,0:T(8,128)S(1)} %get-tuple-element.40.refs_3_, ...), custom_call_target="tpu_custom_call" | custom-call | tf_op jit(solution)/shard_map/add_block/pallas_call | solution.py:256
  (1 shorter events, 0.0 us)
Async XLA Ops:
  0.6 4.1 %copy-start = (bf16[512,128]{1,0:T(8,128)(2,1)S(1)}, bf16[512,128]{1,0:T(8,128)(2,1)}, u32[]{:S(2)}) copy-start(bf16[512,128]{1,0:T(8,128)(2,1)} %omega_ref.1) | copy-start | bytes 393220
  1.6 5.7 %copy-start.1 = (s32[1,64]{1,0:T(1,128)S(1)}, s32[1,64]{1,0:T(1,128)}, u32[]{:S(2)}) copy-start(s32[1,64]{1,0:T(1,128)} %piece_ref.1) | copy-start | bytes 772
  1.7 17.6 %collective-permute-start.10 = (bf16[560,128]{1,0:T(8,128)(2,1)S(1)}, bf16[560,128]{1,0:T(8,128)(2,1)S(1)}, u32[]{:S(2)}, u32[]{:S(2)}) collective-permute-start(bf16[560,128]{1,0:T(8,128)(2,1)S(1)} %get-tuple-element.23.msg_in_ref), channel_id=1, source_target_pairs={{0,4},{4,0},{8,12},{12,8},{16,20},{20,16},{24,28},{28,24},{1,5},{5... | collective-permute-start | bytes 430088 | tf_op jit(solution)/shard_map/ppermute | solution.py:273
  4.7 11.4 %collective-permute-start.3 = (bf16[512,128]{1,0:T(8,128)(2,1)S(1)}, bf16[512,128]{1,0:T(8,128)(2,1)S(1)}, u32[]{:S(2)}, u32[]{:S(2)}) collective-permute-start(bf16[512,128]{1,0:T(8,128)(2,1)S(1)} %copy-done), channel_id=1, source_target_pairs={{0,16},{4,20},{8,24},{12,28},{16,0},{20,4},{24,8},{28,12},{1,17},{... | collective-permute-start | bytes 393224 | tf_op jit(solution)/shard_map/ppermute | solution.py:273
  7.3 3.0 %collective-permute-start = (s32[1,64]{1,0:T(1,128)S(1)}, s32[1,64]{1,0:T(1,128)S(1)}, u32[]{:S(2)}, u32[]{:S(2)}) collective-permute-start(s32[1,64]{1,0:T(1,128)S(1)} %copy-done.1), channel_id=1, source_target_pairs={{0,3},{1,2},{2,1},{3,0},{4,7},{5,6},{6,5},{7,4},{8,11},{9,10},{10,... | collective-permute-start | bytes 776 | tf_op jit(solution)/shard_map/ppermute | solution.py:273
  7.7 3.6 %collective-permute-start.1 = (s32[1,64]{1,0:T(1,128)S(1)}, s32[1,64]{1,0:T(1,128)S(1)}, u32[]{:S(2)}, u32[]{:S(2)}) collective-permute-start(s32[1,64]{1,0:T(1,128)S(1)} %copy-done.1), channel_id=1, source_target_pairs={{0,2},{1,3},{2,0},{3,1},{4,6},{5,7},{6,4},{7,5},{8,10},{9,11},{10,... | collective-permute-start | bytes 776 | tf_op jit(solution)/shard_map/ppermute | solution.py:273
  8.8 2.4 %collective-permute-start.2 = (s32[1,64]{1,0:T(1,128)S(1)}, s32[1,64]{1,0:T(1,128)S(1)}, u32[]{:S(2)}, u32[]{:S(2)}) collective-permute-start(s32[1,64]{1,0:T(1,128)S(1)} %copy-done.1), channel_id=1, source_target_pairs={{0,1},{1,0},{2,3},{3,2},{4,5},{5,4},{6,7},{7,6},{8,9},{9,8},{10,11... | collective-permute-start | bytes 776 | tf_op jit(solution)/shard_map/ppermute | solution.py:273
  11.3 4.8 %collective-permute-start.4 = (bf16[48,128]{1,0:T(8,128)(2,1)S(1)}, bf16[48,128]{1,0:T(8,128)(2,1)S(1)}, u32[]{:S(2)}, u32[]{:S(2)}) collective-permute-start(bf16[48,128]{1,0:T(8,128)(2,1)S(1)} %get-tuple-element.25.own_ref.refs_1_), channel_id=1, source_target_pairs={{0,16},{4,20},{8,24},{12,28},{16,0},{20,4},{24,8},{28,12},{1,17},{... | collective-permute-start | bytes 36872 | tf_op jit(solution)/shard_map/ppermute | solution.py:273
  11.8 9.4 %collective-permute-start.9 = (bf16[560,128]{1,0:T(8,128)(2,1)S(1)}, bf16[560,128]{1,0:T(8,128)(2,1)S(1)}, u32[]{:S(2)}, u32[]{:S(2)}) collective-permute-start(bf16[560,128]{1,0:T(8,128)(2,1)S(1)} %get-tuple-element.23.msg_in_ref), channel_id=1, source_target_pairs={{0,12},{4,8},{8,4},{12,0},{16,28},{20,24},{24,20},{28,16},{1,13},{... | collective-permute-start | bytes 430088 | tf_op jit(solution)/shard_map/ppermute | solution.py:273
  13.6 9.0 %collective-permute-start.8 = (bf16[560,128]{1,0:T(8,128)(2,1)S(1)}, bf16[560,128]{1,0:T(8,128)(2,1)S(1)}, u32[]{:S(2)}, u32[]{:S(2)}) collective-permute-start(bf16[560,128]{1,0:T(8,128)(2,1)S(1)} %get-tuple-element.26.refs_2_), channel_id=1, source_target_pairs={{0,8},{4,12},{8,0},{12,4},{16,24},{20,28},{24,16},{28,20},{1,9},{5... | collective-permute-start | bytes 430088 | tf_op jit(solution)/shard_map/ppermute | solution.py:273
  16.1 7.3 %collective-permute-start.7 = (bf16[560,128]{1,0:T(8,128)(2,1)S(1)}, bf16[560,128]{1,0:T(8,128)(2,1)S(1)}, u32[]{:S(2)}, u32[]{:S(2)}) collective-permute-start(bf16[560,128]{1,0:T(8,128)(2,1)S(1)} %pack.1.refs_2_), channel_id=1, source_target_pairs={{0,4},{4,0},{8,12},{12,8},{16,20},{20,16},{24,28},{28,24},{1,5},{5... | collective-permute-start | bytes 430088 | tf_op jit(solution)/shard_map/ppermute | solution.py:273
  16.7 8.7 %collective-permute-start.6 = (bf16[560,128]{1,0:T(8,128)(2,1)S(1)}, bf16[560,128]{1,0:T(8,128)(2,1)S(1)}, u32[]{:S(2)}, u32[]{:S(2)}) collective-permute-start(bf16[560,128]{1,0:T(8,128)(2,1)S(1)} %pack.1.refs_2_), channel_id=1, source_target_pairs={{0,12},{4,8},{8,4},{12,0},{16,28},{20,24},{24,20},{28,16},{1,13},{... | collective-permute-start | bytes 430088 | tf_op jit(solution)/shard_map/ppermute | solution.py:273
  19.3 7.7 %collective-permute-start.5 = (bf16[560,128]{1,0:T(8,128)(2,1)S(1)}, bf16[560,128]{1,0:T(8,128)(2,1)S(1)}, u32[]{:S(2)}, u32[]{:S(2)}) collective-permute-start(bf16[560,128]{1,0:T(8,128)(2,1)S(1)} %pack.1.refs_2_), channel_id=1, source_target_pairs={{0,8},{4,12},{8,0},{12,4},{16,24},{20,28},{24,16},{28,20},{1,9},{5... | collective-permute-start | bytes 430088 | tf_op jit(solution)/shard_map/ppermute | solution.py:273

commit v7 on v6

--- a/solution.py
+++ b/solution.py
@@ -14,6 +14,7 @@
 soft_term = softening * softening * stretch * stretch
 TERMS = 3
 LANES = 128
+DEPTH = 48
 BASE = 256
 QUAD = (1, 2, 3)
 
@@ -60,10 +61,12 @@
     high, middle, low = split(-2.0 * points if left else points)
     norms = split(norm)
     if left:
-        groups = [high + norms[0], high + norms[1], middle + norms[2], middle + one, high + one, low + one, middle, low]
+        groups = [high + norms[0], high + norms[1], middle + norms[2], middle + one, high + one, low + one]
+        groups += [middle, low, low]
     else:
-        groups = [high + one, middle + one, high + one, middle + norms[0], low + norms[1], high + norms[2], low, middle]
-    return groups
+        groups = [high + one, middle + one, high + one, middle + norms[0], low + norms[1], high + norms[2]]
+        groups += [low, middle, low]
+    return groups + [jnp.zeros_like(points)] * (DEPTH // 4 - len(groups))
 
 
 def chunk_of(groups, k):
@@ -102,7 +105,7 @@
         functools.partial(prep_kernel, lax.axis_size("node")),
         out_shape=(
             jax.ShapeDtypeStruct((leaf + TERMS * term_rows(leaf), LANES), jnp.bfloat16),
-            jax.ShapeDtypeStruct((leaf, 32), jnp.bfloat16),
+            jax.ShapeDtypeStruct((leaf, DEPTH), jnp.bfloat16),
             jax.ShapeDtypeStruct(piece.shape, piece.dtype),
         ),
         in_specs=[pl.BlockSpec(memory_space=pltpu.HBM)] * 3,
@@ -258,7 +261,7 @@
         out_shape=outs,
         in_specs=[VMEM] * (3 + len(totals) + len(waiting)),
         out_specs=[VMEM] * len(outs),
-        scratch_shapes=[pltpu.VMEM((32, leaf), jnp.bfloat16), pltpu.VMEM((leaf, leaf), jnp.bfloat16)],
+        scratch_shapes=[pltpu.VMEM((DEPTH, leaf), jnp.bfloat16), pltpu.VMEM((leaf, leaf), jnp.bfloat16)],
         compiler_params=FAST,
         name="add_block",
     )(left, tail, msg, *totals, *waiting)

time: 28.7 us -> 28.7 us (level)
  no operation moved by 1% of the time
where the time goes in v7:
time: 28.7 us; the launch traced here: 28.5 us
  starting transfers between devices  13.7 us (48%)
  Pallas kernels  8.19 us (29%)
  waiting for transfers between devices  5.89 us (21%)
  between operations  0.72 us (3%)
    ppermute x11, starting transfers between devices, swap(): lax.ppermute(block, axis, [(i, i ^ bits) for i in range(lax.axis_size(axi...  13.7 us
    pallas_call x8, Pallas kernels, add_block(): pl.pallas_call(functools.partial(block_kernel, nodes, list_rows, bits, bo...  7.09 us
    ppermute x11, waiting for transfers between devices, swap(): lax.ppermute(block, axis, [(i, i ^ bits) for i in range(lax.axis_size(axi...  5.89 us
    pallas_call x1, Pallas kernels, prep(): pl.pallas_call(functools.partial(prep_kernel, lax.axis_size('node')), out...  1 us
  transfers between devices with their start and end apart: 11, of which 5 were waited for; matrix products, arithmetic and copies ran while one was open for 0% of the time, Pallas kernels for 20%

profile of v7, /device:TPU:0, one launch (start us, length us, event | category | flops | bytes accessed | tf_op | source)
XLA Modules:
  0.0 28.5 jit_solution(12090738985737274048)
XLA Ops:
  0.6 0.0 copy-start
  0.6 1.0 %prep.1 = (bf16[560,128]{1,0:T(8,128)(2,1)S(1)}, bf16[512,48]{1,0:T(8,128)(2,1)S(1)}, s32[1,64]{1,0:T(1,128)S(1)}) custom-call(f32[3,512]{1,0:T(4,128)} %coords_ref.1, bf16[512,128]{1,0:T(8,128)(2,1)} %omega_ref.1, s32[1,64]{1,0:T(1,128)} %piece_ref.1), custom_call_target="tpu_custom_call" | custom-call | tf_op jit(solution)/shard_map/prep/pallas_call | solution.py:104
  1.6 0.0 copy-start.1
  1.7 3.1 %collective-permute-start.10 = (bf16[560,128]{1,0:T(8,128)(2,1)S(1)}, bf16[560,128]{1,0:T(8,128)(2,1)S(1)}, u32[]{:S(2)}, u32[]{:S(2)}) collective-permute-start(bf16[560,128]{1,0:T(8,128)(2,1)S(1)} %get-tuple-element.23.msg_in_ref), channel_id=1, source_target_pairs={{0,4},{4,0},{8,12},{12,8},{16,20},{20,16},{24,28},{28,24},{1,5},{5... | collective-permute-start | bytes 430088 | tf_op jit(solution)/shard_map/ppermute | solution.py:276
  4.7 0.0 copy-done
  4.7 2.6 %collective-permute-start.3 = (bf16[512,128]{1,0:T(8,128)(2,1)S(1)}, bf16[512,128]{1,0:T(8,128)(2,1)S(1)}, u32[]{:S(2)}, u32[]{:S(2)}) collective-permute-start(bf16[512,128]{1,0:T(8,128)(2,1)S(1)} %copy-done), channel_id=1, source_target_pairs={{0,16},{4,20},{8,24},{12,28},{16,0},{20,4},{24,8},{28,12},{1,17},{... | collective-permute-start | bytes 393224 | tf_op jit(solution)/shard_map/ppermute | solution.py:276
  7.3 0.0 copy-done.1
  7.3 0.4 %collective-permute-start = (s32[1,64]{1,0:T(1,128)S(1)}, s32[1,64]{1,0:T(1,128)S(1)}, u32[]{:S(2)}, u32[]{:S(2)}) collective-permute-start(s32[1,64]{1,0:T(1,128)S(1)} %copy-done.1), channel_id=1, source_target_pairs={{0,3},{1,2},{2,1},{3,0},{4,7},{5,6},{6,5},{7,4},{8,11},{9,10},{10,... | collective-permute-start | bytes 776 | tf_op jit(solution)/shard_map/ppermute | solution.py:276
  7.7 1.1 %collective-permute-start.1 = (s32[1,64]{1,0:T(1,128)S(1)}, s32[1,64]{1,0:T(1,128)S(1)}, u32[]{:S(2)}, u32[]{:S(2)}) collective-permute-start(s32[1,64]{1,0:T(1,128)S(1)} %copy-done.1), channel_id=1, source_target_pairs={{0,2},{1,3},{2,0},{3,1},{4,6},{5,7},{6,4},{7,5},{8,10},{9,11},{10,... | collective-permute-start | bytes 776 | tf_op jit(solution)/shard_map/ppermute | solution.py:276
  8.8 0.4 %collective-permute-start.2 = (s32[1,64]{1,0:T(1,128)S(1)}, s32[1,64]{1,0:T(1,128)S(1)}, u32[]{:S(2)}, u32[]{:S(2)}) collective-permute-start(s32[1,64]{1,0:T(1,128)S(1)} %copy-done.1), channel_id=1, source_target_pairs={{0,1},{1,0},{2,3},{3,2},{4,5},{5,4},{6,7},{7,6},{8,9},{9,8},{10,11... | collective-permute-start | bytes 776 | tf_op jit(solution)/shard_map/ppermute | solution.py:276
  9.2 1.1 %collective-permute-done.refs_1_ = s32[1,64]{1,0:T(1,128)S(1)} collective-permute-done((s32[1,64]{1,0:T(1,128)S(1)}, s32[1,64]{1,0:T(1,128)S(1)}, u32[]{:S(2)}, u32[]{:S(2)}) %collective-permute-start) | collective-permute-done | bytes 288 | tf_op jit(solution)/shard_map/ppermute | solution.py:276
  10.3 0.9 %collective-permute-done.1.refs_2_ = s32[1,64]{1,0:T(1,128)S(1)} collective-permute-done((s32[1,64]{1,0:T(1,128)S(1)}, s32[1,64]{1,0:T(1,128)S(1)}, u32[]{:S(2)}, u32[]{:S(2)}) %collective-permute-start.1) | collective-permute-done | bytes 288 | tf_op jit(solution)/shard_map/ppermute | solution.py:276
  11.3 0.0 collective-permute-done.2.refs_3_
  11.3 0.1 attach.1
  11.3 0.4 %collective-permute-start.4 = (bf16[48,128]{1,0:T(8,128)(2,1)S(1)}, bf16[48,128]{1,0:T(8,128)(2,1)S(1)}, u32[]{:S(2)}, u32[]{:S(2)}) collective-permute-start(bf16[48,128]{1,0:T(8,128)(2,1)S(1)} %get-tuple-element.25.own_ref.refs_1_), channel_id=1, source_target_pairs={{0,16},{4,20},{8,24},{12,28},{16,0},{20,4},{24,8},{28,12},{1,17},{... | collective-permute-start | bytes 36872 | tf_op jit(solution)/shard_map/ppermute | solution.py:276
  11.8 1.8 %collective-permute-start.9 = (bf16[560,128]{1,0:T(8,128)(2,1)S(1)}, bf16[560,128]{1,0:T(8,128)(2,1)S(1)}, u32[]{:S(2)}, u32[]{:S(2)}) collective-permute-start(bf16[560,128]{1,0:T(8,128)(2,1)S(1)} %get-tuple-element.23.msg_in_ref), channel_id=1, source_target_pairs={{0,12},{4,8},{8,4},{12,0},{16,28},{20,24},{24,20},{28,16},{1,13},{... | collective-permute-start | bytes 430088 | tf_op jit(solution)/shard_map/ppermute | solution.py:276
  13.6 0.4 %collective-permute-start.8 = (bf16[560,128]{1,0:T(8,128)(2,1)S(1)}, bf16[560,128]{1,0:T(8,128)(2,1)S(1)}, u32[]{:S(2)}, u32[]{:S(2)}) collective-permute-start(bf16[560,128]{1,0:T(8,128)(2,1)S(1)} %get-tuple-element.26.refs_2_), channel_id=1, source_target_pairs={{0,8},{4,12},{8,0},{12,4},{16,24},{20,28},{24,16},{28,20},{1,9},{5... | collective-permute-start | bytes 430088 | tf_op jit(solution)/shard_map/ppermute | solution.py:276
  14.0 2.1 %collective-permute-done.4.tail_ref = bf16[48,128]{1,0:T(8,128)(2,1)S(1)} collective-permute-done((bf16[48,128]{1,0:T(8,128)(2,1)S(1)}, bf16[48,128]{1,0:T(8,128)(2,1)S(1)}, u32[]{:S(2)}, u32[]{:S(2)}) %collective-permute-start.4) | collective-permute-done | bytes 12320 | tf_op jit(solution)/shard_map/ppermute | solution.py:276
  16.1 0.0 collective-permute-done.3.block_ref
  16.1 0.6 %collective-permute-start.7 = (bf16[560,128]{1,0:T(8,128)(2,1)S(1)}, bf16[560,128]{1,0:T(8,128)(2,1)S(1)}, u32[]{:S(2)}, u32[]{:S(2)}) collective-permute-start(bf16[560,128]{1,0:T(8,128)(2,1)S(1)} %pack.1.refs_2_), channel_id=1, source_target_pairs={{0,4},{4,0},{8,12},{12,8},{16,20},{20,16},{24,28},{28,24},{1,5},{5... | collective-permute-start | bytes 430088 | tf_op jit(solution)/shard_map/ppermute | solution.py:276
  16.7 2.6 %collective-permute-start.6 = (bf16[560,128]{1,0:T(8,128)(2,1)S(1)}, bf16[560,128]{1,0:T(8,128)(2,1)S(1)}, u32[]{:S(2)}, u32[]{:S(2)}) collective-permute-start(bf16[560,128]{1,0:T(8,128)(2,1)S(1)} %pack.1.refs_2_), channel_id=1, source_target_pairs={{0,12},{4,8},{8,4},{12,0},{16,28},{20,24},{24,20},{28,16},{1,13},{... | collective-permute-start | bytes 430088 | tf_op jit(solution)/shard_map/ppermute | solution.py:276
  19.3 0.0 collective-permute-done.10.refs_2_
  19.3 0.4 %collective-permute-start.5 = (bf16[560,128]{1,0:T(8,128)(2,1)S(1)}, bf16[560,128]{1,0:T(8,128)(2,1)S(1)}, u32[]{:S(2)}, u32[]{:S(2)}) collective-permute-start(bf16[560,128]{1,0:T(8,128)(2,1)S(1)} %pack.1.refs_2_), channel_id=1, source_target_pairs={{0,8},{4,12},{8,0},{12,4},{16,24},{20,28},{24,16},{28,20},{1,9},{5... | collective-permute-start | bytes 430088 | tf_op jit(solution)/shard_map/ppermute | solution.py:276
  19.7 0.9 %add_block.8 = (f32[512,128]{1,0:T(8,128)S(1)}, f32[512,128]{1,0:T(8,128)S(1)}, f32[32,128]{1,0:T(8,128)S(1)}) custom-call(bf16[512,48]{1,0:T(8,128)(2,1)S(1)} %get-tuple-element.22.refs_0_, bf16[48,128]{1,0:T(8,128)(2,1)S(1)} %get-tuple-element.25.own_ref.refs_1_, bf16[560,128]{1,0:T(8,128)(2,1)S(1)} %get-tuple-element.26.refs_2_), custom_call_target="tpu_custom_call" | custom-call | tf_op jit(solution)/shard_map/add_block/pallas_call | solution.py:259
  20.6 0.6 %add_block.9 = (f32[512,128]{1,0:T(8,128)S(1)}, f32[512,128]{1,0:T(8,128)S(1)}) custom-call(bf16[512,48]{1,0:T(8,128)(2,1)S(1)} %get-tuple-element.22.refs_0_, bf16[48,128]{1,0:T(8,128)(2,1)S(1)} %get-tuple-element.25.own_ref.refs_1_, bf16[560,128]{1,0:T(8,128)(2,1)S(1)} %collective-permute-done.10.refs_2_, f32[512,128]{1,0:T(8,128)S(1)} %get-tuple-element.27.refs_3_, ...), custom_call_target="tpu_custom_call" | custom-call | tf_op jit(solution)/shard_map/add_block/pallas_call | solution.py:259
  21.2 0.0 collective-permute-done.9.refs_2_
  21.2 0.6 %add_block.10 = (f32[512,128]{1,0:T(8,128)S(1)}, f32[512,128]{1,0:T(8,128)S(1)}) custom-call(bf16[512,48]{1,0:T(8,128)(2,1)S(1)} %get-tuple-element.22.refs_0_, bf16[48,128]{1,0:T(8,128)(2,1)S(1)} %get-tuple-element.25.own_ref.refs_1_, bf16[560,128]{1,0:T(8,128)(2,1)S(1)} %collective-permute-done.9.refs_2_, f32[512,128]{1,0:T(8,128)S(1)} %get-tuple-element.30.refs_3_, ...), custom_call_target="tpu_custom_call" | custom-call | tf_op jit(solution)/shard_map/add_block/pallas_call | solution.py:259
  21.8 0.8 %add_block.11 = (f32[512,128]{1,0:T(8,128)S(1)}, f32[512,128]{1,0:T(8,128)S(1)}) custom-call(bf16[512,48]{1,0:T(8,128)(2,1)S(1)} %get-tuple-element.22.refs_0_, bf16[48,128]{1,0:T(8,128)(2,1)S(1)} %get-tuple-element.25.own_ref.refs_1_, bf16[560,128]{1,0:T(8,128)(2,1)S(1)} %pack.1.refs_2_, f32[512,128]{1,0:T(8,128)S(1)} %get-tuple-element.31.refs_3_, ...), custom_call_target="tpu_custom_call" | custom-call | tf_op jit(solution)/shard_map/add_block/pallas_call | solution.py:259
  22.6 0.0 collective-permute-done.8.refs_2_
  22.6 0.8 %add_block.12 = (f32[512,128]{1,0:T(8,128)S(1)}, f32[512,128]{1,0:T(8,128)S(1)}) custom-call(bf16[512,48]{1,0:T(8,128)(2,1)S(1)} %get-tuple-element.22.refs_0_, bf16[48,128]{1,0:T(8,128)(2,1)S(1)} %get-tuple-element.25.own_ref.refs_1_, bf16[560,128]{1,0:T(8,128)(2,1)S(1)} %collective-permute-done.8.refs_2_, f32[512,128]{1,0:T(8,128)S(1)} %get-tuple-element.32.refs_3_, ...), custom_call_target="tpu_custom_call" | custom-call | tf_op jit(solution)/shard_map/add_block/pallas_call | solution.py:259
  23.5 0.0 collective-permute-done.7.refs_2_
  23.5 0.9 %add_block.13 = (f32[512,128]{1,0:T(8,128)S(1)}, f32[512,128]{1,0:T(8,128)S(1)}) custom-call(bf16[512,48]{1,0:T(8,128)(2,1)S(1)} %get-tuple-element.22.refs_0_, bf16[48,128]{1,0:T(8,128)(2,1)S(1)} %get-tuple-element.25.own_ref.refs_1_, bf16[560,128]{1,0:T(8,128)(2,1)S(1)} %collective-permute-done.7.refs_2_, f32[512,128]{1,0:T(8,128)S(1)} %get-tuple-element.34.refs_3_, ...), custom_call_target="tpu_custom_call" | custom-call | tf_op jit(solution)/shard_map/add_block/pallas_call | solution.py:259
  24.4 1.0 %collective-permute-done.6.refs_2_ = bf16[560,128]{1,0:T(8,128)(2,1)S(1)} collective-permute-done((bf16[560,128]{1,0:T(8,128)(2,1)S(1)}, bf16[560,128]{1,0:T(8,128)(2,1)S(1)}, u32[]{:S(2)}, u32[]{:S(2)}) %collective-permute-start.6) | collective-permute-done | bytes 143392 | tf_op jit(solution)/shard_map/ppermute | solution.py:276
  25.4 0.9 %add_block.14 = (f32[512,128]{1,0:T(8,128)S(1)}, f32[512,128]{1,0:T(8,128)S(1)}) custom-call(bf16[512,48]{1,0:T(8,128)(2,1)S(1)} %get-tuple-element.22.refs_0_, bf16[48,128]{1,0:T(8,128)(2,1)S(1)} %get-tuple-element.25.own_ref.refs_1_, bf16[560,128]{1,0:T(8,128)(2,1)S(1)} %collective-permute-done.6.refs_2_, f32[512,128]{1,0:T(8,128)S(1)} %get-tuple-element.37.refs_3_, ...), custom_call_target="tpu_custom_call" | custom-call | tf_op jit(solution)/shard_map/add_block/pallas_call | solution.py:259
  26.3 0.7 %collective-permute-done.5.refs_2_ = bf16[560,128]{1,0:T(8,128)(2,1)S(1)} collective-permute-done((bf16[560,128]{1,0:T(8,128)(2,1)S(1)}, bf16[560,128]{1,0:T(8,128)(2,1)S(1)}, u32[]{:S(2)}, u32[]{:S(2)}) %collective-permute-start.5) | collective-permute-done | bytes 143392 | tf_op jit(solution)/shard_map/ppermute | solution.py:276
  27.0 1.5 %add_block.15 = (bf16[512,128]{1,0:T(8,128)(2,1)}, f32[512,128]{1,0:T(8,128)}) custom-call(bf16[512,48]{1,0:T(8,128)(2,1)S(1)} %get-tuple-element.22.refs_0_, bf16[48,128]{1,0:T(8,128)(2,1)S(1)} %get-tuple-element.25.own_ref.refs_1_, bf16[560,128]{1,0:T(8,128)(2,1)S(1)} %collective-permute-done.5.refs_2_, f32[512,128]{1,0:T(8,128)S(1)} %get-tuple-element.40.refs_3_, ...), custom_call_target="tpu_custom_call" | custom-call | tf_op jit(solution)/shard_map/add_block/pallas_call | solution.py:259
  (1 shorter events, 0.0 us)
Async XLA Ops:
  0.6 4.1 %copy-start = (bf16[512,128]{1,0:T(8,128)(2,1)S(1)}, bf16[512,128]{1,0:T(8,128)(2,1)}, u32[]{:S(2)}) copy-start(bf16[512,128]{1,0:T(8,128)(2,1)} %omega_ref.1) | copy-start | bytes 393220
  1.6 5.7 %copy-start.1 = (s32[1,64]{1,0:T(1,128)S(1)}, s32[1,64]{1,0:T(1,128)}, u32[]{:S(2)}) copy-start(s32[1,64]{1,0:T(1,128)} %piece_ref.1) | copy-start | bytes 772
  1.7 17.6 %collective-permute-start.10 = (bf16[560,128]{1,0:T(8,128)(2,1)S(1)}, bf16[560,128]{1,0:T(8,128)(2,1)S(1)}, u32[]{:S(2)}, u32[]{:S(2)}) collective-permute-start(bf16[560,128]{1,0:T(8,128)(2,1)S(1)} %get-tuple-element.23.msg_in_ref), channel_id=1, source_target_pairs={{0,4},{4,0},{8,12},{12,8},{16,20},{20,16},{24,28},{28,24},{1,5},{5... | collective-permute-start | bytes 430088 | tf_op jit(solution)/shard_map/ppermute | solution.py:276
  4.7 11.4 %collective-permute-start.3 = (bf16[512,128]{1,0:T(8,128)(2,1)S(1)}, bf16[512,128]{1,0:T(8,128)(2,1)S(1)}, u32[]{:S(2)}, u32[]{:S(2)}) collective-permute-start(bf16[512,128]{1,0:T(8,128)(2,1)S(1)} %copy-done), channel_id=1, source_target_pairs={{0,16},{4,20},{8,24},{12,28},{16,0},{20,4},{24,8},{28,12},{1,17},{... | collective-permute-start | bytes 393224 | tf_op jit(solution)/shard_map/ppermute | solution.py:276
  7.3 3.0 %collective-permute-start = (s32[1,64]{1,0:T(1,128)S(1)}, s32[1,64]{1,0:T(1,128)S(1)}, u32[]{:S(2)}, u32[]{:S(2)}) collective-permute-start(s32[1,64]{1,0:T(1,128)S(1)} %copy-done.1), channel_id=1, source_target_pairs={{0,3},{1,2},{2,1},{3,0},{4,7},{5,6},{6,5},{7,4},{8,11},{9,10},{10,... | collective-permute-start | bytes 776 | tf_op jit(solution)/shard_map/ppermute | solution.py:276
  7.7 3.6 %collective-permute-start.1 = (s32[1,64]{1,0:T(1,128)S(1)}, s32[1,64]{1,0:T(1,128)S(1)}, u32[]{:S(2)}, u32[]{:S(2)}) collective-permute-start(s32[1,64]{1,0:T(1,128)S(1)} %copy-done.1), channel_id=1, source_target_pairs={{0,2},{1,3},{2,0},{3,1},{4,6},{5,7},{6,4},{7,5},{8,10},{9,11},{10,... | collective-permute-start | bytes 776 | tf_op jit(solution)/shard_map/ppermute | solution.py:276
  8.8 2.4 %collective-permute-start.2 = (s32[1,64]{1,0:T(1,128)S(1)}, s32[1,64]{1,0:T(1,128)S(1)}, u32[]{:S(2)}, u32[]{:S(2)}) collective-permute-start(s32[1,64]{1,0:T(1,128)S(1)} %copy-done.1), channel_id=1, source_target_pairs={{0,1},{1,0},{2,3},{3,2},{4,5},{5,4},{6,7},{7,6},{8,9},{9,8},{10,11... | collective-permute-start | bytes 776 | tf_op jit(solution)/shard_map/ppermute | solution.py:276
  11.3 4.8 %collective-permute-start.4 = (bf16[48,128]{1,0:T(8,128)(2,1)S(1)}, bf16[48,128]{1,0:T(8,128)(2,1)S(1)}, u32[]{:S(2)}, u32[]{:S(2)}) collective-permute-start(bf16[48,128]{1,0:T(8,128)(2,1)S(1)} %get-tuple-element.25.own_ref.refs_1_), channel_id=1, source_target_pairs={{0,16},{4,20},{8,24},{12,28},{16,0},{20,4},{24,8},{28,12},{1,17},{... | collective-permute-start | bytes 36872 | tf_op jit(solution)/shard_map/ppermute | solution.py:276
  11.8 9.4 %collective-permute-start.9 = (bf16[560,128]{1,0:T(8,128)(2,1)S(1)}, bf16[560,128]{1,0:T(8,128)(2,1)S(1)}, u32[]{:S(2)}, u32[]{:S(2)}) collective-permute-start(bf16[560,128]{1,0:T(8,128)(2,1)S(1)} %get-tuple-element.23.msg_in_ref), channel_id=1, source_target_pairs={{0,12},{4,8},{8,4},{12,0},{16,28},{20,24},{24,20},{28,16},{1,13},{... | collective-permute-start | bytes 430088 | tf_op jit(solution)/shard_map/ppermute | solution.py:276
  13.6 9.1 %collective-permute-start.8 = (bf16[560,128]{1,0:T(8,128)(2,1)S(1)}, bf16[560,128]{1,0:T(8,128)(2,1)S(1)}, u32[]{:S(2)}, u32[]{:S(2)}) collective-permute-start(bf16[560,128]{1,0:T(8,128)(2,1)S(1)} %get-tuple-element.26.refs_2_), channel_id=1, source_target_pairs={{0,8},{4,12},{8,0},{12,4},{16,24},{20,28},{24,16},{28,20},{1,9},{5... | collective-permute-start | bytes 430088 | tf_op jit(solution)/shard_map/ppermute | solution.py:276
  16.1 7.3 %collective-permute-start.7 = (bf16[560,128]{1,0:T(8,128)(2,1)S(1)}, bf16[560,128]{1,0:T(8,128)(2,1)S(1)}, u32[]{:S(2)}, u32[]{:S(2)}) collective-permute-start(bf16[560,128]{1,0:T(8,128)(2,1)S(1)} %pack.1.refs_2_), channel_id=1, source_target_pairs={{0,4},{4,0},{8,12},{12,8},{16,20},{20,16},{24,28},{28,24},{1,5},{5... | collective-permute-start | bytes 430088 | tf_op jit(solution)/shard_map/ppermute | solution.py:276
  16.7 8.7 %collective-permute-start.6 = (bf16[560,128]{1,0:T(8,128)(2,1)S(1)}, bf16[560,128]{1,0:T(8,128)(2,1)S(1)}, u32[]{:S(2)}, u32[]{:S(2)}) collective-permute-start(bf16[560,128]{1,0:T(8,128)(2,1)S(1)} %pack.1.refs_2_), channel_id=1, source_target_pairs={{0,12},{4,8},{8,4},{12,0},{16,28},{20,24},{24,20},{28,16},{1,13},{... | collective-permute-start | bytes 430088 | tf_op jit(solution)/shard_map/ppermute | solution.py:276
  19.3 7.7 %collective-permute-start.5 = (bf16[560,128]{1,0:T(8,128)(2,1)S(1)}, bf16[560,128]{1,0:T(8,128)(2,1)S(1)}, u32[]{:S(2)}, u32[]{:S(2)}) collective-permute-start(bf16[560,128]{1,0:T(8,128)(2,1)S(1)} %pack.1.refs_2_), channel_id=1, source_target_pairs={{0,8},{4,12},{8,0},{12,4},{16,24},{20,28},{24,16},{28,20},{1,9},{5... | collective-permute-start | bytes 430088 | tf_op jit(solution)/shard_map/ppermute | solution.py:276

commit v8 on v7

--- a/solution.py
+++ b/solution.py
@@ -216,6 +216,11 @@
         table_ref = outs[2]
         table_ref[...] = count_table(mine, 0.0, table_ref.shape[0])
     tail = msg_ref[leaf:, :].astype(jnp.float32)
+    table_rows = -(-chunks // 8) * 8
+    masks = []
+    for slot in range((1 + waiting) * masked):
+        named = count_table(listed_in(tail, leaf, list_rows, slot), first, table_rows)
+        masks.append(widened(named[0:chunks, :]))
     term = term_rows(leaf)
     points = (tail[0:term, :] + tail[term : 2 * term, :]) + tail[2 * term : 3 * term, :]
     groups = factors(centred(points, nodes, me), False)
@@ -237,14 +242,11 @@
     if not masked:
         outs[1][...] = col
         return
-    table_rows = -(-chunks // 8) * 8
-    named = count_table(listed_in(tail, leaf, list_rows), first, table_rows)
-    col = widened(named[0:chunks, :]) * col
+    col = masks[0] * col
     if started:
         col = col_in_ref[...] + col
     if waiting:
-        named = count_table(listed_in(tail, leaf, list_rows, 1), first, table_rows)
-        col = col + widened(named[0:chunks, :]) * refs[6][...]
+        col = col + masks[1] * refs[6][...]
     outs[1][...] = col
 
 

time: 28.7 us -> 28.6 us (level)
  Pallas kernels: 8.19 us -> 7.39 us
  waiting for transfers between devices: 5.89 us -> 6.59 us
    pallas_call x8, Pallas kernels: 7.09 us -> 6.29 us  [add_block(): pl.pallas_call(functools.partial(block_kernel, nodes, list_rows, bits, bo...]
    ppermute x11, waiting for transfers between devices: 5.89 us -> 6.59 us  [swap(): lax.ppermute(block, axis, [(i, i ^ bits) for i in range(lax.axis_size(axi...]
  transfers between devices with their start and end apart: 11 -> 11, of which waited for: 5 -> 5; matrix products, arithmetic and copies ran while one was open for 0% -> 0% of each run, Pallas kernels for 20% -> 17%
where the time goes in v8:
time: 28.6 us; the launch traced here: 28.5 us
  starting transfers between devices  13.7 us (48%)
  Pallas kernels  7.39 us (26%)
  waiting for transfers between devices  6.59 us (23%)
  between operations  0.74 us (3%)
    ppermute x11, starting transfers between devices, swap(): lax.ppermute(block, axis, [(i, i ^ bits) for i in range(lax.axis_size(axi...  13.7 us
    ppermute x11, waiting for transfers between devices, swap(): lax.ppermute(block, axis, [(i, i ^ bits) for i in range(lax.axis_size(axi...  6.59 us
    pallas_call x8, Pallas kernels, add_block(): pl.pallas_call(functools.partial(block_kernel, nodes, list_rows, bits, bo...  6.29 us
    pallas_call x1, Pallas kernels, prep(): pl.pallas_call(functools.partial(prep_kernel, lax.axis_size('node')), out...  1 us
  transfers between devices with their start and end apart: 11, of which 5 were waited for; matrix products, arithmetic and copies ran while one was open for 0% of the time, Pallas kernels for 17%

profile of v8, /device:TPU:0, one launch (start us, length us, event | category | flops | bytes accessed | tf_op | source)
XLA Modules:
  0.0 28.5 jit_solution(17508703485442156449)
XLA Ops:
  0.6 0.0 copy-start
  0.6 1.0 %prep.1 = (bf16[560,128]{1,0:T(8,128)(2,1)S(1)}, bf16[512,48]{1,0:T(8,128)(2,1)S(1)}, s32[1,64]{1,0:T(1,128)S(1)}) custom-call(f32[3,512]{1,0:T(4,128)} %coords_ref.1, bf16[512,128]{1,0:T(8,128)(2,1)} %omega_ref.1, s32[1,64]{1,0:T(1,128)} %piece_ref.1), custom_call_target="tpu_custom_call" | custom-call | tf_op jit(solution)/shard_map/prep/pallas_call | solution.py:104
  1.6 0.0 copy-start.1
  1.7 3.1 %collective-permute-start.10 = (bf16[560,128]{1,0:T(8,128)(2,1)S(1)}, bf16[560,128]{1,0:T(8,128)(2,1)S(1)}, u32[]{:S(2)}, u32[]{:S(2)}) collective-permute-start(bf16[560,128]{1,0:T(8,128)(2,1)S(1)} %get-tuple-element.23.msg_in_ref), channel_id=1, source_target_pairs={{0,4},{4,0},{8,12},{12,8},{16,20},{20,16},{24,28},{28,24},{1,5},{5... | collective-permute-start | bytes 430088 | tf_op jit(solution)/shard_map/ppermute | solution.py:278
  4.7 0.0 copy-done
  4.7 2.6 %collective-permute-start.3 = (bf16[512,128]{1,0:T(8,128)(2,1)S(1)}, bf16[512,128]{1,0:T(8,128)(2,1)S(1)}, u32[]{:S(2)}, u32[]{:S(2)}) collective-permute-start(bf16[512,128]{1,0:T(8,128)(2,1)S(1)} %copy-done), channel_id=1, source_target_pairs={{0,16},{4,20},{8,24},{12,28},{16,0},{20,4},{24,8},{28,12},{1,17},{... | collective-permute-start | bytes 393224 | tf_op jit(solution)/shard_map/ppermute | solution.py:278
  7.3 0.0 copy-done.1
  7.3 0.4 %collective-permute-start = (s32[1,64]{1,0:T(1,128)S(1)}, s32[1,64]{1,0:T(1,128)S(1)}, u32[]{:S(2)}, u32[]{:S(2)}) collective-permute-start(s32[1,64]{1,0:T(1,128)S(1)} %copy-done.1), channel_id=1, source_target_pairs={{0,3},{1,2},{2,1},{3,0},{4,7},{5,6},{6,5},{7,4},{8,11},{9,10},{10,... | collective-permute-start | bytes 776 | tf_op jit(solution)/shard_map/ppermute | solution.py:278
  7.7 1.1 %collective-permute-start.1 = (s32[1,64]{1,0:T(1,128)S(1)}, s32[1,64]{1,0:T(1,128)S(1)}, u32[]{:S(2)}, u32[]{:S(2)}) collective-permute-start(s32[1,64]{1,0:T(1,128)S(1)} %copy-done.1), channel_id=1, source_target_pairs={{0,2},{1,3},{2,0},{3,1},{4,6},{5,7},{6,4},{7,5},{8,10},{9,11},{10,... | collective-permute-start | bytes 776 | tf_op jit(solution)/shard_map/ppermute | solution.py:278
  8.8 0.4 %collective-permute-start.2 = (s32[1,64]{1,0:T(1,128)S(1)}, s32[1,64]{1,0:T(1,128)S(1)}, u32[]{:S(2)}, u32[]{:S(2)}) collective-permute-start(s32[1,64]{1,0:T(1,128)S(1)} %copy-done.1), channel_id=1, source_target_pairs={{0,1},{1,0},{2,3},{3,2},{4,5},{5,4},{6,7},{7,6},{8,9},{9,8},{10,11... | collective-permute-start | bytes 776 | tf_op jit(solution)/shard_map/ppermute | solution.py:278
  9.2 1.1 %collective-permute-done.refs_1_ = s32[1,64]{1,0:T(1,128)S(1)} collective-permute-done((s32[1,64]{1,0:T(1,128)S(1)}, s32[1,64]{1,0:T(1,128)S(1)}, u32[]{:S(2)}, u32[]{:S(2)}) %collective-permute-start) | collective-permute-done | bytes 288 | tf_op jit(solution)/shard_map/ppermute | solution.py:278
  10.3 0.9 %collective-permute-done.1.refs_2_ = s32[1,64]{1,0:T(1,128)S(1)} collective-permute-done((s32[1,64]{1,0:T(1,128)S(1)}, s32[1,64]{1,0:T(1,128)S(1)}, u32[]{:S(2)}, u32[]{:S(2)}) %collective-permute-start.1) | collective-permute-done | bytes 288 | tf_op jit(solution)/shard_map/ppermute | solution.py:278
  11.3 0.0 collective-permute-done.2.refs_3_
  11.3 0.1 attach.1
  11.3 0.4 %collective-permute-start.4 = (bf16[48,128]{1,0:T(8,128)(2,1)S(1)}, bf16[48,128]{1,0:T(8,128)(2,1)S(1)}, u32[]{:S(2)}, u32[]{:S(2)}) collective-permute-start(bf16[48,128]{1,0:T(8,128)(2,1)S(1)} %get-tuple-element.25.own_ref.refs_1_), channel_id=1, source_target_pairs={{0,16},{4,20},{8,24},{12,28},{16,0},{20,4},{24,8},{28,12},{1,17},{... | collective-permute-start | bytes 36872 | tf_op jit(solution)/shard_map/ppermute | solution.py:278
  11.8 1.8 %collective-permute-start.9 = (bf16[560,128]{1,0:T(8,128)(2,1)S(1)}, bf16[560,128]{1,0:T(8,128)(2,1)S(1)}, u32[]{:S(2)}, u32[]{:S(2)}) collective-permute-start(bf16[560,128]{1,0:T(8,128)(2,1)S(1)} %get-tuple-element.23.msg_in_ref), channel_id=1, source_target_pairs={{0,12},{4,8},{8,4},{12,0},{16,28},{20,24},{24,20},{28,16},{1,13},{... | collective-permute-start | bytes 430088 | tf_op jit(solution)/shard_map/ppermute | solution.py:278
  13.6 0.4 %collective-permute-start.8 = (bf16[560,128]{1,0:T(8,128)(2,1)S(1)}, bf16[560,128]{1,0:T(8,128)(2,1)S(1)}, u32[]{:S(2)}, u32[]{:S(2)}) collective-permute-start(bf16[560,128]{1,0:T(8,128)(2,1)S(1)} %get-tuple-element.26.refs_2_), channel_id=1, source_target_pairs={{0,8},{4,12},{8,0},{12,4},{16,24},{20,28},{24,16},{28,20},{1,9},{5... | collective-permute-start | bytes 430088 | tf_op jit(solution)/shard_map/ppermute | solution.py:278
  14.0 2.1 %collective-permute-done.4.tail_ref = bf16[48,128]{1,0:T(8,128)(2,1)S(1)} collective-permute-done((bf16[48,128]{1,0:T(8,128)(2,1)S(1)}, bf16[48,128]{1,0:T(8,128)(2,1)S(1)}, u32[]{:S(2)}, u32[]{:S(2)}) %collective-permute-start.4) | collective-permute-done | bytes 12320 | tf_op jit(solution)/shard_map/ppermute | solution.py:278
  16.1 0.0 collective-permute-done.3.block_ref
  16.1 0.6 %collective-permute-start.7 = (bf16[560,128]{1,0:T(8,128)(2,1)S(1)}, bf16[560,128]{1,0:T(8,128)(2,1)S(1)}, u32[]{:S(2)}, u32[]{:S(2)}) collective-permute-start(bf16[560,128]{1,0:T(8,128)(2,1)S(1)} %pack.1.refs_2_), channel_id=1, source_target_pairs={{0,4},{4,0},{8,12},{12,8},{16,20},{20,16},{24,28},{28,24},{1,5},{5... | collective-permute-start | bytes 430088 | tf_op jit(solution)/shard_map/ppermute | solution.py:278
  16.7 2.6 %collective-permute-start.6 = (bf16[560,128]{1,0:T(8,128)(2,1)S(1)}, bf16[560,128]{1,0:T(8,128)(2,1)S(1)}, u32[]{:S(2)}, u32[]{:S(2)}) collective-permute-start(bf16[560,128]{1,0:T(8,128)(2,1)S(1)} %pack.1.refs_2_), channel_id=1, source_target_pairs={{0,12},{4,8},{8,4},{12,0},{16,28},{20,24},{24,20},{28,16},{1,13},{... | collective-permute-start | bytes 430088 | tf_op jit(solution)/shard_map/ppermute | solution.py:278
  19.3 0.0 collective-permute-done.10.refs_2_
  19.3 0.4 %collective-permute-start.5 = (bf16[560,128]{1,0:T(8,128)(2,1)S(1)}, bf16[560,128]{1,0:T(8,128)(2,1)S(1)}, u32[]{:S(2)}, u32[]{:S(2)}) collective-permute-start(bf16[560,128]{1,0:T(8,128)(2,1)S(1)} %pack.1.refs_2_), channel_id=1, source_target_pairs={{0,8},{4,12},{8,0},{12,4},{16,24},{20,28},{24,16},{28,20},{1,9},{5... | collective-permute-start | bytes 430088 | tf_op jit(solution)/shard_map/ppermute | solution.py:278
  19.7 0.8 %add_block.8 = (f32[512,128]{1,0:T(8,128)S(1)}, f32[512,128]{1,0:T(8,128)S(1)}, f32[32,128]{1,0:T(8,128)S(1)}) custom-call(bf16[512,48]{1,0:T(8,128)(2,1)S(1)} %get-tuple-element.22.refs_0_, bf16[48,128]{1,0:T(8,128)(2,1)S(1)} %get-tuple-element.25.own_ref.refs_1_, bf16[560,128]{1,0:T(8,128)(2,1)S(1)} %get-tuple-element.26.refs_2_), custom_call_target="tpu_custom_call" | custom-call | tf_op jit(solution)/shard_map/add_block/pallas_call | solution.py:261
  20.5 0.6 %add_block.9 = (f32[512,128]{1,0:T(8,128)S(1)}, f32[512,128]{1,0:T(8,128)S(1)}) custom-call(bf16[512,48]{1,0:T(8,128)(2,1)S(1)} %get-tuple-element.22.refs_0_, bf16[48,128]{1,0:T(8,128)(2,1)S(1)} %get-tuple-element.25.own_ref.refs_1_, bf16[560,128]{1,0:T(8,128)(2,1)S(1)} %collective-permute-done.10.refs_2_, f32[512,128]{1,0:T(8,128)S(1)} %get-tuple-element.27.refs_3_, ...), custom_call_target="tpu_custom_call" | custom-call | tf_op jit(solution)/shard_map/add_block/pallas_call | solution.py:261
  21.1 0.0 collective-permute-done.9.refs_2_
  21.1 0.6 %add_block.10 = (f32[512,128]{1,0:T(8,128)S(1)}, f32[512,128]{1,0:T(8,128)S(1)}) custom-call(bf16[512,48]{1,0:T(8,128)(2,1)S(1)} %get-tuple-element.22.refs_0_, bf16[48,128]{1,0:T(8,128)(2,1)S(1)} %get-tuple-element.25.own_ref.refs_1_, bf16[560,128]{1,0:T(8,128)(2,1)S(1)} %collective-permute-done.9.refs_2_, f32[512,128]{1,0:T(8,128)S(1)} %get-tuple-element.30.refs_3_, ...), custom_call_target="tpu_custom_call" | custom-call | tf_op jit(solution)/shard_map/add_block/pallas_call | solution.py:261
  21.8 0.7 %add_block.11 = (f32[512,128]{1,0:T(8,128)S(1)}, f32[512,128]{1,0:T(8,128)S(1)}) custom-call(bf16[512,48]{1,0:T(8,128)(2,1)S(1)} %get-tuple-element.22.refs_0_, bf16[48,128]{1,0:T(8,128)(2,1)S(1)} %get-tuple-element.25.own_ref.refs_1_, bf16[560,128]{1,0:T(8,128)(2,1)S(1)} %pack.1.refs_2_, f32[512,128]{1,0:T(8,128)S(1)} %get-tuple-element.31.refs_3_, ...), custom_call_target="tpu_custom_call" | custom-call | tf_op jit(solution)/shard_map/add_block/pallas_call | solution.py:261
  22.5 0.0 collective-permute-done.8.refs_2_
  22.5 0.7 %add_block.12 = (f32[512,128]{1,0:T(8,128)S(1)}, f32[512,128]{1,0:T(8,128)S(1)}) custom-call(bf16[512,48]{1,0:T(8,128)(2,1)S(1)} %get-tuple-element.22.refs_0_, bf16[48,128]{1,0:T(8,128)(2,1)S(1)} %get-tuple-element.25.own_ref.refs_1_, bf16[560,128]{1,0:T(8,128)(2,1)S(1)} %collective-permute-done.8.refs_2_, f32[512,128]{1,0:T(8,128)S(1)} %get-tuple-element.32.refs_3_, ...), custom_call_target="tpu_custom_call" | custom-call | tf_op jit(solution)/shard_map/add_block/pallas_call | solution.py:261
  23.2 0.0 collective-permute-done.7.refs_2_
  23.2 0.7 %add_block.13 = (f32[512,128]{1,0:T(8,128)S(1)}, f32[512,128]{1,0:T(8,128)S(1)}) custom-call(bf16[512,48]{1,0:T(8,128)(2,1)S(1)} %get-tuple-element.22.refs_0_, bf16[48,128]{1,0:T(8,128)(2,1)S(1)} %get-tuple-element.25.own_ref.refs_1_, bf16[560,128]{1,0:T(8,128)(2,1)S(1)} %collective-permute-done.7.refs_2_, f32[512,128]{1,0:T(8,128)S(1)} %get-tuple-element.34.refs_3_, ...), custom_call_target="tpu_custom_call" | custom-call | tf_op jit(solution)/shard_map/add_block/pallas_call | solution.py:261
  23.9 1.5 %collective-permute-done.6.refs_2_ = bf16[560,128]{1,0:T(8,128)(2,1)S(1)} collective-permute-done((bf16[560,128]{1,0:T(8,128)(2,1)S(1)}, bf16[560,128]{1,0:T(8,128)(2,1)S(1)}, u32[]{:S(2)}, u32[]{:S(2)}) %collective-permute-start.6) | collective-permute-done | bytes 143392 | tf_op jit(solution)/shard_map/ppermute | solution.py:278
  25.4 0.7 %add_block.14 = (f32[512,128]{1,0:T(8,128)S(1)}, f32[512,128]{1,0:T(8,128)S(1)}) custom-call(bf16[512,48]{1,0:T(8,128)(2,1)S(1)} %get-tuple-element.22.refs_0_, bf16[48,128]{1,0:T(8,128)(2,1)S(1)} %get-tuple-element.25.own_ref.refs_1_, bf16[560,128]{1,0:T(8,128)(2,1)S(1)} %collective-permute-done.6.refs_2_, f32[512,128]{1,0:T(8,128)S(1)} %get-tuple-element.37.refs_3_, ...), custom_call_target="tpu_custom_call" | custom-call | tf_op jit(solution)/shard_map/add_block/pallas_call | solution.py:261
  26.1 0.9 %collective-permute-done.5.refs_2_ = bf16[560,128]{1,0:T(8,128)(2,1)S(1)} collective-permute-done((bf16[560,128]{1,0:T(8,128)(2,1)S(1)}, bf16[560,128]{1,0:T(8,128)(2,1)S(1)}, u32[]{:S(2)}, u32[]{:S(2)}) %collective-permute-start.5) | collective-permute-done | bytes 143392 | tf_op jit(solution)/shard_map/ppermute | solution.py:278
  27.0 1.5 %add_block.15 = (bf16[512,128]{1,0:T(8,128)(2,1)}, f32[512,128]{1,0:T(8,128)}) custom-call(bf16[512,48]{1,0:T(8,128)(2,1)S(1)} %get-tuple-element.22.refs_0_, bf16[48,128]{1,0:T(8,128)(2,1)S(1)} %get-tuple-element.25.own_ref.refs_1_, bf16[560,128]{1,0:T(8,128)(2,1)S(1)} %collective-permute-done.5.refs_2_, f32[512,128]{1,0:T(8,128)S(1)} %get-tuple-element.40.refs_3_, ...), custom_call_target="tpu_custom_call" | custom-call | tf_op jit(solution)/shard_map/add_block/pallas_call | solution.py:261
  (1 shorter events, 0.0 us)
Async XLA Ops:
  0.6 4.1 %copy-start = (bf16[512,128]{1,0:T(8,128)(2,1)S(1)}, bf16[512,128]{1,0:T(8,128)(2,1)}, u32[]{:S(2)}) copy-start(bf16[512,128]{1,0:T(8,128)(2,1)} %omega_ref.1) | copy-start | bytes 393220
  1.6 5.7 %copy-start.1 = (s32[1,64]{1,0:T(1,128)S(1)}, s32[1,64]{1,0:T(1,128)}, u32[]{:S(2)}) copy-start(s32[1,64]{1,0:T(1,128)} %piece_ref.1) | copy-start | bytes 772
  1.7 17.6 %collective-permute-start.10 = (bf16[560,128]{1,0:T(8,128)(2,1)S(1)}, bf16[560,128]{1,0:T(8,128)(2,1)S(1)}, u32[]{:S(2)}, u32[]{:S(2)}) collective-permute-start(bf16[560,128]{1,0:T(8,128)(2,1)S(1)} %get-tuple-element.23.msg_in_ref), channel_id=1, source_target_pairs={{0,4},{4,0},{8,12},{12,8},{16,20},{20,16},{24,28},{28,24},{1,5},{5... | collective-permute-start | bytes 430088 | tf_op jit(solution)/shard_map/ppermute | solution.py:278
  4.7 11.4 %collective-permute-start.3 = (bf16[512,128]{1,0:T(8,128)(2,1)S(1)}, bf16[512,128]{1,0:T(8,128)(2,1)S(1)}, u32[]{:S(2)}, u32[]{:S(2)}) collective-permute-start(bf16[512,128]{1,0:T(8,128)(2,1)S(1)} %copy-done), channel_id=1, source_target_pairs={{0,16},{4,20},{8,24},{12,28},{16,0},{20,4},{24,8},{28,12},{1,17},{... | collective-permute-start | bytes 393224 | tf_op jit(solution)/shard_map/ppermute | solution.py:278
  7.3 3.0 %collective-permute-start = (s32[1,64]{1,0:T(1,128)S(1)}, s32[1,64]{1,0:T(1,128)S(1)}, u32[]{:S(2)}, u32[]{:S(2)}) collective-permute-start(s32[1,64]{1,0:T(1,128)S(1)} %copy-done.1), channel_id=1, source_target_pairs={{0,3},{1,2},{2,1},{3,0},{4,7},{5,6},{6,5},{7,4},{8,11},{9,10},{10,... | collective-permute-start | bytes 776 | tf_op jit(solution)/shard_map/ppermute | solution.py:278
  7.7 3.6 %collective-permute-start.1 = (s32[1,64]{1,0:T(1,128)S(1)}, s32[1,64]{1,0:T(1,128)S(1)}, u32[]{:S(2)}, u32[]{:S(2)}) collective-permute-start(s32[1,64]{1,0:T(1,128)S(1)} %copy-done.1), channel_id=1, source_target_pairs={{0,2},{1,3},{2,0},{3,1},{4,6},{5,7},{6,4},{7,5},{8,10},{9,11},{10,... | collective-permute-start | bytes 776 | tf_op jit(solution)/shard_map/ppermute | solution.py:278
  8.8 2.4 %collective-permute-start.2 = (s32[1,64]{1,0:T(1,128)S(1)}, s32[1,64]{1,0:T(1,128)S(1)}, u32[]{:S(2)}, u32[]{:S(2)}) collective-permute-start(s32[1,64]{1,0:T(1,128)S(1)} %copy-done.1), channel_id=1, source_target_pairs={{0,1},{1,0},{2,3},{3,2},{4,5},{5,4},{6,7},{7,6},{8,9},{9,8},{10,11... | collective-permute-start | bytes 776 | tf_op jit(solution)/shard_map/ppermute | solution.py:278
  11.3 4.8 %collective-permute-start.4 = (bf16[48,128]{1,0:T(8,128)(2,1)S(1)}, bf16[48,128]{1,0:T(8,128)(2,1)S(1)}, u32[]{:S(2)}, u32[]{:S(2)}) collective-permute-start(bf16[48,128]{1,0:T(8,128)(2,1)S(1)} %get-tuple-element.25.own_ref.refs_1_), channel_id=1, source_target_pairs={{0,16},{4,20},{8,24},{12,28},{16,0},{20,4},{24,8},{28,12},{1,17},{... | collective-permute-start | bytes 36872 | tf_op jit(solution)/shard_map/ppermute | solution.py:278
  11.8 9.4 %collective-permute-start.9 = (bf16[560,128]{1,0:T(8,128)(2,1)S(1)}, bf16[560,128]{1,0:T(8,128)(2,1)S(1)}, u32[]{:S(2)}, u32[]{:S(2)}) collective-permute-start(bf16[560,128]{1,0:T(8,128)(2,1)S(1)} %get-tuple-element.23.msg_in_ref), channel_id=1, source_target_pairs={{0,12},{4,8},{8,4},{12,0},{16,28},{20,24},{24,20},{28,16},{1,13},{... | collective-permute-start | bytes 430088 | tf_op jit(solution)/shard_map/ppermute | solution.py:278
  13.6 8.9 %collective-permute-start.8 = (bf16[560,128]{1,0:T(8,128)(2,1)S(1)}, bf16[560,128]{1,0:T(8,128)(2,1)S(1)}, u32[]{:S(2)}, u32[]{:S(2)}) collective-permute-start(bf16[560,128]{1,0:T(8,128)(2,1)S(1)} %get-tuple-element.26.refs_2_), channel_id=1, source_target_pairs={{0,8},{4,12},{8,0},{12,4},{16,24},{20,28},{24,16},{28,20},{1,9},{5... | collective-permute-start | bytes 430088 | tf_op jit(solution)/shard_map/ppermute | solution.py:278
  16.1 7.1 %collective-permute-start.7 = (bf16[560,128]{1,0:T(8,128)(2,1)S(1)}, bf16[560,128]{1,0:T(8,128)(2,1)S(1)}, u32[]{:S(2)}, u32[]{:S(2)}) collective-permute-start(bf16[560,128]{1,0:T(8,128)(2,1)S(1)} %pack.1.refs_2_), channel_id=1, source_target_pairs={{0,4},{4,0},{8,12},{12,8},{16,20},{20,16},{24,28},{28,24},{1,5},{5... | collective-permute-start | bytes 430088 | tf_op jit(solution)/shard_map/ppermute | solution.py:278
  16.7 8.7 %collective-permute-start.6 = (bf16[560,128]{1,0:T(8,128)(2,1)S(1)}, bf16[560,128]{1,0:T(8,128)(2,1)S(1)}, u32[]{:S(2)}, u32[]{:S(2)}) collective-permute-start(bf16[560,128]{1,0:T(8,128)(2,1)S(1)} %pack.1.refs_2_), channel_id=1, source_target_pairs={{0,12},{4,8},{8,4},{12,0},{16,28},{20,24},{24,20},{28,16},{1,13},{... | collective-permute-start | bytes 430088 | tf_op jit(solution)/shard_map/ppermute | solution.py:278
  19.3 7.7 %collective-permute-start.5 = (bf16[560,128]{1,0:T(8,128)(2,1)S(1)}, bf16[560,128]{1,0:T(8,128)(2,1)S(1)}, u32[]{:S(2)}, u32[]{:S(2)}) collective-permute-start(bf16[560,128]{1,0:T(8,128)(2,1)S(1)} %pack.1.refs_2_), channel_id=1, source_target_pairs={{0,8},{4,12},{8,0},{12,4},{16,24},{20,28},{24,16},{28,20},{1,9},{5... | collective-permute-start | bytes 430088 | tf_op jit(solution)/shard_map/ppermute | solution.py:278
